TPU v7x, 256 devices: a whole 4x4x8 slice. The times are simulated.
256 devices in a mesh: wide: 64 (over x, y_hi, z), narrow: 4 (over y_lo, core).
Axes of the slice: x: 4, y: 4 (y_hi: 2, y_lo: 2; y = y_hi * 2 + y_lo), z: 8, core: 2. Of those that a mesh axis runs over, the one named last changes fastest.
Arguments:
- tokens: bfloat16 [8192, 2048], P('wide'), may hold values from -6 to 6
- expert_ids: int32 [8192, 6], P('wide'), may hold values from 0 to 63, all different within a row; in each aligned block of 128 rows (0 to 127, 128 to 255, ...) at most 16 rows name the same one
- gate_weights: float32 [8192, 6], P('wide'), may hold values from 0.05 to 0.6
- shared_gate: bfloat16 [2048, 2816], P('wide', 'narrow'), may hold values from -0.125 to 0.125
- shared_up: bfloat16 [2048, 2816], P('wide', 'narrow'), may hold values from -0.125 to 0.125
- shared_down: bfloat16 [2816, 2048], P('narrow', 'wide'), may hold values from -0.109375 to 0.109375
- expert_gate: bfloat16 [64, 2048, 1408], P('wide', None, 'narrow'), may hold values from -0.125 to 0.125
- expert_up: bfloat16 [64, 2048, 1408], P('wide', None, 'narrow'), may hold values from -0.125 to 0.125
- expert_down: bfloat16 [64, 1408, 2048], P('wide', 'narrow'), may hold values from -0.15625 to 0.15625
Outputs:
- moe_out: bfloat16 [8192, 2048], P('wide', 'narrow')
Inputs may be any that keep to these rules, and one draw needn't show every extreme that they name: `expert_ids`: the 6 ids of a row differ. Among the 128 rows of one index of wide, no expert is named by more than 16 rows.
All inputs are finite; a program needn't handle non-finite values.
Results may differ from a plain program's by a relative error of at most 0.0075.
Values may be sent and summed in bfloat16 or wider, within the bound.
No kernel may reach another device: no remote copies, remote signals or barrier semaphores. Data moves between devices by JAX's collectives and lax.ppermute only.
A program may use at most 128 MiB of HBM per device.

v0:
```python
import jax
import jax.numpy as jnp
from jax import lax
from jax.sharding import PartitionSpec as P


def items_in_groups(array, axis, split_dim, concat_dim, work, item_dim, out_dim):
    items = jax.tree.leaves(array)[0].shape[item_dim]
    count = 2 if items % 2 == 0 else 1
    finished = []
    for k in range(count):
        group = jax.tree.map(
            lambda a: lax.slice_in_dim(
                a, k * (items // count), (k + 1) * (items // count), axis=item_dim
            ),
            array,
        )
        finished.append(
            work(
                lax.all_to_all(
                    group, axis, split_axis=split_dim, concat_axis=concat_dim, tiled=True
                )
            )
        )
    return jax.tree.map(lambda *parts: jnp.concatenate(parts, axis=out_dim), *finished)


def split_up(array, dim, length):
    lengths = array.shape
    blocks = array.reshape(*lengths[:dim], length, lengths[dim] // length, *lengths[dim + 1 :])
    return jnp.moveaxis(blocks, dim, 0)


def sum_at_owner(array, axis, dim):
    length = lax.axis_size(axis)
    blocks = lax.all_to_all(split_up(array, dim, length), axis, 0, 0, tiled=True)
    return jnp.sum(blocks.astype(jnp.float32), axis=0)


def sent_together(arrays, axis, dim, along):
    ends, at = ([], 0)
    for a in arrays[:-1]:
        at += a.shape[along]
        ends.append(at)
    both = jnp.concatenate(arrays, axis=along)
    return tuple(jnp.split(lax.all_gather(both, axis, axis=dim, tiled=True), ends, axis=along))


def expert_ffn(received, w_gate, w_up, w_down):
    senders, items, width = received.shape
    flat_rows = received.reshape(senders * items, width)
    gate_part = jnp.dot(flat_rows, w_gate, preferred_element_type=jnp.float32)
    up_part = jnp.dot(flat_rows, w_up, preferred_element_type=jnp.float32)
    hidden = (jax.nn.silu(gate_part) * up_part).astype(jnp.bfloat16)
    partial_value = jnp.dot(hidden, w_down, preferred_element_type=jnp.float32).astype(jnp.bfloat16)
    return partial_value.reshape(senders, items, w_down.shape[1])


def body(
    tokens,
    expert_ids,
    gate_weights,
    shared_gate,
    shared_up,
    shared_down,
    expert_gate,
    expert_up,
    expert_down,
):
    tok_count, width = tokens.shape
    top_count = expert_ids.shape[1]
    experts = lax.axis_size("wide") * expert_gate.shape[0]
    capacity = min(tok_count, 4 * tok_count * top_count // (3 * experts))
    w_gate = expert_gate[0]
    w_up = expert_up[0]
    w_down = expert_down[0]
    pairs = tok_count * top_count
    flat_ids = expert_ids.reshape(pairs)
    onehot = (flat_ids[:, None] == jnp.arange(experts, dtype=jnp.int32)[None, :]).astype(jnp.int32)
    before = jnp.cumsum(onehot, axis=0) - onehot
    slot_pos = jnp.sum(before * onehot, axis=1)
    target_slot = flat_ids * capacity + slot_pos
    source = (
        jnp.full((experts * capacity,), -1, jnp.int32)
        .at[target_slot]
        .set(jnp.arange(pairs, dtype=jnp.int32))
    )
    filled = source >= 0
    token_of = jnp.where(filled, source // top_count, 0)
    outgoing = jnp.where(filled[:, None], tokens[token_of], jnp.zeros((), jnp.bfloat16))
    outgoing = outgoing.reshape(experts, capacity, width)

    def run_expert(received):
        return expert_ffn(received, w_gate, w_up, w_down)

    partial_value = items_in_groups(outgoing, "wide", 0, 0, run_expert, 1, 1)
    expert_out = sum_at_owner(partial_value, "narrow", 2).astype(jnp.bfloat16)
    returned = lax.all_to_all(expert_out, "wide", split_axis=0, concat_axis=0, tiled=True)
    returned_rows = returned.reshape(experts * capacity, returned.shape[2])
    pair_rows = returned_rows[target_slot].astype(jnp.float32)
    weighted = gate_weights.reshape(pairs, 1) * pair_rows
    routed = jnp.sum(weighted.reshape(tok_count, top_count, returned.shape[2]), axis=1)
    blocks = sent_together((shared_gate, shared_up), "wide", 0, 1)
    gate_sum = jnp.dot(tokens, blocks[0], preferred_element_type=jnp.float32)
    up_sum = jnp.dot(tokens, blocks[1], preferred_element_type=jnp.float32)
    shared_hidden = (jax.nn.silu(gate_sum) * up_sum).astype(jnp.bfloat16)
    shared_terms = jnp.dot(
        shared_hidden,
        lax.all_gather(shared_down, "wide", axis=1, tiled=True),
        preferred_element_type=jnp.float32,
    )
    shared = sum_at_owner(shared_terms.astype(jnp.bfloat16), "narrow", 1)
    return (shared + routed).astype(jnp.bfloat16)


def solution(mesh):
    in_specs = (
        P("wide", None),
        P("wide", None),
        P("wide", None),
        P("wide", "narrow"),
        P("wide", "narrow"),
        P("narrow", "wide"),
        P("wide", None, "narrow"),
        P("wide", None, "narrow"),
        P("wide", "narrow", None),
    )
    out_specs = P("wide", "narrow")
    return jax.shard_map(body, mesh=mesh, in_specs=in_specs, out_specs=out_specs, check_vma=False)
```

profile of v0, /device:TPU:1, one launch (start us, length us, event | category | flops | bytes accessed | tf_op | source)
XLA Modules:
  0.0 334.1 jit_solution(4834467579335310039)
XLA Ops:
  6.5 1.7 pad_maximum_fusion.1
  10.3 1.8 reduce-window.6
  12.6 3.4 %scatter_custom_fusion = s32[1024]{0:T(1024)S(1)} fusion(s32[768]{0:T(1024)S(1)} %fusion.85, s32[768]{0:T(1024)S(1)} %iota.11, s32[]{:T(128)} %constant.16.clone.1), kind=kCustom, calls=%fused_computation.79 | custom fusion | bytes 4100 | tf_op jit(solution)/shard_map/scatter | solution.py:86
  16.1 6.1 %gather_fusion = bf16[1024,2048]{1,0:T(8,128)(2,1)} fusion(bf16[128,2048]{1,0:T(8,128)(2,1)S(1)} %copy-done.1, s32[1024]{0:T(1024)S(1)} %fusion.83), kind=kCustom, calls=%fused_computation | custom fusion | bytes 8392704 | tf_op jit(solution)/shard_map/gather | solution.py:90
  22.2 2.5 broadcast_select_fusion
  24.7 1.8 fusion.91
  26.5 68.2 %all_to_all.25 = bf16[64,8,2048]{2,1,0:T(8,128)(2,1)} all-to-all(bf16[64,8,2048]{2,1,0:T(8,128)(2,1)S(1)} %get-tuple-element.6), channel_id=1, replica_groups=mesh['wide'=64,'narrow'=4] {'wide'}, dimensions={0} | all-to-all | bytes 4194304 | tf_op jit(solution)/shard_map/all_to_all | solution.py:20
  94.7 10.2 %all-to-all-start.1 = ((bf16[64,8,2048]{2,1,0:T(8,128)(2,1)}), bf16[64,8,2048]{2,1,0:T(8,128)(2,1)}, u32[]{:S(2)}, u32[]{:S(2)}) async-start(bf16[64,8,2048]{2,1,0:T(8,128)(2,1)} %get-tuple-element.5), calls=%async_computation.1 | async-start | bytes 4194304 | tf_op jit(solution)/shard_map/all_to_all | solution.py:20
  105.7 3.4 %fusion.6 = f32[512,352]{0,1:T(8,128)} fusion(bf16[64,8,2048]{2,1,0:T(8,128)(2,1)} %all_to_all.25, bf16[1,2048,352]{1,2,0:T(8,128)(2,1)S(1)} %copy-done.3), kind=kOutput, calls=%fused_computation.15 | convolution fusion | flops 738197504 | bytes 4259840 | tf_op jit(solution)/shard_map/dot_general | solution.py:52
  109.1 5.7 %convolution_convert_fusion = bf16[512,2048]{1,0:T(8,128)(2,1)} fusion(bf16[1,352,2048]{2,1,0:T(8,128)(2,1)S(1)} %copy-done, bf16[1,2048,352]{1,2,0:T(8,128)(2,1)} %param.16, bf16[64,8,2048]{2,1,0:T(8,128)(2,1)} %all_to_all.25, f32[512,352]{0,1:T(8,128)} %fusion.6), kind=kOutput, calls=%fused_computation.10 | convolution fusion | flops 1478524928 | bytes 7798784 | tf_op jit(solution)/shard_map/dot_general | solution.py:55
  114.8 46.5 %all-to-all-done.1 = bf16[64,8,2048]{2,1,0:T(8,128)(2,1)} async-done(((bf16[64,8,2048]{2,1,0:T(8,128)(2,1)}), bf16[64,8,2048]{2,1,0:T(8,128)(2,1)}, u32[]{:S(2)}, u32[]{:S(2)}) %all-to-all-start.1) | async-done | bytes 2097184 | tf_op jit(solution)/shard_map/all_to_all | solution.py:20
  161.3 3.4 %fusion.10 = f32[512,352]{0,1:T(8,128)} fusion(bf16[64,8,2048]{2,1,0:T(8,128)(2,1)} %all-to-all-done.1, bf16[1,2048,352]{1,2,0:T(8,128)(2,1)S(1)} %copy-done.3), kind=kOutput, calls=%fused_computation.19 | convolution fusion | flops 738197504 | bytes 4259840 | tf_op jit(solution)/shard_map/dot_general | solution.py:52
  164.7 5.8 %convolution_convert_fusion.1 = bf16[512,2048]{1,0:T(8,128)(2,1)} fusion(bf16[1,352,2048]{2,1,0:T(8,128)(2,1)S(1)} %copy-done, bf16[1,2048,352]{1,2,0:T(8,128)(2,1)} %param.16, bf16[64,8,2048]{2,1,0:T(8,128)(2,1)} %all-to-all-done.1, f32[512,352]{0,1:T(8,128)} %fusion.10), kind=kOutput, calls=%fused_computation.11 | convolution fusion | flops 1478524928 | bytes 7798784 | tf_op jit(solution)/shard_map/dot_general | solution.py:55
  170.5 2.5 copy_bitcast_fusion
  173.0 59.4 %all_to_all.26 = bf16[4,64,16,512]{3,2,1,0:T(8,128)(2,1)} all-to-all(bf16[4,64,16,512]{3,2,1,0:T(8,128)(2,1)S(1)} %copy_bitcast_fusion), channel_id=1, replica_groups=mesh['wide'=64,'narrow'=4] {'narrow'}, dimensions={0} | all-to-all | bytes 8388608 | tf_op jit(solution)/shard_map/all_to_all | solution.py:36
  232.4 4.4 %reduce_sum.44 = bf16[64,16,512]{2,1,0:T(8,128)(2,1)} reduce(bf16[4,64,16,512]{3,2,1,0:T(8,128)(2,1)} %all_to_all.26, bf16[]{:T(256)} %constant.35.clone.1), dimensions={0}, to_apply=%region_5.6 | reduce | flops 1572864 | bytes 5242882 | tf_op jit(solution)/shard_map/reduce_sum | solution.py:37
  236.9 9.4 %all-to-all-start.4 = ((bf16[64,16,512]{2,1,0:T(8,128)(2,1)}), bf16[64,16,512]{2,1,0:T(8,128)(2,1)S(1)}, u32[]{:S(2)}, u32[]{:S(2)}) async-start(bf16[64,16,512]{2,1,0:T(8,128)(2,1)} %reduce_sum.44), calls=%async_computation.4 | async-start | bytes 2097152 | tf_op jit(solution)/shard_map/all_to_all | solution.py:98
  246.3 3.6 %fusion.38 = f32[128,704]{0,1:T(8,128)} fusion(bf16[128,2048]{1,0:T(8,128)(2,1)S(1)} %copy-done.1, bf16[2048,1408]{1,0:T(8,128)(2,1)} %all-gather.3.cloned.1.call-done), kind=kOutput, calls=%fused_computation.32 | convolution fusion | flops 369098752 | bytes 4030464 | tf_op jit(solution)/shard_map/dot_general | solution.py:104
  250.0 50.0 %all-gather.5.cloned.1.call-done = bf16[704,2048]{0,1:T(8,128)(2,1)} async-done(((bf16[704,32]{0,1:T(8,128)(2,1)}), bf16[704,2048]{0,1:T(8,128)(2,1)}) %all-gather.5.cloned.1.call-update) | async-done | bytes 2883600 | tf_op jit(solution)/shard_map/all_gather | solution.py:109
  299.9 7.4 %convolution_convert_fusion.2 = bf16[128,2048]{1,0:T(8,128)(2,1)S(1)} fusion(bf16[704,2048]{0,1:T(8,128)(2,1)} %all-gather.5.cloned.1.call-done, bf16[128,2048]{1,0:T(8,128)(2,1)S(1)} %copy-done.1, bf16[2048,1408]{1,0:T(8,128)(2,1)} %all-gather.3.cloned.1.call-done, f32[128,704]{0,1:T(8,128)} %fusion.38), kind=kOutput, calls=%fused_computation.12 | convolution fusion | flops 739000320 | bytes 7700480 | tf_op jit(solution)/shard_map/dot_general | solution.py:107
  308.2 8.4 %all-to-all-start = ((bf16[4,128,512]{2,1,0:T(8,128)(2,1)}), bf16[4,128,512]{2,1,0:T(8,128)(2,1)}, u32[]{:S(2)}, u32[]{:S(2)}) async-start(bf16[4,128,512]{2,1,0:T(8,128)(2,1)} %bitcast.93), calls=%async_computation | async-start | bytes 1048576 | tf_op jit(solution)/shard_map/all_to_all | solution.py:36
  317.3 3.3 gather_fusion.1
  321.9 2.2 multiply_reduce_fusion
  325.7 1.6 add_convert_fusion
  (35 shorter events, 7.8 us)
Async XLA Ops:
  6.5 102.6 %copy-start = (bf16[1,352,2048]{2,1,0:T(8,128)(2,1)S(1)}, bf16[1,352,2048]{2,1,0:T(8,128)(2,1)}, u32[]{:S(2)}) copy-start(bf16[1,352,2048]{2,1,0:T(8,128)(2,1)} %param.17) | copy-start | bytes 4325380
  6.5 9.6 %copy-start.1 = (bf16[128,2048]{1,0:T(8,128)(2,1)S(1)}, bf16[128,2048]{1,0:T(8,128)(2,1)}, u32[]{:S(2)}) copy-start(bf16[128,2048]{1,0:T(8,128)(2,1)} %param.9) | copy-start | bytes 1572868
  6.5 239.8 %all-gather.3.cloned.1.call-start = ((), (), s32[]{:S(2)}) async-start(), calls=%async_computation.5 | async-start | bytes 5857280 | tf_op jit(solution)/shard_map/all_gather | solution.py:46
  94.7 11.0 %copy-start.3 = (bf16[1,2048,352]{1,2,0:T(8,128)(2,1)S(1)}, bf16[1,2048,352]{1,2,0:T(8,128)(2,1)}, u32[]{:S(2)}) copy-start(bf16[1,2048,352]{1,2,0:T(8,128)(2,1)} %param.15) | copy-start | bytes 4325380
  94.7 66.6 %all-to-all-start.1 = ((bf16[64,8,2048]{2,1,0:T(8,128)(2,1)}), bf16[64,8,2048]{2,1,0:T(8,128)(2,1)}, u32[]{:S(2)}, u32[]{:S(2)}) async-start(bf16[64,8,2048]{2,1,0:T(8,128)(2,1)} %get-tuple-element.5), calls=%async_computation.1 | async-start | bytes 4194304 | tf_op jit(solution)/shard_map/all_to_all | solution.py:20
  104.9 195.0 %all-gather.5.cloned.1.call-start = ((), (), s32[]{:S(2)}) async-start(), calls=%async_computation.6 | async-start | bytes 3194880 | tf_op jit(solution)/shard_map/all_gather | solution.py:109
  236.9 71.3 %all-to-all-start.4 = ((bf16[64,16,512]{2,1,0:T(8,128)(2,1)}), bf16[64,16,512]{2,1,0:T(8,128)(2,1)S(1)}, u32[]{:S(2)}, u32[]{:S(2)}) async-start(bf16[64,16,512]{2,1,0:T(8,128)(2,1)} %reduce_sum.44), calls=%async_computation.4 | async-start | bytes 2097152 | tf_op jit(solution)/shard_map/all_to_all | solution.py:98
  307.3 9.2 %copy-start.2 = (f32[128,6]{0,1:T(8,128)S(1)}, f32[128,6]{0,1:T(8,128)}, u32[]{:S(2)}) copy-start(f32[128,6]{0,1:T(8,128)} %param.11) | copy-start | bytes 9220
  308.2 16.3 %all-to-all-start = ((bf16[4,128,512]{2,1,0:T(8,128)(2,1)}), bf16[4,128,512]{2,1,0:T(8,128)(2,1)}, u32[]{:S(2)}, u32[]{:S(2)}) async-start(bf16[4,128,512]{2,1,0:T(8,128)(2,1)} %bitcast.93), calls=%async_computation | async-start | bytes 1048576 | tf_op jit(solution)/shard_map/all_to_all | solution.py:36
Sparse Core Ops, SparseCore 0:
  10.8 162.8 all-gather.2
  177.4 122.4 all-gather.4
where the time goes:
time: 335 us; the launch traced here: 334 us
  blocking collectives  128 us (38%)
  waiting for transfers between devices  97.5 us (29%)
  matrix products  29.3 us (9%)
  starting transfers between devices  28.1 us (8%)
  local copies, waits for them, and re-layouts  19.1 us (6%)
  other arithmetic  18.9 us (6%)
  between operations  13.6 us (4%)
    all_to_all x1, blocking collectives, items_in_groups(): lax.all_to_all(group, axis, split_axis=split_dim, concat_axis=concat_dim,...  68.2 us
    all_to_all x1, blocking collectives, sum_at_owner(): lax.all_to_all(split_up(array, dim, length), axis, 0, 0, tiled=True)  59.4 us
    all_gather x1, waiting for transfers between devices, body(): lax.all_gather(shared_down, 'wide', axis=1, tiled=True)  50 us
    all_to_all x1, waiting for transfers between devices, items_in_groups(): lax.all_to_all(group, axis, split_axis=split_dim, concat_axis=concat_dim,...  46.5 us
    dot_general x2, matrix products, expert_ffn(): jnp.dot(hidden, w_down, preferred_element_type=jnp.float32)  11.5 us
    all_to_all x1, starting transfers between devices, items_in_groups(): lax.all_to_all(group, axis, split_axis=split_dim, concat_axis=concat_dim,...  10.2 us
    all_to_all x1, starting transfers between devices, body(): lax.all_to_all(expert_out, 'wide', split_axis=0, concat_axis=0, tiled=True)  9.44 us
    all_to_all x1, starting transfers between devices, sum_at_owner(): lax.all_to_all(split_up(array, dim, length), axis, 0, 0, tiled=True)  8.38 us
  transfers between devices with their start and end apart: 5, of which 3 were waited for; matrix products, arithmetic and copies ran while one was open for 19% of the time, Pallas kernels for 0%

commit v1 on v0

v1 whole, which is shorter than its diff:
```python
import jax
import jax.numpy as jnp
from jax import lax
from jax.experimental import pallas as pl
from jax.experimental.pallas import tpu as pltpu
from jax.sharding import PartitionSpec as P


F32 = jnp.float32
BF16 = jnp.bfloat16
CAP = 16
EXPERTS = 64
SLOTS = EXPERTS * CAP
TOK = 128
D = 2048
NX = 4
NYZ = 16
X_GROUPS = [[x * NYZ + i for x in range(NX)] for i in range(NYZ)]
YZ_GROUPS = [[x * NYZ + i for i in range(NYZ)] for x in range(NX)]
CORE_SWAP = [(0, 1), (1, 0), (2, 3), (3, 2)]
Y_SWAP = [(0, 2), (2, 0), (1, 3), (3, 1)]
NO_SLOT = 100.0


def x_shift(d):
    return [(x * NYZ + i, (x + d) % NX * NYZ + i) for x in range(NX) for i in range(NYZ)]


def silu(v):
    return v / (1.0 + jnp.exp(-v))


def dot(a, b):
    return lax.dot_general(a, b, (((1,), (0,)), ((), ())), preferred_element_type=F32)


def dot_nt(a, b):
    return lax.dot_general(a, b, (((1,), (1,)), ((), ())), preferred_element_type=F32)


def named_counts(ids, shape, k_axis):
    expert = lax.broadcasted_iota(jnp.int32, shape, k_axis).astype(F32)
    named = jnp.zeros(shape, F32)
    for k in range(ids.shape[k_axis]):
        one = ids[:, k : k + 1] if k_axis else ids[k : k + 1, :]
        named = named + jnp.where(one == expert, 1.0, 0.0)
    return named


def order_matrix(upper):
    row = lax.broadcasted_iota(jnp.int32, (TOK, TOK), 0)
    col = lax.broadcasted_iota(jnp.int32, (TOK, TOK), 1)
    before = row < col if upper else col < row
    return jnp.where(before, 1.0, 0.0).astype(BF16)


def dispatch_kernel(pos_ref, ids_ref, tok_ref, out_ref):
    del pos_ref
    rows = out_ref.shape[0]
    first = pl.program_id(0) * rows
    named = named_counts(ids_ref[...].astype(F32), (EXPERTS, TOK), 0)
    place = dot(named.astype(BF16), order_matrix(True))
    keys = jnp.where(named > 0.0, place, NO_SLOT).astype(BF16)
    r = lax.broadcasted_iota(jnp.int32, (rows, EXPERTS), 0) + first
    e = lax.broadcasted_iota(jnp.int32, (rows, EXPERTS), 1)
    spread = jnp.where((r >> 4) == e, 1.0, 0.0).astype(BF16)
    wanted = dot(spread, keys)
    slot = ((lax.broadcasted_iota(jnp.int32, (rows, TOK), 0) + first) & 15).astype(F32)
    pick = jnp.where(wanted == slot, 1.0, 0.0).astype(BF16)
    out_ref[...] = dot(pick, tok_ref[...]).astype(BF16)


def dispatch(pos, ids_t, tokens):
    blocks = 2
    rows = SLOTS // blocks
    return pl.pallas_call(
        dispatch_kernel,
        grid_spec=pltpu.PrefetchScalarGridSpec(
            num_scalar_prefetch=1,
            grid=(blocks,),
            in_specs=[
                pl.BlockSpec(ids_t.shape, lambda i, p: (0, 0)),
                pl.BlockSpec((TOK, D // 2), lambda i, p: (0, p[0])),
            ],
            out_specs=pl.BlockSpec((rows, D // 2), lambda i, p: (i, 0)),
        ),
        out_shape=jax.ShapeDtypeStruct((SLOTS, D // 2), BF16),
        name="dispatch",
    )(pos, ids_t, tokens)


def pack_kernel(gate_ref, up_ref, down_ref, out_ref):
    fs = out_ref.shape[2] // 3
    for x in range(NX):
        cut = slice(x * fs, (x + 1) * fs)
        out_ref[x] = jnp.concatenate([gate_ref[:, cut], up_ref[:, cut], down_ref[:, cut]], axis=1)


def pack(gate, up, down_t):
    fs = gate.shape[1] // NX
    return pl.pallas_call(
        pack_kernel,
        out_shape=jax.ShapeDtypeStruct((NX, gate.shape[0], 3 * fs), BF16),
        name="pack",
    )(gate, up, down_t)


def expert_kernel(
    pos_ref, own_ref, peer_ref, wg0, wg1, wu0, wu1, wd0, wd1, wd2, wd3, keep_ref, send_ref
):
    del pos_ref
    own = own_ref[...]
    peer = peer_ref[...]
    gate = dot_nt(own, wg0[0]) + dot_nt(peer, wg1[0])
    up = dot_nt(own, wu0[0]) + dot_nt(peer, wu1[0])
    hidden = (silu(gate) * up).astype(BF16)
    keep_ref[:, :512] = dot(hidden, wd0[0]).astype(BF16)
    keep_ref[:, 512:] = dot(hidden, wd1[0]).astype(BF16)
    send_ref[:, :512] = dot(hidden, wd2[0]).astype(BF16)
    send_ref[:, 512:] = dot(hidden, wd3[0]).astype(BF16)


def expert_ffn(pos, own, peer, w_gate, w_up, w_down):
    blocks = 4
    rows = SLOTS // blocks
    mf = w_gate.shape[1]
    x_spec = pl.BlockSpec((rows, D // 2), lambda i, p: (i, 0))
    in_own = pl.BlockSpec((1, mf, D // 2), lambda i, p: (0, 0, p[0]))
    in_peer = pl.BlockSpec((1, mf, D // 2), lambda i, p: (0, 0, 1 - p[0]))
    down = [
        pl.BlockSpec((1, mf, 512), lambda i, p: (0, 0, p[0])),
        pl.BlockSpec((1, mf, 512), lambda i, p: (0, 0, 2 + p[0])),
        pl.BlockSpec((1, mf, 512), lambda i, p: (0, 0, 1 - p[0])),
        pl.BlockSpec((1, mf, 512), lambda i, p: (0, 0, 3 - p[0])),
    ]
    return pl.pallas_call(
        expert_kernel,
        grid_spec=pltpu.PrefetchScalarGridSpec(
            num_scalar_prefetch=1,
            grid=(blocks,),
            in_specs=[x_spec, x_spec, in_own, in_peer, in_own, in_peer] + down,
            out_specs=[x_spec, x_spec],
        ),
        out_shape=[jax.ShapeDtypeStruct((SLOTS, D // 2), BF16)] * 2,
        cost_estimate=pl.CostEstimate(
            flops=2 * SLOTS * D * mf * 3, bytes_accessed=13_000_000, transcendentals=SLOTS * mf
        ),
        name="experts",
    )(pos, own, peer, w_gate, w_gate, w_up, w_up, w_down, w_down, w_down, w_down)


def shared_kernel(pos_ref, tok_ref, w_ref, after_ref, keep_ref, send_ref):
    del after_ref
    core = pos_ref[0]
    fs = w_ref.shape[3] // 3
    rows = w_ref.shape[0] * w_ref.shape[2]
    total = jnp.zeros((TOK, 3 * fs), F32)
    for x in range(NX):
        w = w_ref[:, x].reshape(rows, 3 * fs)
        total = total + dot(tok_ref[0, :, x * rows : (x + 1) * rows], w)
    hidden = silu(total[:, :fs]) * total[:, fs : 2 * fs]
    hidden = jnp.concatenate([jnp.zeros((TOK, 2 * fs), F32), hidden], axis=1).astype(BF16)
    for half in range(2):
        for out_ref, at in ((keep_ref, core), (send_ref, 1 - core)):
            w = w_ref[:, pl.ds(2 * half + at, 1)].reshape(rows, 3 * fs)
            out_ref[0, :, half * 512 : (half + 1) * 512] = dot_nt(hidden, w).astype(BF16)


def shared_ffn(pos, toks, weights, after):
    fs3 = weights.shape[3]
    out_spec = pl.BlockSpec((1, TOK, D // 2), lambda i, p: (i, 0, 0))
    return pl.pallas_call(
        shared_kernel,
        grid_spec=pltpu.PrefetchScalarGridSpec(
            num_scalar_prefetch=1,
            grid=(NX,),
            in_specs=[
                pl.BlockSpec((1, TOK, D), lambda i, p: ((i + p[2]) & 3, 0, 0)),
                pl.BlockSpec(weights.shape, lambda i, p: (0, 0, 0, 0)),
                pl.BlockSpec(memory_space=pl.ANY),
            ],
            out_specs=[out_spec, out_spec],
        ),
        out_shape=[jax.ShapeDtypeStruct((NX, TOK, D // 2), BF16)] * 2,
        cost_estimate=pl.CostEstimate(
            flops=2 * NX * TOK * D * fs3 * 2, bytes_accessed=6_000_000, transcendentals=NX * TOK * fs3 // 3
        ),
        name="shared",
    )(pos, toks, weights, after)


def turned(values):
    row = lax.broadcasted_iota(jnp.int32, (TOK, TOK), 0)
    col = lax.broadcasted_iota(jnp.int32, (TOK, TOK), 1)
    eye = jnp.where(row == col, 1.0, 0.0).astype(BF16)
    total = None
    rest = values
    for _ in range(3):
        part = rest.astype(BF16)
        rest = rest - part.astype(F32)
        moved = dot_nt(eye, part)
        total = moved if total is None else total + moved
    return total


def combine_kernel(pos_ref, ids_ref, gw_ref, ret_ref, sh0, sh1, sh2, sh3, keep_ref, send_ref):
    ids = turned(ids_ref[...].astype(F32))
    gates = turned(gw_ref[...])
    named = named_counts(ids, (TOK, EXPERTS), 1)
    place = dot(order_matrix(False), named.astype(BF16))
    keys = jnp.where(named > 0.0, place, NO_SLOT).astype(BF16)
    lane = lax.broadcasted_iota(jnp.int32, (TOK, EXPERTS), 1).astype(F32)
    weight = jnp.zeros((TOK, EXPERTS), F32)
    for k in range(ids.shape[1]):
        weight = weight + jnp.where(ids[:, k : k + 1] == lane, gates[:, k : k + 1], 0.0)
    e = lax.broadcasted_iota(jnp.int32, (EXPERTS, SLOTS), 0)
    r = lax.broadcasted_iota(jnp.int32, (EXPERTS, SLOTS), 1)
    spread = jnp.where((r >> 4) == e, 1.0, 0.0).astype(BF16)
    slot = (lax.broadcasted_iota(jnp.int32, (TOK, SLOTS), 1) & 15).astype(F32)
    hit = dot(keys, spread) == slot
    ret = ret_ref[...]
    total = jnp.zeros((TOK, D // 2), F32)
    rest = weight
    for _ in range(3):
        part = rest.astype(BF16)
        rest = rest - part.astype(F32)
        row = jnp.where(hit, dot(part, spread), 0.0).astype(BF16)
        total = total + dot(row, ret)
    for shared_ref in (sh0, sh1, sh2, sh3):
        total = total + shared_ref[...].astype(F32)
    low = total[:, :512]
    high = total[:, 512:]
    first = pos_ref[1] == 0
    keep_ref[...] = jnp.where(first, low, high)
    send_ref[...] = jnp.where(first, high, low).astype(BF16)


def combine(pos, ids, gate_weights, returned, shared):
    vmem = pl.BlockSpec(memory_space=pltpu.VMEM)
    return pl.pallas_call(
        combine_kernel,
        in_specs=[pl.BlockSpec(memory_space=pltpu.SMEM)] + [vmem] * 7,
        out_specs=[vmem, vmem],
        out_shape=[
            jax.ShapeDtypeStruct((TOK, 512), F32),
            jax.ShapeDtypeStruct((TOK, 512), BF16),
        ],
        name="combine",
    )(pos, ids, gate_weights, returned, *shared)


def body(
    tokens,
    expert_ids,
    gate_weights,
    shared_gate,
    shared_up,
    shared_down,
    expert_gate,
    expert_up,
    expert_down,
):
    narrow = lax.axis_index("narrow")
    place = lax.axis_index("wide") >> 4
    pos = jnp.stack([narrow & 1, narrow >> 1, place]).astype(jnp.int32)
    ids_t = expert_ids.T
    gates_t = gate_weights.T

    packed = pack(shared_gate, shared_up, shared_down.T)
    packed = lax.all_to_all(packed, "wide", 0, 0, axis_index_groups=X_GROUPS, tiled=True)
    weights = lax.all_gather(packed[None], "wide", axis=0, axis_index_groups=YZ_GROUPS, tiled=True)
    toks = lax.all_gather(tokens[None], "wide", axis=0, axis_index_groups=X_GROUPS, tiled=True)

    outgoing = dispatch(pos, ids_t, tokens).reshape(EXPERTS, CAP, D // 2)
    received = lax.all_to_all(outgoing, "wide", 0, 0, tiled=True).reshape(SLOTS, D // 2)
    peer = lax.ppermute(received, "narrow", CORE_SWAP)
    keep, send = expert_ffn(
        pos, received, peer, expert_gate.transpose(0, 2, 1), expert_up.transpose(0, 2, 1), expert_down
    )
    other = lax.ppermute(send, "narrow", CORE_SWAP)
    summed = (keep.astype(F32) + other.astype(F32)).astype(BF16)
    returned = lax.all_to_all(summed.reshape(EXPERTS, CAP, D // 2), "wide", 0, 0, tiled=True)

    mine, theirs = shared_ffn(pos, toks, weights, summed)
    theirs = lax.ppermute(theirs, "narrow", CORE_SWAP)
    shared = []
    for d in range(NX):
        one = (mine[d].astype(F32) + theirs[d].astype(F32)).astype(BF16)
        if d > 0:
            one = lax.ppermute(one, "wide", x_shift(d))
        shared.append(one)

    kept, sent = combine(pos, ids_t, gates_t, returned.reshape(SLOTS, D // 2), shared)
    got = lax.ppermute(sent, "narrow", Y_SWAP)
    return (kept + got.astype(F32)).astype(BF16)


def solution(mesh):
    in_specs = (
        P("wide", None),
        P("wide", None),
        P("wide", None),
        P("wide", "narrow"),
        P("wide", "narrow"),
        P("narrow", "wide"),
        P("wide", None, "narrow"),
        P("wide", None, "narrow"),
        P("wide", "narrow", None),
    )
    out_specs = P("wide", "narrow")
    return jax.shard_map(body, mesh=mesh, in_specs=in_specs, out_specs=out_specs, check_vma=False)
```

time: 335 us -> 259 us (0.77)
  blocking collectives: 128 us -> 75.3 us
  Pallas kernels: 0 us -> 31.1 us
  matrix products: 29.3 us -> 0 us
  local copies, waits for them, and re-layouts: 19.1 us -> 1.46 us
  other arithmetic: 18.9 us -> 8.44 us
  waiting for transfers between devices: 97.5 us -> 107 us
  starting transfers between devices: 28.1 us -> 20.4 us
    all_to_all x2, blocking collectives: 128 us -> 75.3 us  [the longest x1 64.1 us: body(): lax.all_to_all(outgoing, 'wide', 0, 0, tiled=True).reshape(SLOTS, D // 2)]
    all_to_all x3 -> x1, waiting for transfers between devices: 46.9 us -> 0.01 us  [body(): lax.all_to_all(summed.reshape(EXPERTS, CAP, D // 2), 'wide', 0, 0, tiled=...]
    all_gather x2, waiting for transfers between devices: 50 us -> 86.7 us  [the longest x1 86.6 us: body(): lax.all_gather(packed[None], 'wide', axis=0, axis_index_groups=YZ_GROUPS,...]
    pallas_call x0 -> x5, Pallas kernels: none -> 31.1 us  [the longest x1 12 us: expert_ffn(): pl.pallas_call(expert_kernel, grid_spec=pltpu.PrefetchScalarGridSpec(num_...]
    dot_general x6 -> x0, matrix products: 29.3 us -> none  [the longest x2 11.5 us: expert_ffn(): jnp.dot(hidden, w_down, preferred_element_type=jnp.float32)]
    all_to_all x3 -> x1, starting transfers between devices: 28 us -> 5.57 us  [body(): lax.all_to_all(summed.reshape(EXPERTS, CAP, D // 2), 'wide', 0, 0, tiled=...]
    ppermute x0 -> x7, waiting for transfers between devices: none -> 20.5 us  [the longest x3 10.5 us: body(): one = lax.ppermute(one, 'wide', x_shift(d))]
    ppermute x0 -> x7, starting transfers between devices: none -> 14.8 us  [the longest x1 4.94 us: body(): peer = lax.ppermute(received, 'narrow', CORE_SWAP)]
  transfers between devices with their start and end apart: 5 -> 10, of which waited for: 3 -> 6; matrix products, arithmetic and copies ran while one was open for 19% -> 2% of each run, Pallas kernels for 0% -> 9%
where the time goes in v1:
time: 259 us; the launch traced here: 257 us
  waiting for transfers between devices  107 us (41%)
  blocking collectives  75.3 us (29%)
  Pallas kernels  31.1 us (12%)
  starting transfers between devices  20.4 us (8%)
  between operations  13.5 us (5%)
  other arithmetic  8.44 us (3%)
    all_gather x1, waiting for transfers between devices, body(): lax.all_gather(packed[None], 'wide', axis=0, axis_index_groups=YZ_GROUPS,...  86.6 us
    all_to_all x1, blocking collectives, body(): lax.all_to_all(outgoing, 'wide', 0, 0, tiled=True).reshape(SLOTS, D // 2)  64.1 us
    pallas_call x1, Pallas kernels, expert_ffn(): pl.pallas_call(expert_kernel, grid_spec=pltpu.PrefetchScalarGridSpec(num_...  12 us
    all_to_all x1, blocking collectives, body(): lax.all_to_all(packed, 'wide', 0, 0, axis_index_groups=X_GROUPS, tiled=True)  11.2 us
    ppermute x3, waiting for transfers between devices, body(): one = lax.ppermute(one, 'wide', x_shift(d))  10.5 us
    pallas_call x1, Pallas kernels, shared_ffn(): pl.pallas_call(shared_kernel, grid_spec=pltpu.PrefetchScalarGridSpec(num_...  8.89 us
    all_to_all x1, starting transfers between devices, body(): lax.all_to_all(summed.reshape(EXPERTS, CAP, D // 2), 'wide', 0, 0, tiled=...  5.57 us
  transfers between devices with their start and end apart: 10, of which 6 were waited for; matrix products, arithmetic and copies ran while one was open for 2% of the time, Pallas kernels for 9%

profile of v1, /device:TPU:1, one launch (start us, length us, event | category | flops | bytes accessed | tf_op | source)
XLA Modules:
  0.0 257.4 jit_solution(12616318081589927826)
XLA Ops:
  7.2 4.0 %dispatch.1 = bf16[1024,1024]{1,0:T(8,128)(2,1)} custom-call(s32[3]{0:T(128)} %pad_add_fusion.pos_ref, s32[6,128]{1,0:T(8,128)} %bitcast.27, bf16[128,2048]{1,0:T(8,128)(2,1)} %tok_ref.1), custom_call_target="tpu_custom_call" | custom-call | tf_op jit(solution)/shard_map/dispatch/pallas_call | solution.py:76
  11.2 64.1 %all_to_all.15 = bf16[64,16,1024]{2,1,0:T(8,128)(2,1)S(1)} all-to-all(bf16[64,16,1024]{2,1,0:T(8,128)(2,1)} %bitcast.23), channel_id=1, replica_groups=mesh['wide'=64,'narrow'=4] {'wide'}, dimensions={0} | all-to-all | bytes 4194304 | tf_op jit(solution)/shard_map/all_to_all | solution.py:275
  75.3 4.9 %collective-permute-start = (bf16[1024,1024]{1,0:T(8,128)(2,1)S(1)}, bf16[1024,1024]{1,0:T(8,128)(2,1)}, u32[]{:S(2)}, u32[]{:S(2)}) collective-permute-start(bf16[1024,1024]{1,0:T(8,128)(2,1)S(1)} %bitcast.24), channel_id=1, source_target_pairs={{0,1},{1,0},{2,3},{3,2},{4,5},{5,4},{6,7},{7,6},{8,9},{9,8},{10,11... | collective-permute-start | bytes 6291464 | tf_op jit(solution)/shard_map/ppermute | solution.py:276
  80.3 3.8 %collective-permute-done.peer_ref = bf16[1024,1024]{1,0:T(8,128)(2,1)} collective-permute-done((bf16[1024,1024]{1,0:T(8,128)(2,1)S(1)}, bf16[1024,1024]{1,0:T(8,128)(2,1)}, u32[]{:S(2)}, u32[]{:S(2)}) %collective-permute-start) | collective-permute-done | bytes 2097184 | tf_op jit(solution)/shard_map/ppermute | solution.py:276
  84.1 12.0 %experts.1 = (bf16[1024,1024]{1,0:T(8,128)(2,1)}, bf16[1024,1024]{1,0:T(8,128)(2,1)}) custom-call(s32[3]{0:T(128)} %pad_add_fusion.pos_ref, bf16[1024,1024]{1,0:T(8,128)(2,1)} %bitcast.25, bf16[1024,1024]{1,0:T(8,128)(2,1)} %collective-permute-done.peer_ref, bf16[1,352,2048]{2,1,0:T(8,128)(2,1)} %bitcast.32, bf16[1,352,2048]{2,1,0:T(8,128)(2,1)} %bitcast.33, ...), custom_call_target="tpu_custom_call" | custom-call | flops 4429185024 | bytes 13000000 | tf_op jit(solution)/shard_map/experts/pallas_call | solution.py:136
  96.6 1.6 pack.1
  98.2 11.2 %all_to_all.16 = bf16[4,32,528]{2,1,0:T(8,128)(2,1)} all-to-all(bf16[4,32,528]{2,1,0:T(8,128)(2,1)} %pack.1), channel_id=1, replica_groups={{0,64,128,192},{4,68,132,196},{8,72,136,200},{12,76,140,204},{16,80,144..., dimensions={0} | all-to-all | bytes 270336 | tf_op jit(solution)/shard_map/all_to_all | solution.py:270
  109.5 3.9 %add_convert_fusion.after_ref = bf16[1024,1024]{1,0:T(8,128)(2,1)} fusion(bf16[1024,1024]{1,0:T(8,128)(2,1)S(1)} %collective-permute-done.1, bf16[1024,1024]{1,0:T(8,128)(2,1)} %get-tuple-element.11), kind=kLoop, calls=%fused_computation | loop fusion | flops 4194304 | bytes 6291456 | tf_op jit(solution)/shard_map/convert_element_type | solution.py:281
  113.3 5.6 %all-to-all-start.1 = ((bf16[64,16,1024]{2,1,0:T(8,128)(2,1)}), bf16[64,16,1024]{2,1,0:T(8,128)(2,1)S(1)}, u32[]{:S(2)}, u32[]{:S(2)}) async-start(bf16[64,16,1024]{2,1,0:T(8,128)(2,1)} %bitcast.9), calls=%async_computation.1 | async-start | bytes 4194304 | tf_op jit(solution)/shard_map/all_to_all | solution.py:282
  118.9 86.6 %all-gather.7.cloned.1.call-done = bf16[64,32,528]{2,1,0:T(8,128)(2,1)} async-done(((bf16[4,32,528]{2,1,0:T(8,128)(2,1)}), bf16[64,32,528]{2,1,0:T(8,128)(2,1)}) %all-gather.7.cloned.1.call-update) | async-done | bytes 2162704 | tf_op jit(solution)/shard_map/all_gather | solution.py:271
  205.6 8.9 %shared.1 = (bf16[4,128,1024]{2,1,0:T(8,128)(2,1)}, bf16[4,128,1024]{2,1,0:T(8,128)(2,1)}) custom-call(s32[3]{0:T(128)} %pad_add_fusion.pos_ref, bf16[4,128,2048]{2,1,0:T(8,128)(2,1)} %bitcast.31, bf16[16,4,32,528]{3,2,1,0:T(8,128)(2,1)} %bitcast.30, bf16[1024,1024]{1,0:T(8,128)(2,1)} %add_convert_fusion.after_ref), custom_call_target="tpu_custom_call" | custom-call | flops 2214592512 | bytes 6000000 | tf_op jit(solution)/shard_map/shared/pallas_call | solution.py:172
  214.5 4.7 %collective-permute-start.2 = (bf16[4,128,1024]{2,1,0:T(8,128)(2,1)}, bf16[4,128,1024]{2,1,0:T(8,128)(2,1)S(1)}, u32[]{:S(2)}, u32[]{:S(2)}) collective-permute-start(bf16[4,128,1024]{2,1,0:T(8,128)(2,1)} %get-tuple-element.14), channel_id=1, source_target_pairs={{0,1},{1,0},{2,3},{3,2},{4,5},{5,4},{6,7},{7,6},{8,9},{9,8},{10,11... | collective-permute-start | bytes 3145736 | tf_op jit(solution)/shard_map/ppermute | solution.py:285
  219.2 2.5 collective-permute-done.2
  221.7 2.3 fusion.3
  224.0 0.8 collective-permute-start.3
  224.8 2.4 collective-permute-start.4
  227.2 1.2 collective-permute-start.5
  228.4 4.3 %collective-permute-done.3.sh1 = bf16[128,1024]{1,0:T(8,128)(2,1)S(1)} collective-permute-done((bf16[128,1024]{1,0:T(8,128)(2,1)S(1)}, bf16[128,1024]{1,0:T(8,128)(2,1)S(1)}, u32[]{:S(2)}, u32[]{:S(2)}) %collective-permute-start.3) | collective-permute-done | bytes 262176 | tf_op jit(solution)/shard_map/ppermute | solution.py:290
  232.7 6.2 %collective-permute-done.4.sh2 = bf16[128,1024]{1,0:T(8,128)(2,1)S(1)} collective-permute-done((bf16[128,1024]{1,0:T(8,128)(2,1)S(1)}, bf16[128,1024]{1,0:T(8,128)(2,1)S(1)}, u32[]{:S(2)}, u32[]{:S(2)}) %collective-permute-start.4) | collective-permute-done | bytes 262176 | tf_op jit(solution)/shard_map/ppermute | solution.py:290
  238.9 0.7 copy-done.3
  239.7 0.7 copy-done
  240.3 4.6 %combine.1 = (f32[128,512]{1,0:T(8,128)}, bf16[128,512]{1,0:T(8,128)(2,1)}) custom-call(s32[3]{0:T(128)} %pad_add_fusion.pos_ref, s32[6,128]{1,0:T(8,128)} %bitcast.28, f32[6,128]{1,0:T(8,128)} %bitcast.29, bf16[1024,1024]{1,0:T(8,128)(2,1)} %bitcast.22, bf16[128,1024]{1,0:T(8,128)(2,1)} %get-tuple-element.20.sh0, bf16[128,1024]{1,0:T(8,128)(2,1)} %copy-done.2, ...), custom_call_target="tpu_custom_call" | custom-call | tf_op jit(solution)/shard_map/combine/pallas_call | solution.py:240
  245.2 3.7 %collective-permute-done.6 = bf16[128,512]{1,0:T(8,128)(2,1)S(1)} collective-permute-done((bf16[128,512]{1,0:T(8,128)(2,1)}, bf16[128,512]{1,0:T(8,128)(2,1)S(1)}, u32[]{:S(2)}, u32[]{:S(2)}) %collective-permute-start.6) | collective-permute-done | bytes 131104 | tf_op jit(solution)/shard_map/ppermute | solution.py:294
  248.9 1.6 add_convert_fusion.5
  (19 shorter events, 1.5 us)
Async XLA Ops:
  6.5 112.4 %all-gather.5.cloned.1.call-start = ((), (), s32[]{:S(2)}) async-start(), calls=%async_computation.3 | async-start | bytes 2621440 | tf_op jit(solution)/shard_map/all_gather | solution.py:272
  75.3 8.9 %copy-start.1 = (bf16[64,16,1024]{2,1,0:T(8,128)(2,1)}, bf16[64,16,1024]{2,1,0:T(8,128)(2,1)S(1)}, u32[]{:S(2)}) copy-start(bf16[64,16,1024]{2,1,0:T(8,128)(2,1)S(1)} %all_to_all.15) | copy-start | bytes 6291460
  75.3 8.9 %collective-permute-start = (bf16[1024,1024]{1,0:T(8,128)(2,1)S(1)}, bf16[1024,1024]{1,0:T(8,128)(2,1)}, u32[]{:S(2)}, u32[]{:S(2)}) collective-permute-start(bf16[1024,1024]{1,0:T(8,128)(2,1)S(1)} %bitcast.24), channel_id=1, source_target_pairs={{0,1},{1,0},{2,3},{3,2},{4,5},{5,4},{6,7},{7,6},{8,9},{9,8},{10,11... | collective-permute-start | bytes 6291464 | tf_op jit(solution)/shard_map/ppermute | solution.py:276
  80.3 125.3 %all-gather.7.cloned.1.call-start = ((), (), s32[]{:S(2)}) async-start(), calls=%async_computation.4 | async-start | bytes 2785280 | tf_op jit(solution)/shard_map/all_gather | solution.py:271
  96.2 13.3 %collective-permute-start.1 = (bf16[1024,1024]{1,0:T(8,128)(2,1)}, bf16[1024,1024]{1,0:T(8,128)(2,1)S(1)}, u32[]{:S(2)}, u32[]{:S(2)}) collective-permute-start(bf16[1024,1024]{1,0:T(8,128)(2,1)} %get-tuple-element.12), channel_id=1, source_target_pairs={{0,1},{1,0},{2,3},{3,2},{4,5},{5,4},{6,7},{7,6},{8,9},{9,8},{10,11... | collective-permute-start | bytes 6291464 | tf_op jit(solution)/shard_map/ppermute | solution.py:280
  113.3 125.5 %all-to-all-start.1 = ((bf16[64,16,1024]{2,1,0:T(8,128)(2,1)}), bf16[64,16,1024]{2,1,0:T(8,128)(2,1)S(1)}, u32[]{:S(2)}, u32[]{:S(2)}) async-start(bf16[64,16,1024]{2,1,0:T(8,128)(2,1)} %bitcast.9), calls=%async_computation.1 | async-start | bytes 4194304 | tf_op jit(solution)/shard_map/all_to_all | solution.py:282
  214.5 7.2 %collective-permute-start.2 = (bf16[4,128,1024]{2,1,0:T(8,128)(2,1)}, bf16[4,128,1024]{2,1,0:T(8,128)(2,1)S(1)}, u32[]{:S(2)}, u32[]{:S(2)}) collective-permute-start(bf16[4,128,1024]{2,1,0:T(8,128)(2,1)} %get-tuple-element.14), channel_id=1, source_target_pairs={{0,1},{1,0},{2,3},{3,2},{4,5},{5,4},{6,7},{7,6},{8,9},{9,8},{10,11... | collective-permute-start | bytes 3145736 | tf_op jit(solution)/shard_map/ppermute | solution.py:285
  224.0 8.7 %collective-permute-start.3 = (bf16[128,1024]{1,0:T(8,128)(2,1)S(1)}, bf16[128,1024]{1,0:T(8,128)(2,1)S(1)}, u32[]{:S(2)}, u32[]{:S(2)}) collective-permute-start(bf16[128,1024]{1,0:T(8,128)(2,1)S(1)} %get-tuple-element.19), channel_id=1, source_target_pairs={{0,64},{4,68},{8,72},{12,76},{16,80},{20,84},{24,88},{28,92},{32,9... | collective-permute-start | bytes 786440 | tf_op jit(solution)/shard_map/ppermute | solution.py:290
  224.8 14.0 %collective-permute-start.4 = (bf16[128,1024]{1,0:T(8,128)(2,1)S(1)}, bf16[128,1024]{1,0:T(8,128)(2,1)S(1)}, u32[]{:S(2)}, u32[]{:S(2)}) collective-permute-start(bf16[128,1024]{1,0:T(8,128)(2,1)S(1)} %get-tuple-element.18), channel_id=1, source_target_pairs={{0,128},{4,132},{8,136},{12,140},{16,144},{20,148},{24,152},{28,15... | collective-permute-start | bytes 786440 | tf_op jit(solution)/shard_map/ppermute | solution.py:290
  227.2 11.6 %collective-permute-start.5 = (bf16[128,1024]{1,0:T(8,128)(2,1)S(1)}, bf16[128,1024]{1,0:T(8,128)(2,1)S(1)}, u32[]{:S(2)}, u32[]{:S(2)}) collective-permute-start(bf16[128,1024]{1,0:T(8,128)(2,1)S(1)} %get-tuple-element.17), channel_id=1, source_target_pairs={{0,192},{4,196},{8,200},{12,204},{16,208},{20,212},{24,216},{28,22... | collective-permute-start | bytes 786440 | tf_op jit(solution)/shard_map/ppermute | solution.py:290
  232.7 6.2 %copy-start.2 = (bf16[128,1024]{1,0:T(8,128)(2,1)}, bf16[128,1024]{1,0:T(8,128)(2,1)S(1)}, u32[]{:S(2)}) copy-start(bf16[128,1024]{1,0:T(8,128)(2,1)S(1)} %collective-permute-done.3.sh1) | copy-start | bytes 786436
  238.9 0.7 copy-start.3
  238.9 0.8 copy-start.4
  238.9 1.5 copy-start
  244.9 4.0 %collective-permute-start.6 = (bf16[128,512]{1,0:T(8,128)(2,1)}, bf16[128,512]{1,0:T(8,128)(2,1)S(1)}, u32[]{:S(2)}, u32[]{:S(2)}) collective-permute-start(bf16[128,512]{1,0:T(8,128)(2,1)} %get-tuple-element.16), channel_id=1, source_target_pairs={{0,2},{2,0},{1,3},{3,1},{4,6},{6,4},{5,7},{7,5},{8,10},{10,8},{9,1... | collective-permute-start | bytes 393224 | tf_op jit(solution)/shard_map/ppermute | solution.py:294
Sparse Core Ops, SparseCore 0:
  80.4 27.5 all-gather.4
  110.6 94.9 all-gather.6

commit v2 on v1

--- a/solution.py
+++ b/solution.py
@@ -105,88 +105,104 @@
     )(gate, up, down_t)
 
 
-def expert_kernel(
-    pos_ref, own_ref, peer_ref, wg0, wg1, wu0, wu1, wd0, wd1, wd2, wd3, keep_ref, send_ref
-):
+def hidden_kernel(pos_ref, own_ref, peer_ref, wg0, wg1, wu0, wu1, out_ref):
     del pos_ref
     own = own_ref[...]
     peer = peer_ref[...]
     gate = dot_nt(own, wg0[0]) + dot_nt(peer, wg1[0])
     up = dot_nt(own, wu0[0]) + dot_nt(peer, wu1[0])
-    hidden = (silu(gate) * up).astype(BF16)
-    keep_ref[:, :512] = dot(hidden, wd0[0]).astype(BF16)
-    keep_ref[:, 512:] = dot(hidden, wd1[0]).astype(BF16)
-    send_ref[:, :512] = dot(hidden, wd2[0]).astype(BF16)
-    send_ref[:, 512:] = dot(hidden, wd3[0]).astype(BF16)
-
-
-def expert_ffn(pos, own, peer, w_gate, w_up, w_down):
+    mf = gate.shape[1]
+    out_ref[:, :mf] = (silu(gate) * up).astype(BF16)
+    out_ref[:, mf:] = jnp.zeros((own.shape[0], out_ref.shape[1] - mf), BF16)
+
+
+def expert_hidden(pos, own, peer, w_gate, w_up):
     blocks = 4
     rows = SLOTS // blocks
     mf = w_gate.shape[1]
+    padded = -(-mf // 128) * 128
     x_spec = pl.BlockSpec((rows, D // 2), lambda i, p: (i, 0))
     in_own = pl.BlockSpec((1, mf, D // 2), lambda i, p: (0, 0, p[0]))
     in_peer = pl.BlockSpec((1, mf, D // 2), lambda i, p: (0, 0, 1 - p[0]))
-    down = [
-        pl.BlockSpec((1, mf, 512), lambda i, p: (0, 0, p[0])),
-        pl.BlockSpec((1, mf, 512), lambda i, p: (0, 0, 2 + p[0])),
-        pl.BlockSpec((1, mf, 512), lambda i, p: (0, 0, 1 - p[0])),
-        pl.BlockSpec((1, mf, 512), lambda i, p: (0, 0, 3 - p[0])),
-    ]
-    return pl.pallas_call(
-        expert_kernel,
+    return pl.pallas_call(
+        hidden_kernel,
         grid_spec=pltpu.PrefetchScalarGridSpec(
             num_scalar_prefetch=1,
             grid=(blocks,),
-            in_specs=[x_spec, x_spec, in_own, in_peer, in_own, in_peer] + down,
-            out_specs=[x_spec, x_spec],
-        ),
-        out_shape=[jax.ShapeDtypeStruct((SLOTS, D // 2), BF16)] * 2,
+            in_specs=[x_spec, x_spec, in_own, in_peer, in_own, in_peer],
+            out_specs=pl.BlockSpec((rows, padded), lambda i, p: (i, 0)),
+        ),
+        out_shape=jax.ShapeDtypeStruct((SLOTS, padded), BF16),
         cost_estimate=pl.CostEstimate(
-            flops=2 * SLOTS * D * mf * 3, bytes_accessed=13_000_000, transcendentals=SLOTS * mf
-        ),
-        name="experts",
-    )(pos, own, peer, w_gate, w_gate, w_up, w_up, w_down, w_down, w_down, w_down)
-
-
-def shared_kernel(pos_ref, tok_ref, w_ref, after_ref, keep_ref, send_ref):
+            flops=4 * SLOTS * D * mf, bytes_accessed=8_000_000, transcendentals=SLOTS * mf
+        ),
+        name="hidden",
+    )(pos, own, peer, w_gate, w_gate, w_up, w_up)
+
+
+def down_kernel(pos_ref, own_ref, peer_ref, a0, a1, b0, b1, out_ref):
+    del pos_ref
+    mf = a0.shape[1]
+    own = own_ref[:, :mf]
+    peer = peer_ref[:, :mf]
+    out_ref[:, :512] = (dot(own, a0[0]) + dot(peer, b0[0])).astype(BF16)
+    out_ref[:, 512:] = (dot(own, a1[0]) + dot(peer, b1[0])).astype(BF16)
+
+
+def expert_down_half(pos, own, peer, w_own, w_peer):
+    blocks = 4
+    rows = SLOTS // blocks
+    mf = w_own.shape[1]
+    h_spec = pl.BlockSpec((rows, own.shape[1]), lambda i, p: (i, 0))
+    low = pl.BlockSpec((1, mf, 512), lambda i, p: (0, 0, p[0]))
+    high = pl.BlockSpec((1, mf, 512), lambda i, p: (0, 0, 2 + p[0]))
+    return pl.pallas_call(
+        down_kernel,
+        grid_spec=pltpu.PrefetchScalarGridSpec(
+            num_scalar_prefetch=1,
+            grid=(blocks,),
+            in_specs=[h_spec, h_spec, low, high, low, high],
+            out_specs=pl.BlockSpec((rows, D // 2), lambda i, p: (i, 0)),
+        ),
+        out_shape=jax.ShapeDtypeStruct((SLOTS, D // 2), BF16),
+        cost_estimate=pl.CostEstimate(
+            flops=2 * SLOTS * D * mf, bytes_accessed=5_000_000, transcendentals=0
+        ),
+        name="down",
+    )(pos, own, peer, w_own, w_own, w_peer, w_peer)
+
+
+def shared_kernel(pos_ref, t0, t1, t2, t3, w_ref, after_ref, keep_ref, send_ref):
     del after_ref
     core = pos_ref[0]
     fs = w_ref.shape[3] // 3
     rows = w_ref.shape[0] * w_ref.shape[2]
-    total = jnp.zeros((TOK, 3 * fs), F32)
-    for x in range(NX):
-        w = w_ref[:, x].reshape(rows, 3 * fs)
-        total = total + dot(tok_ref[0, :, x * rows : (x + 1) * rows], w)
-    hidden = silu(total[:, :fs]) * total[:, fs : 2 * fs]
-    hidden = jnp.concatenate([jnp.zeros((TOK, 2 * fs), F32), hidden], axis=1).astype(BF16)
-    for half in range(2):
-        for out_ref, at in ((keep_ref, core), (send_ref, 1 - core)):
-            w = w_ref[:, pl.ds(2 * half + at, 1)].reshape(rows, 3 * fs)
-            out_ref[0, :, half * 512 : (half + 1) * 512] = dot_nt(hidden, w).astype(BF16)
+    for d, tok_ref in enumerate((t0, t1, t2, t3)):
+        total = jnp.zeros((TOK, 3 * fs), F32)
+        for x in range(NX):
+            w = w_ref[:, x].reshape(rows, 3 * fs)
+            total = total + dot(tok_ref[:, x * rows : (x + 1) * rows], w)
+        hidden = silu(total[:, :fs]) * total[:, fs : 2 * fs]
+        hidden = jnp.concatenate([jnp.zeros((TOK, 2 * fs), F32), hidden], axis=1).astype(BF16)
+        for half in range(2):
+            for out_ref, at in ((keep_ref, core), (send_ref, 1 - core)):
+                w = w_ref[:, pl.ds(2 * half + at, 1)].reshape(rows, 3 * fs)
+                out_ref[d, :, half * 512 : (half + 1) * 512] = dot_nt(hidden, w).astype(BF16)
 
 
 def shared_ffn(pos, toks, weights, after):
     fs3 = weights.shape[3]
-    out_spec = pl.BlockSpec((1, TOK, D // 2), lambda i, p: (i, 0, 0))
+    vmem = pl.BlockSpec(memory_space=pltpu.VMEM)
     return pl.pallas_call(
         shared_kernel,
-        grid_spec=pltpu.PrefetchScalarGridSpec(
-            num_scalar_prefetch=1,
-            grid=(NX,),
-            in_specs=[
-                pl.BlockSpec((1, TOK, D), lambda i, p: ((i + p[2]) & 3, 0, 0)),
-                pl.BlockSpec(weights.shape, lambda i, p: (0, 0, 0, 0)),
-                pl.BlockSpec(memory_space=pl.ANY),
-            ],
-            out_specs=[out_spec, out_spec],
-        ),
+        in_specs=[pl.BlockSpec(memory_space=pltpu.SMEM)] + [vmem] * 5 + [pl.BlockSpec(memory_space=pl.ANY)],
+        out_specs=[vmem, vmem],
         out_shape=[jax.ShapeDtypeStruct((NX, TOK, D // 2), BF16)] * 2,
         cost_estimate=pl.CostEstimate(
             flops=2 * NX * TOK * D * fs3 * 2, bytes_accessed=6_000_000, transcendentals=NX * TOK * fs3 // 3
         ),
         name="shared",
-    )(pos, toks, weights, after)
+    )(pos, *toks, weights, after)
 
 
 def turned(values):
@@ -261,24 +277,26 @@
     expert_down,
 ):
     narrow = lax.axis_index("narrow")
-    place = lax.axis_index("wide") >> 4
-    pos = jnp.stack([narrow & 1, narrow >> 1, place]).astype(jnp.int32)
+    pos = jnp.stack([narrow & 1, narrow >> 1]).astype(jnp.int32)
     ids_t = expert_ids.T
     gates_t = gate_weights.T
 
     packed = pack(shared_gate, shared_up, shared_down.T)
     packed = lax.all_to_all(packed, "wide", 0, 0, axis_index_groups=X_GROUPS, tiled=True)
     weights = lax.all_gather(packed[None], "wide", axis=0, axis_index_groups=YZ_GROUPS, tiled=True)
-    toks = lax.all_gather(tokens[None], "wide", axis=0, axis_index_groups=X_GROUPS, tiled=True)
 
     outgoing = dispatch(pos, ids_t, tokens).reshape(EXPERTS, CAP, D // 2)
     received = lax.all_to_all(outgoing, "wide", 0, 0, tiled=True).reshape(SLOTS, D // 2)
+    toks = [tokens]
+    peer_down = lax.ppermute(expert_down, "narrow", CORE_SWAP)
+    for d in range(1, NX):
+        toks.append(lax.ppermute(tokens, "wide", x_shift(d)))
     peer = lax.ppermute(received, "narrow", CORE_SWAP)
-    keep, send = expert_ffn(
-        pos, received, peer, expert_gate.transpose(0, 2, 1), expert_up.transpose(0, 2, 1), expert_down
+    hidden = expert_hidden(
+        pos, received, peer, expert_gate.transpose(0, 2, 1), expert_up.transpose(0, 2, 1)
     )
-    other = lax.ppermute(send, "narrow", CORE_SWAP)
-    summed = (keep.astype(F32) + other.astype(F32)).astype(BF16)
+    peer_hidden = lax.ppermute(hidden, "narrow", CORE_SWAP)
+    summed = expert_down_half(pos, hidden, peer_hidden, expert_down, peer_down)
     returned = lax.all_to_all(summed.reshape(EXPERTS, CAP, D // 2), "wide", 0, 0, tiled=True)
 
     mine, theirs = shared_ffn(pos, toks, weights, summed)
@@ -287,7 +305,7 @@
     for d in range(NX):
         one = (mine[d].astype(F32) + theirs[d].astype(F32)).astype(BF16)
         if d > 0:
-            one = lax.ppermute(one, "wide", x_shift(d))
+            one = lax.ppermute(one, "wide", x_shift(NX - d))
         shared.append(one)
 
     kept, sent = combine(pos, ids_t, gates_t, returned.reshape(SLOTS, D // 2), shared)

time: 259 us -> 238 us (0.919)
  waiting for transfers between devices: 107 us -> 84.6 us
  starting transfers between devices: 20.4 us -> 24.5 us
  other arithmetic: 8.44 us -> 4.49 us
  Pallas kernels: 31.1 us -> 33.7 us
    all_gather x1, waiting for transfers between devices: 86.6 us -> 22.1 us  [body(): lax.all_gather(packed[None], 'wide', axis=0, axis_index_groups=YZ_GROUPS,...]
    ppermute x4 -> x8, waiting for transfers between devices: 10.5 us -> 55.9 us  [the longest x3 39.2 us: body(): toks.append(lax.ppermute(tokens, 'wide', x_shift(d)))]
    ppermute x4 -> x8, starting transfers between devices: 4.77 us -> 9.55 us  [the longest x3 4.76 us: body(): toks.append(lax.ppermute(tokens, 'wide', x_shift(d)))]
    convert_element_type x1 -> x0, other arithmetic: 3.86 us -> none  [body(): summed = (keep.astype(F32) + other.astype(F32)).astype(BF16)]
    ppermute x1, waiting for transfers between devices: 3.84 us -> 0.01 us  [body(): peer = lax.ppermute(received, 'narrow', CORE_SWAP)]
    pallas_call x2 -> x3, Pallas kernels: 20.9 us -> 23.6 us  [the longest x1 8.58 us: expert_hidden(): pl.pallas_call(hidden_kernel, grid_spec=pltpu.PrefetchScalarGridSpec(num_...]
  transfers between devices with their start and end apart: 10 -> 13, of which waited for: 6 -> 8; matrix products, arithmetic and copies ran while one was open for 2% -> 1% of each run, Pallas kernels for 9% -> 11%
where the time goes in v2:
time: 238 us; the launch traced here: 237 us
  waiting for transfers between devices  84.6 us (36%)
  blocking collectives  74.1 us (31%)
  Pallas kernels  33.7 us (14%)
  starting transfers between devices  24.5 us (10%)
  between operations  13.4 us (6%)
  other arithmetic  4.49 us (2%)
    all_to_all x1, blocking collectives, body(): lax.all_to_all(outgoing, 'wide', 0, 0, tiled=True).reshape(SLOTS, D // 2)  64.3 us
    ppermute x3, waiting for transfers between devices, body(): toks.append(lax.ppermute(tokens, 'wide', x_shift(d)))  39.2 us
    all_gather x1, waiting for transfers between devices, body(): lax.all_gather(packed[None], 'wide', axis=0, axis_index_groups=YZ_GROUPS,...  22.1 us
    ppermute x3, waiting for transfers between devices, body(): one = lax.ppermute(one, 'wide', x_shift(NX - d))  14.1 us
    all_to_all x1, blocking collectives, body(): lax.all_to_all(packed, 'wide', 0, 0, axis_index_groups=X_GROUPS, tiled=True)  9.74 us
    pallas_call x1, Pallas kernels, expert_hidden(): pl.pallas_call(hidden_kernel, grid_spec=pltpu.PrefetchScalarGridSpec(num_...  8.58 us
    pallas_call x1, Pallas kernels, shared_ffn(): pl.pallas_call(shared_kernel, in_specs=[pl.BlockSpec(memory_space=pltpu.S...  8.54 us
    pallas_call x1, Pallas kernels, expert_down_half(): pl.pallas_call(down_kernel, grid_spec=pltpu.PrefetchScalarGridSpec(num_sc...  6.45 us
  transfers between devices with their start and end apart: 13, of which 8 were waited for; matrix products, arithmetic and copies ran while one was open for 1% of the time, Pallas kernels for 11%

profile of v2, /device:TPU:1, one launch (start us, length us, event | category | flops | bytes accessed | tf_op | source)
XLA Modules:
  0.0 237.0 jit_solution(246105320005508052)
XLA Ops:
  7.1 4.0 %dispatch.1 = bf16[1024,1024]{1,0:T(8,128)(2,1)} custom-call(s32[2]{0:T(128)} %pad_add_fusion.pos_ref, s32[6,128]{1,0:T(8,128)} %bitcast.24, bf16[128,2048]{1,0:T(8,128)(2,1)} %t0.1), custom_call_target="tpu_custom_call" | custom-call | tf_op jit(solution)/shard_map/dispatch/pallas_call | solution.py:76
  11.1 64.3 %all_to_all.15 = bf16[64,16,1024]{2,1,0:T(8,128)(2,1)} all-to-all(bf16[64,16,1024]{2,1,0:T(8,128)(2,1)} %bitcast.22), channel_id=1, replica_groups=mesh['wide'=64,'narrow'=4] {'wide'}, dimensions={0} | all-to-all | bytes 4194304 | tf_op jit(solution)/shard_map/all_to_all | solution.py:289
  75.4 4.9 %collective-permute-start = (bf16[1024,1024]{1,0:T(8,128)(2,1)}, bf16[1024,1024]{1,0:T(8,128)(2,1)}, u32[]{:S(2)}, u32[]{:S(2)}) collective-permute-start(bf16[1024,1024]{1,0:T(8,128)(2,1)} %bitcast.5.own_ref), channel_id=1, source_target_pairs={{0,1},{1,0},{2,3},{3,2},{4,5},{5,4},{6,7},{7,6},{8,9},{9,8},{10,11... | collective-permute-start | bytes 6291464 | tf_op jit(solution)/shard_map/ppermute | solution.py:294
  80.4 1.6 pack.1
  82.0 9.7 %all_to_all.16 = bf16[4,32,528]{2,1,0:T(8,128)(2,1)} all-to-all(bf16[4,32,528]{2,1,0:T(8,128)(2,1)} %pack.1), channel_id=1, replica_groups={{0,64,128,192},{4,68,132,196},{8,72,136,200},{12,76,140,204},{16,80,144..., dimensions={0} | all-to-all | bytes 270336 | tf_op jit(solution)/shard_map/all_to_all | solution.py:285
  92.7 8.6 %hidden.1.own_ref = bf16[1024,384]{1,0:T(8,128)(2,1)} custom-call(s32[2]{0:T(128)} %pad_add_fusion.pos_ref, bf16[1024,1024]{1,0:T(8,128)(2,1)} %bitcast.5.own_ref, bf16[1024,1024]{1,0:T(8,128)(2,1)} %collective-permute-done.peer_ref, bf16[1,352,2048]{2,1,0:T(8,128)(2,1)} %bitcast.28, bf16[1,352,2048]{2,1,0:T(8,128)(2,1)} %bitcast.29, ...), custom_call_target="tpu_custom_call" | custom-call | flops 2952790016 | bytes 8000000 | tf_op jit(solution)/shard_map/hidden/pallas_call | solution.py:127
  101.3 2.6 %collective-permute-done.1.peer_ref = bf16[1024,384]{1,0:T(8,128)(2,1)} collective-permute-done((bf16[1024,384]{1,0:T(8,128)(2,1)}, bf16[1024,384]{1,0:T(8,128)(2,1)}, u32[]{:S(2)}, u32[]{:S(2)}) %collective-permute-start.1) | collective-permute-done | bytes 786464 | tf_op jit(solution)/shard_map/ppermute | solution.py:298
  103.9 6.4 %down.1.after_ref = bf16[1024,1024]{1,0:T(8,128)(2,1)} custom-call(s32[2]{0:T(128)} %pad_add_fusion.pos_ref, bf16[1024,384]{1,0:T(8,128)(2,1)} %hidden.1.own_ref, bf16[1024,384]{1,0:T(8,128)(2,1)} %collective-permute-done.1.peer_ref, bf16[1,352,2048]{2,1,0:T(8,128)(2,1)} %a1.1, bf16[1,352,2048]{2,1,0:T(8,128)(2,1)} %a1.1, bf16[1,352,2048]{2,1,0:T(8,128)(2,1)} %copy-done.2, ...), custom_call_target="tpu_custom_call" | custom-call | flops 1476395008 | bytes 5000000 | tf_op jit(solution)/shard_map/down/pallas_call | solution.py:159
  110.4 5.4 %all-to-all-start.1 = ((bf16[64,16,1024]{2,1,0:T(8,128)(2,1)}), bf16[64,16,1024]{2,1,0:T(8,128)(2,1)S(1)}, u32[]{:S(2)}, u32[]{:S(2)}) async-start(bf16[64,16,1024]{2,1,0:T(8,128)(2,1)} %bitcast.20), calls=%async_computation.1 | async-start | bytes 4194304 | tf_op jit(solution)/shard_map/all_to_all | solution.py:300
  115.8 1.1 collective-permute-start.3
  116.9 2.6 %collective-permute-start.4 = (bf16[128,2048]{1,0:T(8,128)(2,1)S(1)}, bf16[128,2048]{1,0:T(8,128)(2,1)S(1)}, u32[]{:S(2)}, u32[]{:S(2)}) collective-permute-start(bf16[128,2048]{1,0:T(8,128)(2,1)S(1)} %copy-done.3), channel_id=1, source_target_pairs={{0,128},{4,132},{8,136},{12,140},{16,144},{20,148},{24,152},{28,15... | collective-permute-start | bytes 1572872 | tf_op jit(solution)/shard_map/ppermute | solution.py:293
  120.6 20.5 %collective-permute-done.3.t1 = bf16[128,2048]{1,0:T(8,128)(2,1)S(1)} collective-permute-done((bf16[128,2048]{1,0:T(8,128)(2,1)S(1)}, bf16[128,2048]{1,0:T(8,128)(2,1)S(1)}, u32[]{:S(2)}, u32[]{:S(2)}) %collective-permute-start.3) | collective-permute-done | bytes 524320 | tf_op jit(solution)/shard_map/ppermute | solution.py:293
  141.1 18.7 %collective-permute-done.4.t2 = bf16[128,2048]{1,0:T(8,128)(2,1)S(1)} collective-permute-done((bf16[128,2048]{1,0:T(8,128)(2,1)S(1)}, bf16[128,2048]{1,0:T(8,128)(2,1)S(1)}, u32[]{:S(2)}, u32[]{:S(2)}) %collective-permute-start.4) | collective-permute-done | bytes 524320 | tf_op jit(solution)/shard_map/ppermute | solution.py:293
  160.6 22.1 %all-gather.3.cloned.1.call-done = bf16[64,32,528]{2,1,0:T(8,128)(2,1)} async-done(((bf16[4,32,528]{2,1,0:T(8,128)(2,1)}), bf16[64,32,528]{2,1,0:T(8,128)(2,1)}) %all-gather.3.cloned.1.call-update) | async-done | bytes 2162704 | tf_op jit(solution)/shard_map/all_gather | solution.py:286
  182.6 8.5 %shared.1 = (bf16[4,128,1024]{2,1,0:T(8,128)(2,1)}, bf16[4,128,1024]{2,1,0:T(8,128)(2,1)}) custom-call(s32[2]{0:T(128)} %pad_add_fusion.pos_ref, bf16[128,2048]{1,0:T(8,128)(2,1)} %t0.1, bf16[128,2048]{1,0:T(8,128)(2,1)} %copy-done.7, bf16[128,2048]{1,0:T(8,128)(2,1)} %copy-done.8, bf16[128,2048]{1,0:T(8,128)(2,1)} %collective-permute-done.5.t3, ...), custom_call_target="tpu_custom_call" | custom-call | flops 2214592512 | bytes 6000000 | tf_op jit(solution)/shard_map/shared/pallas_call | solution.py:196
  191.2 3.9 %collective-permute-start.6 = (bf16[4,128,1024]{2,1,0:T(8,128)(2,1)}, bf16[4,128,1024]{2,1,0:T(8,128)(2,1)S(1)}, u32[]{:S(2)}, u32[]{:S(2)}) collective-permute-start(bf16[4,128,1024]{2,1,0:T(8,128)(2,1)} %get-tuple-element.10), channel_id=1, source_target_pairs={{0,1},{1,0},{2,3},{3,2},{4,5},{5,4},{6,7},{7,6},{8,9},{9,8},{10,11... | collective-permute-start | bytes 3145736 | tf_op jit(solution)/shard_map/ppermute | solution.py:303
  195.1 2.5 %collective-permute-done.6 = bf16[4,128,1024]{2,1,0:T(8,128)(2,1)S(1)} collective-permute-done((bf16[4,128,1024]{2,1,0:T(8,128)(2,1)}, bf16[4,128,1024]{2,1,0:T(8,128)(2,1)S(1)}, u32[]{:S(2)}, u32[]{:S(2)}) %collective-permute-start.6) | collective-permute-done | bytes 1048608 | tf_op jit(solution)/shard_map/ppermute | solution.py:303
  197.6 2.3 fusion.3
  199.9 2.6 %collective-permute-start.7 = (bf16[128,1024]{1,0:T(8,128)(2,1)S(1)}, bf16[128,1024]{1,0:T(8,128)(2,1)S(1)}, u32[]{:S(2)}, u32[]{:S(2)}) collective-permute-start(bf16[128,1024]{1,0:T(8,128)(2,1)S(1)} %get-tuple-element.15), channel_id=1, source_target_pairs={{0,192},{4,196},{8,200},{12,204},{16,208},{20,212},{24,216},{28,22... | collective-permute-start | bytes 786440 | tf_op jit(solution)/shard_map/ppermute | solution.py:308
  203.7 9.5 %collective-permute-done.7.sh1 = bf16[128,1024]{1,0:T(8,128)(2,1)S(1)} collective-permute-done((bf16[128,1024]{1,0:T(8,128)(2,1)S(1)}, bf16[128,1024]{1,0:T(8,128)(2,1)S(1)}, u32[]{:S(2)}, u32[]{:S(2)}) %collective-permute-start.7) | collective-permute-done | bytes 262176 | tf_op jit(solution)/shard_map/ppermute | solution.py:308
  213.2 4.6 %collective-permute-done.9.sh3 = bf16[128,1024]{1,0:T(8,128)(2,1)S(1)} collective-permute-done((bf16[128,1024]{1,0:T(8,128)(2,1)S(1)}, bf16[128,1024]{1,0:T(8,128)(2,1)S(1)}, u32[]{:S(2)}, u32[]{:S(2)}) %collective-permute-start.9) | collective-permute-done | bytes 262176 | tf_op jit(solution)/shard_map/ppermute | solution.py:308
  219.2 4.6 %combine.1 = (f32[128,512]{1,0:T(8,128)}, bf16[128,512]{1,0:T(8,128)(2,1)}) custom-call(s32[2]{0:T(128)} %pad_add_fusion.pos_ref, s32[6,128]{1,0:T(8,128)} %bitcast.25, f32[6,128]{1,0:T(8,128)} %bitcast.26, bf16[1024,1024]{1,0:T(8,128)(2,1)} %bitcast.21, bf16[128,1024]{1,0:T(8,128)(2,1)} %get-tuple-element.16.sh0, bf16[128,1024]{1,0:T(8,128)(2,1)} %copy-done.4, ...), custom_call_target="tpu_custom_call" | custom-call | tf_op jit(solution)/shard_map/combine/pallas_call | solution.py:256
  224.4 4.1 %collective-permute-done.10 = bf16[128,512]{1,0:T(8,128)(2,1)S(1)} collective-permute-done((bf16[128,512]{1,0:T(8,128)(2,1)}, bf16[128,512]{1,0:T(8,128)(2,1)S(1)}, u32[]{:S(2)}, u32[]{:S(2)}) %collective-permute-start.10) | collective-permute-done | bytes 131104 | tf_op jit(solution)/shard_map/ppermute | solution.py:312
  228.5 1.6 add_convert_fusion.4
  (32 shorter events, 6.8 us)
Async XLA Ops:
  6.5 176.1 %all-gather.3.cloned.1.call-start = ((), (), s32[]{:S(2)}) async-start(), calls=%async_computation.3 | async-start | bytes 2785280 | tf_op jit(solution)/shard_map/all_gather | solution.py:286
  11.1 80.7 %copy-start.1 = (bf16[1,352,2048]{2,1,0:T(8,128)(2,1)S(1)}, bf16[1,352,2048]{2,1,0:T(8,128)(2,1)}, u32[]{:S(2)}) copy-start(bf16[1,352,2048]{2,1,0:T(8,128)(2,1)} %a1.1) | copy-start | bytes 4325380
  75.4 17.3 %collective-permute-start = (bf16[1024,1024]{1,0:T(8,128)(2,1)}, bf16[1024,1024]{1,0:T(8,128)(2,1)}, u32[]{:S(2)}, u32[]{:S(2)}) collective-permute-start(bf16[1024,1024]{1,0:T(8,128)(2,1)} %bitcast.5.own_ref), channel_id=1, source_target_pairs={{0,1},{1,0},{2,3},{3,2},{4,5},{5,4},{6,7},{7,6},{8,9},{9,8},{10,11... | collective-permute-start | bytes 6291464 | tf_op jit(solution)/shard_map/ppermute | solution.py:294
  91.8 9.6 %collective-permute-start.2 = (bf16[1,352,2048]{2,1,0:T(8,128)(2,1)S(1)}, bf16[1,352,2048]{2,1,0:T(8,128)(2,1)S(1)}, u32[]{:S(2)}, u32[]{:S(2)}) collective-permute-start(bf16[1,352,2048]{2,1,0:T(8,128)(2,1)S(1)} %copy-done.1), channel_id=1, source_target_pairs={{0,1},{1,0},{2,3},{3,2},{4,5},{5,4},{6,7},{7,6},{8,9},{9,8},{10,11... | collective-permute-start | bytes 4325384 | tf_op jit(solution)/shard_map/ppermute | solution.py:291
  101.3 2.6 %collective-permute-start.1 = (bf16[1024,384]{1,0:T(8,128)(2,1)}, bf16[1024,384]{1,0:T(8,128)(2,1)}, u32[]{:S(2)}, u32[]{:S(2)}) collective-permute-start(bf16[1024,384]{1,0:T(8,128)(2,1)} %hidden.1.own_ref), channel_id=1, source_target_pairs={{0,1},{1,0},{2,3},{3,2},{4,5},{5,4},{6,7},{7,6},{8,9},{9,8},{10,11... | collective-permute-start | bytes 2359304 | tf_op jit(solution)/shard_map/ppermute | solution.py:298
  101.3 2.6 %copy-start.2 = (bf16[1,352,2048]{2,1,0:T(8,128)(2,1)}, bf16[1,352,2048]{2,1,0:T(8,128)(2,1)S(1)}, u32[]{:S(2)}) copy-start(bf16[1,352,2048]{2,1,0:T(8,128)(2,1)S(1)} %collective-permute-done.2.b0.b1) | copy-start | bytes 4325380
  110.4 5.4 %copy-start.3 = (bf16[128,2048]{1,0:T(8,128)(2,1)S(1)}, bf16[128,2048]{1,0:T(8,128)(2,1)}, u32[]{:S(2)}) copy-start(bf16[128,2048]{1,0:T(8,128)(2,1)} %t0.1) | copy-start | bytes 1572868
  110.4 107.4 %all-to-all-start.1 = ((bf16[64,16,1024]{2,1,0:T(8,128)(2,1)}), bf16[64,16,1024]{2,1,0:T(8,128)(2,1)S(1)}, u32[]{:S(2)}, u32[]{:S(2)}) async-start(bf16[64,16,1024]{2,1,0:T(8,128)(2,1)} %bitcast.20), calls=%async_computation.1 | async-start | bytes 4194304 | tf_op jit(solution)/shard_map/all_to_all | solution.py:300
  115.8 25.3 %collective-permute-start.3 = (bf16[128,2048]{1,0:T(8,128)(2,1)S(1)}, bf16[128,2048]{1,0:T(8,128)(2,1)S(1)}, u32[]{:S(2)}, u32[]{:S(2)}) collective-permute-start(bf16[128,2048]{1,0:T(8,128)(2,1)S(1)} %copy-done.3), channel_id=1, source_target_pairs={{0,64},{4,68},{8,72},{12,76},{16,80},{20,84},{24,88},{28,92},{32,9... | collective-permute-start | bytes 1572872 | tf_op jit(solution)/shard_map/ppermute | solution.py:293
  116.9 42.9 %collective-permute-start.4 = (bf16[128,2048]{1,0:T(8,128)(2,1)S(1)}, bf16[128,2048]{1,0:T(8,128)(2,1)S(1)}, u32[]{:S(2)}, u32[]{:S(2)}) collective-permute-start(bf16[128,2048]{1,0:T(8,128)(2,1)S(1)} %copy-done.3), channel_id=1, source_target_pairs={{0,128},{4,132},{8,136},{12,140},{16,144},{20,148},{24,152},{28,15... | collective-permute-start | bytes 1572872 | tf_op jit(solution)/shard_map/ppermute | solution.py:293
  119.5 41.1 %collective-permute-start.5 = (bf16[128,2048]{1,0:T(8,128)(2,1)S(1)}, bf16[128,2048]{1,0:T(8,128)(2,1)}, u32[]{:S(2)}, u32[]{:S(2)}) collective-permute-start(bf16[128,2048]{1,0:T(8,128)(2,1)S(1)} %copy-done.3), channel_id=1, source_target_pairs={{0,192},{4,196},{8,200},{12,204},{16,208},{20,212},{24,216},{28,22... | collective-permute-start | bytes 1572872 | tf_op jit(solution)/shard_map/ppermute | solution.py:293
  141.1 41.5 %copy-start.7 = (bf16[128,2048]{1,0:T(8,128)(2,1)}, bf16[128,2048]{1,0:T(8,128)(2,1)S(1)}, u32[]{:S(2)}) copy-start(bf16[128,2048]{1,0:T(8,128)(2,1)S(1)} %collective-permute-done.3.t1) | copy-start | bytes 1572868
  159.8 0.8 copy-start.8
  191.2 6.4 %collective-permute-start.6 = (bf16[4,128,1024]{2,1,0:T(8,128)(2,1)}, bf16[4,128,1024]{2,1,0:T(8,128)(2,1)S(1)}, u32[]{:S(2)}, u32[]{:S(2)}) collective-permute-start(bf16[4,128,1024]{2,1,0:T(8,128)(2,1)} %get-tuple-element.10), channel_id=1, source_target_pairs={{0,1},{1,0},{2,3},{3,2},{4,5},{5,4},{6,7},{7,6},{8,9},{9,8},{10,11... | collective-permute-start | bytes 3145736 | tf_op jit(solution)/shard_map/ppermute | solution.py:303
  199.9 13.3 %collective-permute-start.7 = (bf16[128,1024]{1,0:T(8,128)(2,1)S(1)}, bf16[128,1024]{1,0:T(8,128)(2,1)S(1)}, u32[]{:S(2)}, u32[]{:S(2)}) collective-permute-start(bf16[128,1024]{1,0:T(8,128)(2,1)S(1)} %get-tuple-element.15), channel_id=1, source_target_pairs={{0,192},{4,196},{8,200},{12,204},{16,208},{20,212},{24,216},{28,22... | collective-permute-start | bytes 786440 | tf_op jit(solution)/shard_map/ppermute | solution.py:308
  202.4 10.8 %collective-permute-start.8 = (bf16[128,1024]{1,0:T(8,128)(2,1)S(1)}, bf16[128,1024]{1,0:T(8,128)(2,1)S(1)}, u32[]{:S(2)}, u32[]{:S(2)}) collective-permute-start(bf16[128,1024]{1,0:T(8,128)(2,1)S(1)} %get-tuple-element.14), channel_id=1, source_target_pairs={{0,128},{4,132},{8,136},{12,140},{16,144},{20,148},{24,152},{28,15... | collective-permute-start | bytes 786440 | tf_op jit(solution)/shard_map/ppermute | solution.py:308
  203.1 14.7 %collective-permute-start.9 = (bf16[128,1024]{1,0:T(8,128)(2,1)S(1)}, bf16[128,1024]{1,0:T(8,128)(2,1)S(1)}, u32[]{:S(2)}, u32[]{:S(2)}) collective-permute-start(bf16[128,1024]{1,0:T(8,128)(2,1)S(1)} %get-tuple-element.13), channel_id=1, source_target_pairs={{0,64},{4,68},{8,72},{12,76},{16,80},{20,84},{24,88},{28,92},{32,9... | collective-permute-start | bytes 786440 | tf_op jit(solution)/shard_map/ppermute | solution.py:308
  213.2 4.6 %copy-start.4 = (bf16[128,1024]{1,0:T(8,128)(2,1)}, bf16[128,1024]{1,0:T(8,128)(2,1)S(1)}, u32[]{:S(2)}) copy-start(bf16[128,1024]{1,0:T(8,128)(2,1)S(1)} %collective-permute-done.7.sh1) | copy-start | bytes 786436
  213.2 4.6 %copy-start.5 = (bf16[128,1024]{1,0:T(8,128)(2,1)}, bf16[128,1024]{1,0:T(8,128)(2,1)S(1)}, u32[]{:S(2)}) copy-start(bf16[128,1024]{1,0:T(8,128)(2,1)S(1)} %collective-permute-done.8.sh2) | copy-start | bytes 786436
  217.8 0.7 copy-start.6
  217.8 1.4 copy-start
  223.8 4.8 %collective-permute-start.10 = (bf16[128,512]{1,0:T(8,128)(2,1)}, bf16[128,512]{1,0:T(8,128)(2,1)S(1)}, u32[]{:S(2)}, u32[]{:S(2)}) collective-permute-start(bf16[128,512]{1,0:T(8,128)(2,1)} %get-tuple-element.12), channel_id=1, source_target_pairs={{0,2},{2,0},{1,3},{3,1},{4,6},{6,4},{5,7},{7,5},{8,10},{10,8},{9,1... | collective-permute-start | bytes 393224 | tf_op jit(solution)/shard_map/ppermute | solution.py:312
Sparse Core Ops, SparseCore 0:
  91.9 90.7 all-gather.2

commit v3 on v2

--- a/solution.py
+++ b/solution.py
@@ -19,6 +19,11 @@
 YZ_GROUPS = [[x * NYZ + i for i in range(NYZ)] for x in range(NX)]
 CORE_SWAP = [(0, 1), (1, 0), (2, 3), (3, 2)]
 Y_SWAP = [(0, 2), (2, 0), (1, 3), (3, 1)]
+BOTH_SWAP = [(0, 3), (3, 0), (1, 2), (2, 1)]
+COLS = D // 4
+CHUNKS = 2
+CHUNK_ROWS = SLOTS // CHUNKS
+STEP_ROWS = 256
 NO_SLOT = 100.0
 
 
@@ -80,11 +85,11 @@
             grid=(blocks,),
             in_specs=[
                 pl.BlockSpec(ids_t.shape, lambda i, p: (0, 0)),
-                pl.BlockSpec((TOK, D // 2), lambda i, p: (0, p[0])),
+                pl.BlockSpec((TOK, COLS), lambda i, p: (0, p[0])),
             ],
-            out_specs=pl.BlockSpec((rows, D // 2), lambda i, p: (i, 0)),
-        ),
-        out_shape=jax.ShapeDtypeStruct((SLOTS, D // 2), BF16),
+            out_specs=pl.BlockSpec((rows, COLS), lambda i, p: (i, 0)),
+        ),
+        out_shape=jax.ShapeDtypeStruct((SLOTS, COLS), BF16),
         name="dispatch",
     )(pos, ids_t, tokens)
 
@@ -105,76 +110,112 @@
     )(gate, up, down_t)
 
 
-def hidden_kernel(pos_ref, own_ref, peer_ref, wg0, wg1, wu0, wu1, out_ref):
+def cut_kernel(pos_ref, a, b, c, out_a, out_b, out_c):
     del pos_ref
-    own = own_ref[...]
-    peer = peer_ref[...]
-    gate = dot_nt(own, wg0[0]) + dot_nt(peer, wg1[0])
-    up = dot_nt(own, wu0[0]) + dot_nt(peer, wu1[0])
+    out_a[...] = a[0]
+    out_b[...] = b[0]
+    out_c[...] = c[0]
+
+
+def cut(pos, w_down):
+    mf = w_down.shape[1]
+    return pl.pallas_call(
+        cut_kernel,
+        grid_spec=pltpu.PrefetchScalarGridSpec(
+            num_scalar_prefetch=1,
+            grid=(1,),
+            in_specs=[
+                pl.BlockSpec((1, mf, COLS), lambda i, p: (0, 0, p[0] ^ 1)),
+                pl.BlockSpec((1, mf, COLS), lambda i, p: (0, 0, p[0] ^ 2)),
+                pl.BlockSpec((1, mf, COLS), lambda i, p: (0, 0, p[0] ^ 3)),
+            ],
+            out_specs=[pl.BlockSpec((mf, COLS), lambda i, p: (0, 0))] * 3,
+        ),
+        out_shape=[jax.ShapeDtypeStruct((mf, COLS), BF16)] * 3,
+        name="cut",
+    )(pos, w_down, w_down, w_down)
+
+
+def hidden_kernel(pos_ref, x0, x1, x2, x3, g0, g1, g2, g3, u0, u1, u2, u3, out_ref):
+    del pos_ref
+    gate = jnp.zeros((x0.shape[0], g0.shape[1]), F32)
+    up = gate
+    for x, g, u in ((x0, g0, u0), (x1, g1, u1), (x2, g2, u2), (x3, g3, u3)):
+        rows = x[...]
+        gate = gate + dot_nt(rows, g[0])
+        up = up + dot_nt(rows, u[0])
     mf = gate.shape[1]
     out_ref[:, :mf] = (silu(gate) * up).astype(BF16)
-    out_ref[:, mf:] = jnp.zeros((own.shape[0], out_ref.shape[1] - mf), BF16)
-
-
-def expert_hidden(pos, own, peer, w_gate, w_up):
-    blocks = 4
-    rows = SLOTS // blocks
+    out_ref[:, mf:] = jnp.zeros((gate.shape[0], out_ref.shape[1] - mf), BF16)
+
+
+def expert_hidden(pos, chunk, own, core, y, both, w_gate, w_up):
+    steps = CHUNK_ROWS // STEP_ROWS
     mf = w_gate.shape[1]
     padded = -(-mf // 128) * 128
-    x_spec = pl.BlockSpec((rows, D // 2), lambda i, p: (i, 0))
-    in_own = pl.BlockSpec((1, mf, D // 2), lambda i, p: (0, 0, p[0]))
-    in_peer = pl.BlockSpec((1, mf, D // 2), lambda i, p: (0, 0, 1 - p[0]))
+    whole = pl.BlockSpec((STEP_ROWS, COLS), lambda i, p: (chunk * steps + i, 0))
+    part = pl.BlockSpec((STEP_ROWS, COLS), lambda i, p: (i, 0))
+    w_specs = [
+        pl.BlockSpec((1, mf, COLS), lambda i, p: (0, 0, p[0])),
+        pl.BlockSpec((1, mf, COLS), lambda i, p: (0, 0, p[0] ^ 1)),
+        pl.BlockSpec((1, mf, COLS), lambda i, p: (0, 0, p[0] ^ 2)),
+        pl.BlockSpec((1, mf, COLS), lambda i, p: (0, 0, p[0] ^ 3)),
+    ]
     return pl.pallas_call(
         hidden_kernel,
         grid_spec=pltpu.PrefetchScalarGridSpec(
             num_scalar_prefetch=1,
-            grid=(blocks,),
-            in_specs=[x_spec, x_spec, in_own, in_peer, in_own, in_peer],
-            out_specs=pl.BlockSpec((rows, padded), lambda i, p: (i, 0)),
-        ),
-        out_shape=jax.ShapeDtypeStruct((SLOTS, padded), BF16),
+            grid=(steps,),
+            in_specs=[whole, whole, part, part] + w_specs + w_specs,
+            out_specs=pl.BlockSpec((STEP_ROWS, padded), lambda i, p: (i, 0)),
+        ),
+        out_shape=jax.ShapeDtypeStruct((CHUNK_ROWS, padded), BF16),
         cost_estimate=pl.CostEstimate(
-            flops=4 * SLOTS * D * mf, bytes_accessed=8_000_000, transcendentals=SLOTS * mf
+            flops=4 * CHUNK_ROWS * D * mf, bytes_accessed=6_000_000, transcendentals=CHUNK_ROWS * mf
         ),
         name="hidden",
-    )(pos, own, peer, w_gate, w_gate, w_up, w_up)
-
-
-def down_kernel(pos_ref, own_ref, peer_ref, a0, a1, b0, b1, out_ref):
+    )(pos, own, core, y, both, *[w_gate] * 4, *[w_up] * 4)
+
+
+def down_kernel(pos_ref, h0, h1, h2, h3, w0, w1, w2, w3, *rest):
     del pos_ref
-    mf = a0.shape[1]
-    own = own_ref[:, :mf]
-    peer = peer_ref[:, :mf]
-    out_ref[:, :512] = (dot(own, a0[0]) + dot(peer, b0[0])).astype(BF16)
-    out_ref[:, 512:] = (dot(own, a1[0]) + dot(peer, b1[0])).astype(BF16)
-
-
-def expert_down_half(pos, own, peer, w_own, w_peer):
-    blocks = 4
-    rows = SLOTS // blocks
+    out_ref = rest[-1]
+    mf = w1.shape[0]
+    total = dot(h0[:, :mf], w0[0])
+    for h, w in ((h1, w1), (h2, w2), (h3, w3)):
+        total = total + dot(h[:, :mf], w[...])
+    out_ref[...] = total.astype(BF16)
+
+
+def expert_columns(pos, chunk, hiddens, w_own, w_others, so_far):
+    steps = CHUNK_ROWS // STEP_ROWS
     mf = w_own.shape[1]
-    h_spec = pl.BlockSpec((rows, own.shape[1]), lambda i, p: (i, 0))
-    low = pl.BlockSpec((1, mf, 512), lambda i, p: (0, 0, p[0]))
-    high = pl.BlockSpec((1, mf, 512), lambda i, p: (0, 0, 2 + p[0]))
+    h_spec = pl.BlockSpec((STEP_ROWS, hiddens[0].shape[1]), lambda i, p: (i, 0))
+    w_spec = pl.BlockSpec((mf, COLS), lambda i, p: (0, 0))
+    more = [] if so_far is None else [so_far]
     return pl.pallas_call(
         down_kernel,
         grid_spec=pltpu.PrefetchScalarGridSpec(
             num_scalar_prefetch=1,
-            grid=(blocks,),
-            in_specs=[h_spec, h_spec, low, high, low, high],
-            out_specs=pl.BlockSpec((rows, D // 2), lambda i, p: (i, 0)),
-        ),
-        out_shape=jax.ShapeDtypeStruct((SLOTS, D // 2), BF16),
+            grid=(steps,),
+            in_specs=[h_spec] * 4
+            + [pl.BlockSpec((1, mf, COLS), lambda i, p: (0, 0, p[0]))]
+            + [w_spec] * 3
+            + [pl.BlockSpec(memory_space=pl.ANY)] * len(more),
+            out_specs=pl.BlockSpec((STEP_ROWS, COLS), lambda i, p: (chunk * steps + i, 0)),
+        ),
+        out_shape=jax.ShapeDtypeStruct((SLOTS, COLS), BF16),
+        input_output_aliases={9: 0} if more else {},
         cost_estimate=pl.CostEstimate(
-            flops=2 * SLOTS * D * mf, bytes_accessed=5_000_000, transcendentals=0
+            flops=8 * CHUNK_ROWS * COLS * mf, bytes_accessed=4_000_000, transcendentals=0
         ),
         name="down",
-    )(pos, own, peer, w_own, w_own, w_peer, w_peer)
+    )(pos, *hiddens, w_own, *w_others, *more)
 
 
 def shared_kernel(pos_ref, t0, t1, t2, t3, w_ref, after_ref, keep_ref, send_ref):
     del after_ref
-    core = pos_ref[0]
+    core = pos_ref[0] & 1
     fs = w_ref.shape[3] // 3
     rows = w_ref.shape[0] * w_ref.shape[2]
     for d, tok_ref in enumerate((t0, t1, t2, t3)):
@@ -219,7 +260,29 @@
     return total
 
 
-def combine_kernel(pos_ref, ids_ref, gw_ref, ret_ref, sh0, sh1, sh2, sh3, keep_ref, send_ref):
+def fold_kernel(pos_ref, s0, s1, s2, s3, keep_ref, send_ref):
+    total = s0[...].astype(F32)
+    for one in (s1, s2, s3):
+        total = total + one[...].astype(F32)
+    low = total[:, :COLS]
+    high = total[:, COLS:]
+    first = pos_ref[0] < 2
+    keep_ref[...] = jnp.where(first, low, high)
+    send_ref[...] = jnp.where(first, high, low).astype(BF16)
+
+
+def fold(pos, parts):
+    vmem = pl.BlockSpec(memory_space=pltpu.VMEM)
+    return pl.pallas_call(
+        fold_kernel,
+        in_specs=[pl.BlockSpec(memory_space=pltpu.SMEM)] + [vmem] * 4,
+        out_specs=[vmem, vmem],
+        out_shape=[jax.ShapeDtypeStruct((TOK, COLS), F32), jax.ShapeDtypeStruct((TOK, COLS), BF16)],
+        name="fold",
+    )(pos, *parts)
+
+
+def combine_kernel(ids_ref, gw_ref, ret_ref, keep_ref, got_ref, out_ref):
     ids = turned(ids_ref[...].astype(F32))
     gates = turned(gw_ref[...])
     named = named_counts(ids, (TOK, EXPERTS), 1)
@@ -235,34 +298,22 @@
     slot = (lax.broadcasted_iota(jnp.int32, (TOK, SLOTS), 1) & 15).astype(F32)
     hit = dot(keys, spread) == slot
     ret = ret_ref[...]
-    total = jnp.zeros((TOK, D // 2), F32)
+    total = keep_ref[...] + got_ref[...].astype(F32)
     rest = weight
     for _ in range(3):
         part = rest.astype(BF16)
         rest = rest - part.astype(F32)
         row = jnp.where(hit, dot(part, spread), 0.0).astype(BF16)
         total = total + dot(row, ret)
-    for shared_ref in (sh0, sh1, sh2, sh3):
-        total = total + shared_ref[...].astype(F32)
-    low = total[:, :512]
-    high = total[:, 512:]
-    first = pos_ref[1] == 0
-    keep_ref[...] = jnp.where(first, low, high)
-    send_ref[...] = jnp.where(first, high, low).astype(BF16)
-
-
-def combine(pos, ids, gate_weights, returned, shared):
-    vmem = pl.BlockSpec(memory_space=pltpu.VMEM)
+    out_ref[...] = total.astype(BF16)
+
+
+def combine(ids, gate_weights, returned, keep, got):
     return pl.pallas_call(
         combine_kernel,
-        in_specs=[pl.BlockSpec(memory_space=pltpu.SMEM)] + [vmem] * 7,
-        out_specs=[vmem, vmem],
-        out_shape=[
-            jax.ShapeDtypeStruct((TOK, 512), F32),
-            jax.ShapeDtypeStruct((TOK, 512), BF16),
-        ],
+        out_shape=jax.ShapeDtypeStruct((TOK, COLS), BF16),
         name="combine",
-    )(pos, ids, gate_weights, returned, *shared)
+    )(ids, gate_weights, returned, keep, got)
 
 
 def body(
@@ -276,30 +327,45 @@
     expert_up,
     expert_down,
 ):
-    narrow = lax.axis_index("narrow")
-    pos = jnp.stack([narrow & 1, narrow >> 1]).astype(jnp.int32)
+    pos = lax.axis_index("narrow").astype(jnp.int32).reshape(1)
     ids_t = expert_ids.T
     gates_t = gate_weights.T
+    gate_t = expert_gate.transpose(0, 2, 1)
+    up_t = expert_up.transpose(0, 2, 1)
 
     packed = pack(shared_gate, shared_up, shared_down.T)
     packed = lax.all_to_all(packed, "wide", 0, 0, axis_index_groups=X_GROUPS, tiled=True)
     weights = lax.all_gather(packed[None], "wide", axis=0, axis_index_groups=YZ_GROUPS, tiled=True)
 
-    outgoing = dispatch(pos, ids_t, tokens).reshape(EXPERTS, CAP, D // 2)
-    received = lax.all_to_all(outgoing, "wide", 0, 0, tiled=True).reshape(SLOTS, D // 2)
+    outgoing = dispatch(pos, ids_t, tokens).reshape(EXPERTS, CAP, COLS)
+    own = lax.all_to_all(outgoing, "wide", 0, 0, tiled=True).reshape(SLOTS, COLS)
     toks = [tokens]
-    peer_down = lax.ppermute(expert_down, "narrow", CORE_SWAP)
+    cuts = cut(pos, expert_down)
+    others = [
+        lax.ppermute(w, "narrow", swap)
+        for w, swap in zip(cuts, (CORE_SWAP, Y_SWAP, BOTH_SWAP))
+    ]
     for d in range(1, NX):
         toks.append(lax.ppermute(tokens, "wide", x_shift(d)))
-    peer = lax.ppermute(received, "narrow", CORE_SWAP)
-    hidden = expert_hidden(
-        pos, received, peer, expert_gate.transpose(0, 2, 1), expert_up.transpose(0, 2, 1)
-    )
-    peer_hidden = lax.ppermute(hidden, "narrow", CORE_SWAP)
-    summed = expert_down_half(pos, hidden, peer_hidden, expert_down, peer_down)
-    returned = lax.all_to_all(summed.reshape(EXPERTS, CAP, D // 2), "wide", 0, 0, tiled=True)
-
-    mine, theirs = shared_ffn(pos, toks, weights, summed)
+
+    ys = []
+    for k in range(CHUNKS):
+        ys.append(lax.ppermute(own[k * CHUNK_ROWS : (k + 1) * CHUNK_ROWS], "narrow", Y_SWAP))
+    core = lax.ppermute(own, "narrow", CORE_SWAP)
+    hiddens = []
+    for k in range(CHUNKS):
+        both = lax.ppermute(ys[k], "narrow", CORE_SWAP)
+        hidden = expert_hidden(pos, k, own, core, ys[k], both, gate_t, up_t)
+        hidden_y = lax.ppermute(hidden, "narrow", Y_SWAP)
+        hidden_core = lax.ppermute(hidden, "narrow", CORE_SWAP)
+        hiddens.append([hidden, hidden_core, hidden_y])
+    mine, theirs = shared_ffn(pos, toks, weights, hiddens[-1][0])
+    outputs = None
+    for k in range(CHUNKS):
+        hidden_both = lax.ppermute(hiddens[k][2], "narrow", CORE_SWAP)
+        outputs = expert_columns(pos, k, hiddens[k] + [hidden_both], expert_down, others, outputs)
+    returned = lax.all_to_all(outputs.reshape(EXPERTS, CAP, COLS), "wide", 0, 0, tiled=True)
+
     theirs = lax.ppermute(theirs, "narrow", CORE_SWAP)
     shared = []
     for d in range(NX):
@@ -307,10 +373,9 @@
         if d > 0:
             one = lax.ppermute(one, "wide", x_shift(NX - d))
         shared.append(one)
-
-    kept, sent = combine(pos, ids_t, gates_t, returned.reshape(SLOTS, D // 2), shared)
+    kept, sent = fold(pos, shared)
     got = lax.ppermute(sent, "narrow", Y_SWAP)
-    return (kept + got.astype(F32)).astype(BF16)
+    return combine(ids_t, gates_t, returned.reshape(SLOTS, COLS), kept, got)
 
 
 def solution(mesh):

time: 238 us -> 216 us (0.908)
  blocking collectives: 74.1 us -> 0 us
  starting transfers between devices: 24.5 us -> 52.6 us
  waiting for transfers between devices: 84.6 us -> 101 us
  Pallas kernels: 33.7 us -> 39.7 us
  local copies, waits for them, and re-layouts: 2.2 us -> 5.18 us
    all_to_all x2 -> x0, blocking collectives: 74.1 us -> none  [the longest x1 64.3 us: body(): lax.all_to_all(outgoing, 'wide', 0, 0, tiled=True).reshape(SLOTS, D // 2)]
    ppermute x3 -> x14, waiting for transfers between devices: 2.59 us -> 49.7 us  [the longest x3 22.3 us: body(): lax.ppermute(w, 'narrow', swap)]
    ppermute x3, waiting for transfers between devices: 39.2 us -> 2.13 us  [body(): toks.append(lax.ppermute(tokens, 'wide', x_shift(d)))]
    all_to_all x1 -> x3, waiting for transfers between devices: 0.01 us -> 26.8 us  [the longest x1 24.7 us: body(): lax.all_to_all(outgoing, 'wide', 0, 0, tiled=True).reshape(SLOTS, COLS)]
    all_gather x1, waiting for transfers between devices: 22.1 us -> 0.01 us  [body(): lax.all_gather(packed[None], 'wide', axis=0, axis_index_groups=YZ_GROUPS,...]
    all_to_all x1 -> x3, starting transfers between devices: 5.42 us -> 26.9 us  [the longest x1 12.4 us: body(): lax.all_to_all(outgoing, 'wide', 0, 0, tiled=True).reshape(SLOTS, COLS)]
    ppermute x3 -> x14, starting transfers between devices: 5.92 us -> 15.3 us  [the longest x1 6.9 us: body(): core = lax.ppermute(own, 'narrow', CORE_SWAP)]
    pallas_call x2 -> x5, Pallas kernels: 11 us -> 15.7 us  [the longest x2 7.81 us: expert_columns(): pl.pallas_call(down_kernel, grid_spec=pltpu.PrefetchScalarGridSpec(num_sc...]
  transfers between devices with their start and end apart: 13 -> 26, of which waited for: 8 -> 13; matrix products, arithmetic and copies ran while one was open for 1% -> 1% of each run, Pallas kernels for 11% -> 16%
where the time goes in v3:
time: 216 us; the launch traced here: 215 us
  waiting for transfers between devices  101 us (47%)
  starting transfers between devices  52.6 us (24%)
  Pallas kernels  39.7 us (18%)
  between operations  13.5 us (6%)
  local copies, waits for them, and re-layouts  5.18 us (2%)
  other arithmetic  2.29 us (1%)
    all_to_all x1, waiting for transfers between devices, body(): lax.all_to_all(outgoing, 'wide', 0, 0, tiled=True).reshape(SLOTS, COLS)  24.7 us
    ppermute x3, waiting for transfers between devices, body(): lax.ppermute(w, 'narrow', swap)  22.3 us
    ppermute x2, waiting for transfers between devices, body(): lax.ppermute(own[k * CHUNK_ROWS:(k + 1) * CHUNK_ROWS], 'narrow', Y_SWAP)  22 us
    ppermute x3, waiting for transfers between devices, body(): one = lax.ppermute(one, 'wide', x_shift(NX - d))  15.2 us
    all_to_all x1, starting transfers between devices, body(): lax.all_to_all(outgoing, 'wide', 0, 0, tiled=True).reshape(SLOTS, COLS)  12.4 us
    pallas_call x2, Pallas kernels, expert_hidden(): pl.pallas_call(hidden_kernel, grid_spec=pltpu.PrefetchScalarGridSpec(num_...  10.9 us
    all_to_all x1, starting transfers between devices, body(): lax.all_to_all(outputs.reshape(EXPERTS, CAP, COLS), 'wide', 0, 0, tiled=T...  9.65 us
    pallas_call x1, Pallas kernels, shared_ffn(): pl.pallas_call(shared_kernel, in_specs=[pl.BlockSpec(memory_space=pltpu.S...  8.55 us
  transfers between devices with their start and end apart: 26, of which 13 were waited for; matrix products, arithmetic and copies ran while one was open for 1% of the time, Pallas kernels for 16%

profile of v3, /device:TPU:1, one launch (start us, length us, event | category | flops | bytes accessed | tf_op | source)
XLA Modules:
  0.0 214.7 jit_solution(7304390589051924866)
XLA Ops:
  8.2 4.8 %all-to-all-start.2 = ((bf16[4,32,528]{2,1,0:T(8,128)(2,1)}), bf16[4,32,528]{2,1,0:T(8,128)(2,1)S(1)}, u32[]{:S(2)}, u32[]{:S(2)}) async-start(bf16[4,32,528]{2,1,0:T(8,128)(2,1)} %pack.1), calls=%async_computation.2 | async-start | bytes 327680 | tf_op jit(solution)/shard_map/all_to_all | solution.py:337
  13.0 2.8 %dispatch.1 = bf16[1024,512]{1,0:T(8,128)(2,1)} custom-call(s32[1]{0:T(128)} %bitcast.2.pos_ref, s32[6,128]{1,0:T(8,128)} %bitcast.46, bf16[128,2048]{1,0:T(8,128)(2,1)} %t0.1), custom_call_target="tpu_custom_call" | custom-call | tf_op jit(solution)/shard_map/dispatch/pallas_call | solution.py:81
  18.0 12.4 %all-to-all-start = ((bf16[64,16,512]{2,1,0:T(8,128)(2,1)}), bf16[64,16,512]{2,1,0:T(8,128)(2,1)S(1)}, u32[]{:S(2)}, u32[]{:S(2)}) async-start(bf16[64,16,512]{2,1,0:T(8,128)(2,1)} %bitcast.42), calls=%async_computation | async-start | bytes 2097152 | tf_op jit(solution)/shard_map/all_to_all | solution.py:341
  31.2 24.7 %all-to-all-done = bf16[64,16,512]{2,1,0:T(8,128)(2,1)S(1)} async-done(((bf16[64,16,512]{2,1,0:T(8,128)(2,1)}), bf16[64,16,512]{2,1,0:T(8,128)(2,1)S(1)}, u32[]{:S(2)}, u32[]{:S(2)}) %all-to-all-start) | async-done | bytes 1048608 | tf_op jit(solution)/shard_map/all_to_all | solution.py:341
  55.8 6.9 %collective-permute-start = (bf16[1024,512]{1,0:T(8,128)(2,1)S(1)}, bf16[1024,512]{1,0:T(8,128)(2,1)S(1)}, u32[]{:S(2)}, u32[]{:S(2)}) collective-permute-start(bf16[1024,512]{1,0:T(8,128)(2,1)S(1)} %bitcast.37), channel_id=1, source_target_pairs={{0,1},{1,0},{2,3},{3,2},{4,5},{5,4},{6,7},{7,6},{8,9},{9,8},{10,11... | collective-permute-start | bytes 3145736 | tf_op jit(solution)/shard_map/ppermute | solution.py:354
  64.4 12.1 %collective-permute-done.9.x2 = bf16[512,512]{1,0:T(8,128)(2,1)S(1)} collective-permute-done((bf16[512,512]{1,0:T(8,128)(2,1)S(1)}, bf16[512,512]{1,0:T(8,128)(2,1)S(1)}, u32[]{:S(2)}, u32[]{:S(2)}) %collective-permute-start.9) | collective-permute-done | bytes 524320 | tf_op jit(solution)/shard_map/ppermute | solution.py:353
  77.7 9.9 %collective-permute-done.1.x2 = bf16[512,512]{1,0:T(8,128)(2,1)S(1)} collective-permute-done((bf16[512,512]{1,0:T(8,128)(2,1)S(1)}, bf16[512,512]{1,0:T(8,128)(2,1)S(1)}, u32[]{:S(2)}, u32[]{:S(2)}) %collective-permute-start.1) | collective-permute-done | bytes 524320 | tf_op jit(solution)/shard_map/ppermute | solution.py:353
  89.6 5.4 %hidden.3.h0 = bf16[512,384]{1,0:T(8,128)(2,1)} custom-call(s32[1]{0:T(128)} %bitcast.2.pos_ref, bf16[1024,512]{1,0:T(8,128)(2,1)} %bitcast.38, bf16[1024,512]{1,0:T(8,128)(2,1)} %copy-done.1, bf16[512,512]{1,0:T(8,128)(2,1)} %copy-done.9, bf16[512,512]{1,0:T(8,128)(2,1)} %copy-done.10, bf16[1,352,2048]{2,1,0:T(8,128)(2,1)} %bitcast.21, ...), custom_call_target="tpu_custom_call" | custom-call | flops 1476395008 | bytes 6000000 | tf_op jit(solution)/shard_map/hidden/pallas_call | solution.py:164
  95.6 2.3 %cut.1 = (bf16[352,512]{1,0:T(8,128)(2,1)}, bf16[352,512]{1,0:T(8,128)(2,1)}, bf16[352,512]{1,0:T(8,128)(2,1)}) custom-call(s32[1]{0:T(128)} %bitcast.2.pos_ref, bf16[1,352,2048]{2,1,0:T(8,128)(2,1)} %w0.3, bf16[1,352,2048]{2,1,0:T(8,128)(2,1)} %w0.3, bf16[1,352,2048]{2,1,0:T(8,128)(2,1)} %w0.3), custom_call_target="tpu_custom_call" | custom-call | tf_op jit(solution)/shard_map/cut/pallas_call | solution.py:122
  98.4 5.5 %hidden.2.h0.after_ref = bf16[512,384]{1,0:T(8,128)(2,1)} custom-call(s32[1]{0:T(128)} %bitcast.2.pos_ref, bf16[1024,512]{1,0:T(8,128)(2,1)} %bitcast.39, bf16[1024,512]{1,0:T(8,128)(2,1)} %copy-done.1, bf16[512,512]{1,0:T(8,128)(2,1)} %copy-done.8, bf16[512,512]{1,0:T(8,128)(2,1)} %collective-permute-done.2.x3, bf16[1,352,2048]{2,1,0:T(8,128)(2,1)} %bitcast.25, ...), custom_call_target="tpu_custom_call" | custom-call | flops 1476395008 | bytes 6000000 | tf_op jit(solution)/shard_map/hidden/pallas_call | solution.py:164
  106.2 5.3 %collective-permute-done.12.h2 = bf16[512,384]{1,0:T(8,128)(2,1)} collective-permute-done((bf16[512,384]{1,0:T(8,128)(2,1)}, bf16[512,384]{1,0:T(8,128)(2,1)}, u32[]{:S(2)}, u32[]{:S(2)}) %collective-permute-start.12) | collective-permute-done | bytes 393248 | tf_op jit(solution)/shard_map/ppermute | solution.py:359
  112.3 15.3 %collective-permute-done.7.w2 = bf16[352,512]{1,0:T(8,128)(2,1)S(1)} collective-permute-done((bf16[352,512]{1,0:T(8,128)(2,1)S(1)}, bf16[352,512]{1,0:T(8,128)(2,1)S(1)}, u32[]{:S(2)}, u32[]{:S(2)}) %collective-permute-start.7) | collective-permute-done | bytes 360480 | tf_op jit(solution)/shard_map/ppermute | solution.py:345
  128.4 7.0 %collective-permute-done.8.w3 = bf16[352,512]{1,0:T(8,128)(2,1)S(1)} collective-permute-done((bf16[352,512]{1,0:T(8,128)(2,1)S(1)}, bf16[352,512]{1,0:T(8,128)(2,1)S(1)}, u32[]{:S(2)}, u32[]{:S(2)}) %collective-permute-start.8) | collective-permute-done | bytes 360480 | tf_op jit(solution)/shard_map/ppermute | solution.py:345
  136.8 2.3 %collective-permute-start.15 = (bf16[128,2048]{1,0:T(8,128)(2,1)S(1)}, bf16[128,2048]{1,0:T(8,128)(2,1)}, u32[]{:S(2)}, u32[]{:S(2)}) collective-permute-start(bf16[128,2048]{1,0:T(8,128)(2,1)S(1)} %copy-done.11), channel_id=1, source_target_pairs={{0,128},{4,132},{8,136},{12,140},{16,144},{20,148},{24,152},{28,15... | collective-permute-start | bytes 1572872 | tf_op jit(solution)/shard_map/ppermute | solution.py:349
  141.1 3.9 %down.2.rest_0_ = bf16[1024,512]{1,0:T(8,128)(2,1)} custom-call(s32[1]{0:T(128)} %bitcast.2.pos_ref, bf16[512,384]{1,0:T(8,128)(2,1)} %hidden.3.h0, bf16[512,384]{1,0:T(8,128)(2,1)} %copy-done.15, bf16[512,384]{1,0:T(8,128)(2,1)} %collective-permute-done.12.h2, bf16[512,384]{1,0:T(8,128)(2,1)} %copy-done.16, bf16[1,352,2048]{2,1,0:T(8,128)(2,1)} %w0.3, ...), custom_call_target="tpu_custom_call" | custom-call | flops 738197504 | bytes 4000000 | tf_op jit(solution)/shard_map/down/pallas_call | solution.py:196
  146.5 3.9 %down.3 = bf16[1024,512]{1,0:T(8,128)(2,1)} custom-call(s32[1]{0:T(128)} %bitcast.2.pos_ref, bf16[512,384]{1,0:T(8,128)(2,1)} %hidden.2.h0.after_ref, bf16[512,384]{1,0:T(8,128)(2,1)} %copy-done.13, bf16[512,384]{1,0:T(8,128)(2,1)} %copy-done.12, bf16[512,384]{1,0:T(8,128)(2,1)} %copy-done.14, ...), custom_call_target="tpu_custom_call", output_to_operand_aliasing={{}: (9, {})} | custom-call | flops 738197504 | bytes 4000000 | tf_op jit(solution)/shard_map/down/pallas_call | solution.py:196
  150.4 9.7 %all-to-all-start.1 = ((bf16[64,16,512]{2,1,0:T(8,128)(2,1)}), bf16[64,16,512]{2,1,0:T(8,128)(2,1)S(1)}, u32[]{:S(2)}, u32[]{:S(2)}) async-start(bf16[64,16,512]{2,1,0:T(8,128)(2,1)} %bitcast.40), calls=%async_computation.1 | async-start | bytes 2097152 | tf_op jit(solution)/shard_map/all_to_all | solution.py:367
  162.2 8.5 %shared.1 = (bf16[4,128,1024]{2,1,0:T(8,128)(2,1)}, bf16[4,128,1024]{2,1,0:T(8,128)(2,1)}) custom-call(s32[1]{0:T(128)} %bitcast.2.pos_ref, bf16[128,2048]{1,0:T(8,128)(2,1)} %t0.1, bf16[128,2048]{1,0:T(8,128)(2,1)} %collective-permute-done.14.t1, bf16[128,2048]{1,0:T(8,128)(2,1)} %collective-permute-done.15.t2, ...), custom_call_target="tpu_custom_call" | custom-call | flops 2214592512 | bytes 6000000 | tf_op jit(solution)/shard_map/shared/pallas_call | solution.py:237
  171.9 2.5 %collective-permute-done.17 = bf16[4,128,1024]{2,1,0:T(8,128)(2,1)S(1)} collective-permute-done((bf16[4,128,1024]{2,1,0:T(8,128)(2,1)}, bf16[4,128,1024]{2,1,0:T(8,128)(2,1)S(1)}, u32[]{:S(2)}, u32[]{:S(2)}) %collective-permute-start.17) | collective-permute-done | bytes 1048608 | tf_op jit(solution)/shard_map/ppermute | solution.py:369
  174.4 2.3 %fusion.3 = (bf16[128,1024]{1,0:T(8,128)(2,1)S(1)}, bf16[128,1024]{1,0:T(8,128)(2,1)S(1)}, bf16[128,1024]{1,0:T(8,128)(2,1)S(1)}, bf16[128,1024]{1,0:T(8,128)(2,1)}) fusion(bf16[4,128,1024]{2,1,0:T(8,128)(2,1)S(1)} %collective-permute-done.17, bf16[4,128,1024]{2,1,0:T(8,128)(2,1)} %get-tuple-element.15), kind=kLoop, calls=%fused_computation.7 | loop fusion | flops 2097152 | bytes 3145728 | tf_op jit(solution)/shard_map/convert_element_type | solution.py:372
  180.5 7.4 %collective-permute-done.18.s1 = bf16[128,1024]{1,0:T(8,128)(2,1)S(1)} collective-permute-done((bf16[128,1024]{1,0:T(8,128)(2,1)S(1)}, bf16[128,1024]{1,0:T(8,128)(2,1)S(1)}, u32[]{:S(2)}, u32[]{:S(2)}) %collective-permute-start.18) | collective-permute-done | bytes 262176 | tf_op jit(solution)/shard_map/ppermute | solution.py:374
  189.5 6.3 %collective-permute-done.20.s3 = bf16[128,1024]{1,0:T(8,128)(2,1)S(1)} collective-permute-done((bf16[128,1024]{1,0:T(8,128)(2,1)S(1)}, bf16[128,1024]{1,0:T(8,128)(2,1)S(1)}, u32[]{:S(2)}, u32[]{:S(2)}) %collective-permute-start.20) | collective-permute-done | bytes 262176 | tf_op jit(solution)/shard_map/ppermute | solution.py:374
  198.8 4.4 %collective-permute-done.21.got_ref = bf16[128,512]{1,0:T(8,128)(2,1)S(1)} collective-permute-done((bf16[128,512]{1,0:T(8,128)(2,1)}, bf16[128,512]{1,0:T(8,128)(2,1)S(1)}, u32[]{:S(2)}, u32[]{:S(2)}) %collective-permute-start.21) | collective-permute-done | bytes 131104 | tf_op jit(solution)/shard_map/ppermute | solution.py:377
  204.3 3.6 %combine.1 = bf16[128,512]{1,0:T(8,128)(2,1)} custom-call(s32[6,128]{1,0:T(8,128)} %bitcast.47, f32[6,128]{1,0:T(8,128)} %bitcast.48, bf16[1024,512]{1,0:T(8,128)(2,1)} %bitcast.41, f32[128,512]{1,0:T(8,128)} %get-tuple-element.17.keep_ref, bf16[128,512]{1,0:T(8,128)(2,1)} %copy-done.20), custom_call_target="tpu_custom_call" | custom-call | tf_op jit(solution)/shard_map/combine/pallas_call | solution.py:312
  (87 shorter events, 31.8 us)
Async XLA Ops:
  8.2 9.8 %all-to-all-start.2 = ((bf16[4,32,528]{2,1,0:T(8,128)(2,1)}), bf16[4,32,528]{2,1,0:T(8,128)(2,1)S(1)}, u32[]{:S(2)}, u32[]{:S(2)}) async-start(bf16[4,32,528]{2,1,0:T(8,128)(2,1)} %pack.1), calls=%async_computation.2 | async-start | bytes 327680 | tf_op jit(solution)/shard_map/all_to_all | solution.py:337
  18.0 37.8 %all-to-all-start = ((bf16[64,16,512]{2,1,0:T(8,128)(2,1)}), bf16[64,16,512]{2,1,0:T(8,128)(2,1)S(1)}, u32[]{:S(2)}, u32[]{:S(2)}) async-start(bf16[64,16,512]{2,1,0:T(8,128)(2,1)} %bitcast.42), calls=%async_computation | async-start | bytes 2097152 | tf_op jit(solution)/shard_map/all_to_all | solution.py:341
  30.4 131.8 %all-gather.3.cloned.1.call-start = ((), (), s32[]{:S(2)}) async-start(), calls=%async_computation.3 | async-start | bytes 2785280 | tf_op jit(solution)/shard_map/all_gather | solution.py:338
  55.8 32.6 %collective-permute-start = (bf16[1024,512]{1,0:T(8,128)(2,1)S(1)}, bf16[1024,512]{1,0:T(8,128)(2,1)S(1)}, u32[]{:S(2)}, u32[]{:S(2)}) collective-permute-start(bf16[1024,512]{1,0:T(8,128)(2,1)S(1)} %bitcast.37), channel_id=1, source_target_pairs={{0,1},{1,0},{2,3},{3,2},{4,5},{5,4},{6,7},{7,6},{8,9},{9,8},{10,11... | collective-permute-start | bytes 3145736 | tf_op jit(solution)/shard_map/ppermute | solution.py:354
  62.8 13.7 %collective-permute-start.9 = (bf16[512,512]{1,0:T(8,128)(2,1)S(1)}, bf16[512,512]{1,0:T(8,128)(2,1)S(1)}, u32[]{:S(2)}, u32[]{:S(2)}) collective-permute-start(bf16[512,512]{1,0:T(8,128)(2,1)S(1)} %bitcast.44), channel_id=1, source_target_pairs={{0,2},{2,0},{1,3},{3,1},{4,6},{6,4},{5,7},{7,5},{8,10},{10,8},{9,1... | collective-permute-start | bytes 1572872 | tf_op jit(solution)/shard_map/ppermute | solution.py:353
  63.4 24.2 %collective-permute-start.1 = (bf16[512,512]{1,0:T(8,128)(2,1)S(1)}, bf16[512,512]{1,0:T(8,128)(2,1)S(1)}, u32[]{:S(2)}, u32[]{:S(2)}) collective-permute-start(bf16[512,512]{1,0:T(8,128)(2,1)S(1)} %bitcast.43), channel_id=1, source_target_pairs={{0,2},{2,0},{1,3},{3,1},{4,6},{6,4},{5,7},{7,5},{8,10},{10,8},{9,1... | collective-permute-start | bytes 1572872 | tf_op jit(solution)/shard_map/ppermute | solution.py:353
  76.5 12.0 %collective-permute-start.10 = (bf16[512,512]{1,0:T(8,128)(2,1)S(1)}, bf16[512,512]{1,0:T(8,128)(2,1)S(1)}, u32[]{:S(2)}, u32[]{:S(2)}) collective-permute-start(bf16[512,512]{1,0:T(8,128)(2,1)S(1)} %collective-permute-done.9.x2), channel_id=1, source_target_pairs={{0,1},{1,0},{2,3},{3,2},{4,5},{5,4},{6,7},{7,6},{8,9},{9,8},{10,11... | collective-permute-start | bytes 1572872 | tf_op jit(solution)/shard_map/ppermute | solution.py:357
  87.6 10.7 %collective-permute-start.2 = (bf16[512,512]{1,0:T(8,128)(2,1)S(1)}, bf16[512,512]{1,0:T(8,128)(2,1)}, u32[]{:S(2)}, u32[]{:S(2)}) collective-permute-start(bf16[512,512]{1,0:T(8,128)(2,1)S(1)} %collective-permute-done.1.x2), channel_id=1, source_target_pairs={{0,1},{1,0},{2,3},{3,2},{4,5},{5,4},{6,7},{7,6},{8,9},{9,8},{10,11... | collective-permute-start | bytes 1572872 | tf_op jit(solution)/shard_map/ppermute | solution.py:357
  95.1 16.5 %collective-permute-start.12 = (bf16[512,384]{1,0:T(8,128)(2,1)}, bf16[512,384]{1,0:T(8,128)(2,1)}, u32[]{:S(2)}, u32[]{:S(2)}) collective-permute-start(bf16[512,384]{1,0:T(8,128)(2,1)} %hidden.3.h0), channel_id=1, source_target_pairs={{0,2},{2,0},{1,3},{3,1},{4,6},{6,4},{5,7},{7,5},{8,10},{10,8},{9,1... | collective-permute-start | bytes 1179656 | tf_op jit(solution)/shard_map/ppermute | solution.py:359
  98.0 14.3 %collective-permute-start.6 = (bf16[352,512]{1,0:T(8,128)(2,1)}, bf16[352,512]{1,0:T(8,128)(2,1)S(1)}, u32[]{:S(2)}, u32[]{:S(2)}) collective-permute-start(bf16[352,512]{1,0:T(8,128)(2,1)} %get-tuple-element.12), channel_id=1, source_target_pairs={{0,1},{1,0},{2,3},{3,2},{4,5},{5,4},{6,7},{7,6},{8,9},{9,8},{10,11... | collective-permute-start | bytes 1081352 | tf_op jit(solution)/shard_map/ppermute | solution.py:345
  103.9 24.4 %collective-permute-start.4 = (bf16[512,384]{1,0:T(8,128)(2,1)}, bf16[512,384]{1,0:T(8,128)(2,1)S(1)}, u32[]{:S(2)}, u32[]{:S(2)}) collective-permute-start(bf16[512,384]{1,0:T(8,128)(2,1)} %hidden.2.h0.after_ref), channel_id=1, source_target_pairs={{0,2},{2,0},{1,3},{3,1},{4,6},{6,4},{5,7},{7,5},{8,10},{10,8},{9,1... | collective-permute-start | bytes 1179656 | tf_op jit(solution)/shard_map/ppermute | solution.py:359
  104.9 22.8 %collective-permute-start.7 = (bf16[352,512]{1,0:T(8,128)(2,1)S(1)}, bf16[352,512]{1,0:T(8,128)(2,1)S(1)}, u32[]{:S(2)}, u32[]{:S(2)}) collective-permute-start(bf16[352,512]{1,0:T(8,128)(2,1)S(1)} %copy-done.22), channel_id=1, source_target_pairs={{0,2},{2,0},{1,3},{3,1},{4,6},{6,4},{5,7},{7,5},{8,10},{10,8},{9,1... | collective-permute-start | bytes 1081352 | tf_op jit(solution)/shard_map/ppermute | solution.py:345
  105.4 31.4 %collective-permute-start.11 = (bf16[512,384]{1,0:T(8,128)(2,1)S(1)}, bf16[512,384]{1,0:T(8,128)(2,1)S(1)}, u32[]{:S(2)}, u32[]{:S(2)}) collective-permute-start(bf16[512,384]{1,0:T(8,128)(2,1)S(1)} %copy-done.3), channel_id=1, source_target_pairs={{0,1},{1,0},{2,3},{3,2},{4,5},{5,4},{6,7},{7,6},{8,9},{9,8},{10,11... | collective-permute-start | bytes 1179656 | tf_op jit(solution)/shard_map/ppermute | solution.py:360
  111.6 27.5 %collective-permute-start.13 = (bf16[512,384]{1,0:T(8,128)(2,1)}, bf16[512,384]{1,0:T(8,128)(2,1)S(1)}, u32[]{:S(2)}, u32[]{:S(2)}) collective-permute-start(bf16[512,384]{1,0:T(8,128)(2,1)} %collective-permute-done.12.h2), channel_id=1, source_target_pairs={{0,1},{1,0},{2,3},{3,2},{4,5},{5,4},{6,7},{7,6},{8,9},{9,8},{10,11... | collective-permute-start | bytes 1179656 | tf_op jit(solution)/shard_map/ppermute | solution.py:365
  112.2 23.1 %collective-permute-start.8 = (bf16[352,512]{1,0:T(8,128)(2,1)S(1)}, bf16[352,512]{1,0:T(8,128)(2,1)S(1)}, u32[]{:S(2)}, u32[]{:S(2)}) collective-permute-start(bf16[352,512]{1,0:T(8,128)(2,1)S(1)} %copy-done.21), channel_id=1, source_target_pairs={{0,3},{3,0},{1,2},{2,1},{4,7},{7,4},{5,6},{6,5},{8,11},{11,8},{9,1... | collective-permute-start | bytes 1081352 | tf_op jit(solution)/shard_map/ppermute | solution.py:345
  127.6 17.4 %collective-permute-start.3 = (bf16[512,384]{1,0:T(8,128)(2,1)}, bf16[512,384]{1,0:T(8,128)(2,1)S(1)}, u32[]{:S(2)}, u32[]{:S(2)}) collective-permute-start(bf16[512,384]{1,0:T(8,128)(2,1)} %hidden.2.h0.after_ref), channel_id=1, source_target_pairs={{0,1},{1,0},{2,3},{3,2},{4,5},{5,4},{6,7},{7,6},{8,9},{9,8},{10,11... | collective-permute-start | bytes 1179656 | tf_op jit(solution)/shard_map/ppermute | solution.py:360
  128.3 16.8 %collective-permute-start.5 = (bf16[512,384]{1,0:T(8,128)(2,1)S(1)}, bf16[512,384]{1,0:T(8,128)(2,1)S(1)}, u32[]{:S(2)}, u32[]{:S(2)}) collective-permute-start(bf16[512,384]{1,0:T(8,128)(2,1)S(1)} %collective-permute-done.4.h2), channel_id=1, source_target_pairs={{0,1},{1,0},{2,3},{3,2},{4,5},{5,4},{6,7},{7,6},{8,9},{9,8},{10,11... | collective-permute-start | bytes 1179656 | tf_op jit(solution)/shard_map/ppermute | solution.py:365
  135.3 24.7 %collective-permute-start.14 = (bf16[128,2048]{1,0:T(8,128)(2,1)S(1)}, bf16[128,2048]{1,0:T(8,128)(2,1)}, u32[]{:S(2)}, u32[]{:S(2)}) collective-permute-start(bf16[128,2048]{1,0:T(8,128)(2,1)S(1)} %copy-done.11), channel_id=1, source_target_pairs={{0,64},{4,68},{8,72},{12,76},{16,80},{20,84},{24,88},{28,92},{32,9... | collective-permute-start | bytes 1572872 | tf_op jit(solution)/shard_map/ppermute | solution.py:349
  136.8 25.4 %collective-permute-start.15 = (bf16[128,2048]{1,0:T(8,128)(2,1)S(1)}, bf16[128,2048]{1,0:T(8,128)(2,1)}, u32[]{:S(2)}, u32[]{:S(2)}) collective-permute-start(bf16[128,2048]{1,0:T(8,128)(2,1)S(1)} %copy-done.11), channel_id=1, source_target_pairs={{0,128},{4,132},{8,136},{12,140},{16,144},{20,148},{24,152},{28,15... | collective-permute-start | bytes 1572872 | tf_op jit(solution)/shard_map/ppermute | solution.py:349
  139.8 22.4 %collective-permute-start.16 = (bf16[128,2048]{1,0:T(8,128)(2,1)S(1)}, bf16[128,2048]{1,0:T(8,128)(2,1)}, u32[]{:S(2)}, u32[]{:S(2)}) collective-permute-start(bf16[128,2048]{1,0:T(8,128)(2,1)S(1)} %copy-done.11), channel_id=1, source_target_pairs={{0,192},{4,196},{8,200},{12,204},{16,208},{20,212},{24,216},{28,22... | collective-permute-start | bytes 1572872 | tf_op jit(solution)/shard_map/ppermute | solution.py:349
  150.4 52.8 %all-to-all-start.1 = ((bf16[64,16,512]{2,1,0:T(8,128)(2,1)}), bf16[64,16,512]{2,1,0:T(8,128)(2,1)S(1)}, u32[]{:S(2)}, u32[]{:S(2)}) async-start(bf16[64,16,512]{2,1,0:T(8,128)(2,1)} %bitcast.40), calls=%async_computation.1 | async-start | bytes 2097152 | tf_op jit(solution)/shard_map/all_to_all | solution.py:367
  176.7 11.3 %collective-permute-start.18 = (bf16[128,1024]{1,0:T(8,128)(2,1)S(1)}, bf16[128,1024]{1,0:T(8,128)(2,1)S(1)}, u32[]{:S(2)}, u32[]{:S(2)}) collective-permute-start(bf16[128,1024]{1,0:T(8,128)(2,1)S(1)} %get-tuple-element.21), channel_id=1, source_target_pairs={{0,192},{4,196},{8,200},{12,204},{16,208},{20,212},{24,216},{28,22... | collective-permute-start | bytes 786440 | tf_op jit(solution)/shard_map/ppermute | solution.py:374
  178.6 10.8 %collective-permute-start.19 = (bf16[128,1024]{1,0:T(8,128)(2,1)S(1)}, bf16[128,1024]{1,0:T(8,128)(2,1)S(1)}, u32[]{:S(2)}, u32[]{:S(2)}) collective-permute-start(bf16[128,1024]{1,0:T(8,128)(2,1)S(1)} %get-tuple-element.20), channel_id=1, source_target_pairs={{0,128},{4,132},{8,136},{12,140},{16,144},{20,148},{24,152},{28,15... | collective-permute-start | bytes 786440 | tf_op jit(solution)/shard_map/ppermute | solution.py:374
  180.5 15.2 %collective-permute-start.20 = (bf16[128,1024]{1,0:T(8,128)(2,1)S(1)}, bf16[128,1024]{1,0:T(8,128)(2,1)S(1)}, u32[]{:S(2)}, u32[]{:S(2)}) collective-permute-start(bf16[128,1024]{1,0:T(8,128)(2,1)S(1)} %get-tuple-element.19), channel_id=1, source_target_pairs={{0,64},{4,68},{8,72},{12,76},{16,80},{20,84},{24,88},{28,92},{32,9... | collective-permute-start | bytes 786440 | tf_op jit(solution)/shard_map/ppermute | solution.py:374
  (25 other events, 228.6 us)
Sparse Core Ops, SparseCore 0:
  33.8 96.2 all-gather.2

commit v4 on v3

--- a/solution.py
+++ b/solution.py
@@ -14,9 +14,8 @@
 TOK = 128
 D = 2048
 NX = 4
-NYZ = 16
-X_GROUPS = [[x * NYZ + i for x in range(NX)] for i in range(NYZ)]
-YZ_GROUPS = [[x * NYZ + i for i in range(NYZ)] for x in range(NX)]
+NY = 2
+NZ = 8
 CORE_SWAP = [(0, 1), (1, 0), (2, 3), (3, 2)]
 Y_SWAP = [(0, 2), (2, 0), (1, 3), (3, 1)]
 BOTH_SWAP = [(0, 3), (3, 0), (1, 2), (2, 1)]
@@ -27,8 +26,16 @@
 NO_SLOT = 100.0
 
 
-def x_shift(d):
-    return [(x * NYZ + i, (x + d) % NX * NYZ + i) for x in range(NX) for i in range(NYZ)]
+def moved(dx, flip, dz):
+    def index(x, y, z):
+        return (x % NX * NY + y) * NZ + z % NZ
+
+    return [
+        (index(x, y, z), index(x + dx, y ^ flip, z + dz))
+        for x in range(NX)
+        for y in range(NY)
+        for z in range(NZ)
+    ]
 
 
 def silu(v):
@@ -94,20 +101,24 @@
     )(pos, ids_t, tokens)
 
 
-def pack_kernel(gate_ref, up_ref, down_ref, out_ref):
+def pack_kernel(place_ref, gate_ref, up_ref, down_ref, out_ref):
     fs = out_ref.shape[2] // 3
     for x in range(NX):
         cut = slice(x * fs, (x + 1) * fs)
-        out_ref[x] = jnp.concatenate([gate_ref[:, cut], up_ref[:, cut], down_ref[:, cut]], axis=1)
-
-
-def pack(gate, up, down_t):
+        one = jnp.concatenate([gate_ref[:, cut], up_ref[:, cut], down_ref[:, cut]], axis=1)
+        out_ref[pl.ds((x - place_ref[1]) & (NX - 1), 1)] = one[None]
+
+
+def pack(place, gate, up, down_t):
     fs = gate.shape[1] // NX
+    vmem = pl.BlockSpec(memory_space=pltpu.VMEM)
     return pl.pallas_call(
         pack_kernel,
+        in_specs=[pl.BlockSpec(memory_space=pltpu.SMEM)] + [vmem] * 3,
+        out_specs=vmem,
         out_shape=jax.ShapeDtypeStruct((NX, gate.shape[0], 3 * fs), BF16),
         name="pack",
-    )(gate, up, down_t)
+    )(place, gate, up, down_t)
 
 
 def cut_kernel(pos_ref, a, b, c, out_a, out_b, out_c):
@@ -213,37 +224,68 @@
     )(pos, *hiddens, w_own, *w_others, *more)
 
 
-def shared_kernel(pos_ref, t0, t1, t2, t3, w_ref, after_ref, keep_ref, send_ref):
-    del after_ref
-    core = pos_ref[0] & 1
-    fs = w_ref.shape[3] // 3
-    rows = w_ref.shape[0] * w_ref.shape[2]
-    for d, tok_ref in enumerate((t0, t1, t2, t3)):
-        total = jnp.zeros((TOK, 3 * fs), F32)
-        for x in range(NX):
-            w = w_ref[:, x].reshape(rows, 3 * fs)
-            total = total + dot(tok_ref[:, x * rows : (x + 1) * rows], w)
-        hidden = silu(total[:, :fs]) * total[:, fs : 2 * fs]
-        hidden = jnp.concatenate([jnp.zeros((TOK, 2 * fs), F32), hidden], axis=1).astype(BF16)
-        for half in range(2):
+def shared_kernel(place_ref, t0, t1, t2, t3, *refs):
+    blocks, (keep_ref, send_ref, w_ref, sems) = refs[:9], refs[10:]
+    core, x, y, z = place_ref[0] & 1, place_ref[1], place_ref[2], place_ref[3]
+    copies = []
+    for j, (block, step) in enumerate(zip(blocks, (0, 1, 2, 3, 4, 4, 5, 6, 7))):
+        to = w_ref.at[(z - step) & (NZ - 1)]
+        if block.shape[0] < w_ref.shape[1]:
+            first = 0 if j == 4 else block.shape[0]
+            to = to.at[pl.ds(first, block.shape[0])]
+        copies.append(pltpu.make_async_copy(block, to, sems.at[j]))
+    for copy in copies:
+        copy.start()
+    for copy in copies:
+        copy.wait()
+    fs3 = w_ref.shape[3]
+    fs = fs3 // 3
+    rows = NZ * w_ref.shape[2]
+
+    def columns(quarter, half):
+        at = ((x - quarter) & (NX - 1)) * NY + (half ^ y)
+        return w_ref[:, pl.ds(at, 1)].reshape(rows, fs3)
+
+    toks = (t0, t1, t2, t3)
+    totals = [jnp.zeros((TOK, fs3), F32) for _ in toks]
+    for quarter in range(NX):
+        for half in range(NY):
+            w = columns(quarter, half)
+            first = (quarter * NY + half) * rows
+            for d, tok_ref in enumerate(toks):
+                totals[d] = totals[d] + dot(tok_ref[:, first : first + rows], w)
+    hidden = []
+    for total in totals:
+        one = silu(total[:, :fs]) * total[:, fs : 2 * fs]
+        hidden.append(jnp.concatenate([jnp.zeros((TOK, 2 * fs), F32), one], axis=1).astype(BF16))
+    for side in range(2):
+        for half in range(NY):
+            cut = slice((side * NY + half) * rows, (side * NY + half + 1) * rows)
             for out_ref, at in ((keep_ref, core), (send_ref, 1 - core)):
-                w = w_ref[:, pl.ds(2 * half + at, 1)].reshape(rows, 3 * fs)
-                out_ref[d, :, half * 512 : (half + 1) * 512] = dot_nt(hidden, w).astype(BF16)
-
-
-def shared_ffn(pos, toks, weights, after):
-    fs3 = weights.shape[3]
+                w = columns(2 * side + at, half)
+                for d in range(NX):
+                    out_ref[d, :, cut] = dot_nt(hidden[d], w).astype(BF16)
+
+
+def shared_ffn(place, toks, blocks, after):
+    fs3 = blocks[0].shape[2]
     vmem = pl.BlockSpec(memory_space=pltpu.VMEM)
     return pl.pallas_call(
         shared_kernel,
-        in_specs=[pl.BlockSpec(memory_space=pltpu.SMEM)] + [vmem] * 5 + [pl.BlockSpec(memory_space=pl.ANY)],
+        in_specs=[pl.BlockSpec(memory_space=pltpu.SMEM)]
+        + [vmem] * 4
+        + [pl.BlockSpec(memory_space=pl.ANY)] * 10,
         out_specs=[vmem, vmem],
         out_shape=[jax.ShapeDtypeStruct((NX, TOK, D // 2), BF16)] * 2,
+        scratch_shapes=[
+            pltpu.VMEM((NZ,) + blocks[0].shape, BF16),
+            pltpu.SemaphoreType.DMA((9,)),
+        ],
         cost_estimate=pl.CostEstimate(
             flops=2 * NX * TOK * D * fs3 * 2, bytes_accessed=6_000_000, transcendentals=NX * TOK * fs3 // 3
         ),
         name="shared",
-    )(pos, *toks, weights, after)
+    )(place, *toks, *blocks, after)
 
 
 def turned(values):
@@ -333,20 +375,35 @@
     gate_t = expert_gate.transpose(0, 2, 1)
     up_t = expert_up.transpose(0, 2, 1)
 
-    packed = pack(shared_gate, shared_up, shared_down.T)
-    packed = lax.all_to_all(packed, "wide", 0, 0, axis_index_groups=X_GROUPS, tiled=True)
-    weights = lax.all_gather(packed[None], "wide", axis=0, axis_index_groups=YZ_GROUPS, tiled=True)
+    wide = lax.axis_index("wide").astype(jnp.int32)
+    place = jnp.stack([pos[0], wide >> 4, (wide >> 3) & 1, wide & 7])
 
     outgoing = dispatch(pos, ids_t, tokens).reshape(EXPERTS, CAP, COLS)
     own = lax.all_to_all(outgoing, "wide", 0, 0, tiled=True).reshape(SLOTS, COLS)
+
+    pieces = pack(place, shared_gate, shared_up, shared_down.T)
+    column = []
+    for d in range(NX):
+        for flip in range(NY):
+            one = pieces[d]
+            if d or flip:
+                one = lax.ppermute(one, "wide", moved(d, flip, 0))
+            column.append(one)
+    column = jnp.stack(column)
+    cuts = cut(pos, expert_down)
     toks = [tokens]
-    cuts = cut(pos, expert_down)
     others = [
         lax.ppermute(w, "narrow", swap)
         for w, swap in zip(cuts, (CORE_SWAP, Y_SWAP, BOTH_SWAP))
     ]
     for d in range(1, NX):
-        toks.append(lax.ppermute(tokens, "wide", x_shift(d)))
+        toks.append(lax.ppermute(tokens, "wide", moved(d, 0, 0)))
+    near = {k: lax.ppermute(column, "wide", moved(0, 0, k)) for k in (2, -2, 1, -1)}
+    third = lax.ppermute(near[2], "wide", moved(0, 0, 1))
+    fifth = lax.ppermute(near[-2], "wide", moved(0, 0, -1))
+    fourth_a = lax.ppermute(near[2][:4], "wide", moved(0, 0, 2))
+    fourth_b = lax.ppermute(near[-2][4:], "wide", moved(0, 0, -2))
+    blocks = [column, near[1], near[2], third, fourth_a, fourth_b, fifth, near[-2], near[-1]]
 
     ys = []
     for k in range(CHUNKS):
@@ -359,7 +416,7 @@
         hidden_y = lax.ppermute(hidden, "narrow", Y_SWAP)
         hidden_core = lax.ppermute(hidden, "narrow", CORE_SWAP)
         hiddens.append([hidden, hidden_core, hidden_y])
-    mine, theirs = shared_ffn(pos, toks, weights, hiddens[-1][0])
+    mine, theirs = shared_ffn(place, toks, blocks, hiddens[-1][0])
     outputs = None
     for k in range(CHUNKS):
         hidden_both = lax.ppermute(hiddens[k][2], "narrow", CORE_SWAP)
@@ -371,7 +428,7 @@
     for d in range(NX):
         one = (mine[d].astype(F32) + theirs[d].astype(F32)).astype(BF16)
         if d > 0:
-            one = lax.ppermute(one, "wide", x_shift(NX - d))
+            one = lax.ppermute(one, "wide", moved(-d, 0, 0))
         shared.append(one)
     kept, sent = fold(pos, shared)
     got = lax.ppermute(sent, "narrow", Y_SWAP)

time: 216 us -> 221 us (1.023)
  starting transfers between devices: 52.6 us -> 97 us
  waiting for transfers between devices: 101 us -> 70.1 us
  between operations: 13.5 us -> 0.25 us
  local copies, waits for them, and re-layouts: 5.18 us -> 9.84 us
    ppermute x6 -> x21, starting transfers between devices: 8.89 us -> 38.7 us  [the longest x7 13.1 us: body(): one = lax.ppermute(one, 'wide', moved(d, flip, 0))]
    ppermute x6 -> x21, waiting for transfers between devices: 17.3 us -> 42.3 us  [the longest x4 20.6 us: body(): lax.ppermute(column, 'wide', moved(0, 0, k))]
    ppermute x3, waiting for transfers between devices: 22.3 us -> 0.01 us  [body(): lax.ppermute(w, 'narrow', swap)]
    ppermute x2, waiting for transfers between devices: 22 us -> 1.22 us  [body(): lax.ppermute(own[k * CHUNK_ROWS:(k + 1) * CHUNK_ROWS], 'narrow', Y_SWAP)]
    ppermute x2, starting transfers between devices: 2.08 us -> 15.6 us  [body(): both = lax.ppermute(ys[k], 'narrow', CORE_SWAP)]
    all_to_all x1, waiting for transfers between devices: 24.7 us -> 12.3 us  [body(): lax.all_to_all(outgoing, 'wide', 0, 0, tiled=True).reshape(SLOTS, COLS)]
    all_to_all x1 -> x0, starting transfers between devices: 4.83 us -> none  [body(): lax.all_to_all(packed, 'wide', 0, 0, axis_index_groups=X_GROUPS, tiled=True)]
    ppermute x3, starting transfers between devices: 0.99 us -> 5.17 us  [body(): lax.ppermute(w, 'narrow', swap)]
  transfers between devices with their start and end apart: 26 -> 39, of which waited for: 13 -> 15; matrix products, arithmetic and copies ran while one was open for 1% -> 3% of each run, Pallas kernels for 16% -> 15%
where the time goes in v4:
time: 221 us; the launch traced here: 219 us
  starting transfers between devices  97 us (44%)
  waiting for transfers between devices  70.1 us (32%)
  Pallas kernels  38.9 us (18%)
  local copies, waits for them, and re-layouts  9.84 us (4%)
  other arithmetic  2.87 us (1%)
    ppermute x4, waiting for transfers between devices, body(): lax.ppermute(column, 'wide', moved(0, 0, k))  20.6 us
    ppermute x2, starting transfers between devices, body(): both = lax.ppermute(ys[k], 'narrow', CORE_SWAP)  15.6 us
    all_to_all x1, starting transfers between devices, body(): lax.all_to_all(outgoing, 'wide', 0, 0, tiled=True).reshape(SLOTS, COLS)  15.1 us
    ppermute x3, waiting for transfers between devices, body(): one = lax.ppermute(one, 'wide', moved(-d, 0, 0))  13.8 us
    ppermute x7, starting transfers between devices, body(): one = lax.ppermute(one, 'wide', moved(d, flip, 0))  13.1 us
    all_to_all x1, waiting for transfers between devices, body(): lax.all_to_all(outgoing, 'wide', 0, 0, tiled=True).reshape(SLOTS, COLS)  12.3 us
    pallas_call x2, Pallas kernels, expert_hidden(): pl.pallas_call(hidden_kernel, grid_spec=pltpu.PrefetchScalarGridSpec(num_...  10.9 us
    ppermute x2, waiting for transfers between devices, body(): hidden_y = lax.ppermute(hidden, 'narrow', Y_SWAP)  8.28 us
  transfers between devices with their start and end apart: 39, of which 15 were waited for; matrix products, arithmetic and copies ran while one was open for 3% of the time, Pallas kernels for 15%

profile of v4, /device:TPU:1, one launch (start us, length us, event | category | flops | bytes accessed | tf_op | source)
XLA Modules:
  0.0 219.0 jit_solution(10733402286942445253)
XLA Ops:
  0.0 2.8 %dispatch.1 = bf16[1024,512]{1,0:T(8,128)(2,1)} custom-call(s32[1]{0:T(128)} %bitcast.2.pos_ref, s32[6,128]{1,0:T(8,128)} %bitcast.70, bf16[128,2048]{1,0:T(8,128)(2,1)} %t0.1), custom_call_target="tpu_custom_call" | custom-call | tf_op jit(solution)/shard_map/dispatch/pallas_call | solution.py:88
  2.8 15.1 %all-to-all-start = ((bf16[64,16,512]{2,1,0:T(8,128)(2,1)}), bf16[64,16,512]{2,1,0:T(8,128)(2,1)S(1)}, u32[]{:S(2)}, u32[]{:S(2)}) async-start(bf16[64,16,512]{2,1,0:T(8,128)(2,1)} %bitcast.66), calls=%async_computation | async-start | bytes 2097152 | tf_op jit(solution)/shard_map/all_to_all | solution.py:382
  27.7 3.9 %collective-permute-start.21 = (bf16[32,528]{1,0:T(8,128)(2,1)S(1)}, bf16[32,528]{1,0:T(8,128)(2,1)S(1)}, u32[]{:S(2)}, u32[]{:S(2)}) collective-permute-start(bf16[32,528]{1,0:T(8,128)(2,1)S(1)} %get-tuple-element.27), channel_id=1, source_target_pairs={{0,160},{4,164},{8,168},{12,172},{16,176},{20,180},{24,184},{28,18... | collective-permute-start | bytes 101384 | tf_op jit(solution)/shard_map/ppermute | solution.py:390
  33.0 12.3 %all-to-all-done = bf16[64,16,512]{2,1,0:T(8,128)(2,1)S(1)} async-done(((bf16[64,16,512]{2,1,0:T(8,128)(2,1)}), bf16[64,16,512]{2,1,0:T(8,128)(2,1)S(1)}, u32[]{:S(2)}, u32[]{:S(2)}) %all-to-all-start) | async-done | bytes 1048608 | tf_op jit(solution)/shard_map/all_to_all | solution.py:382
  46.5 4.5 %collective-permute-start = (bf16[1024,512]{1,0:T(8,128)(2,1)S(1)}, bf16[1024,512]{1,0:T(8,128)(2,1)S(1)}, u32[]{:S(2)}, u32[]{:S(2)}) collective-permute-start(bf16[1024,512]{1,0:T(8,128)(2,1)S(1)} %bitcast.61), channel_id=1, source_target_pairs={{0,1},{1,0},{2,3},{3,2},{4,5},{5,4},{6,7},{7,6},{8,9},{9,8},{10,11... | collective-permute-start | bytes 3145736 | tf_op jit(solution)/shard_map/ppermute | solution.py:411
  54.7 10.5 %collective-permute-start.2 = (bf16[512,512]{1,0:T(8,128)(2,1)S(1)}, bf16[512,512]{1,0:T(8,128)(2,1)}, u32[]{:S(2)}, u32[]{:S(2)}) collective-permute-start(bf16[512,512]{1,0:T(8,128)(2,1)S(1)} %collective-permute-done.1.x2), channel_id=1, source_target_pairs={{0,1},{1,0},{2,3},{3,2},{4,5},{5,4},{6,7},{7,6},{8,9},{9,8},{10,11... | collective-permute-start | bytes 1572872 | tf_op jit(solution)/shard_map/ppermute | solution.py:414
  66.9 5.0 %collective-permute-start.10 = (bf16[512,512]{1,0:T(8,128)(2,1)}, bf16[512,512]{1,0:T(8,128)(2,1)}, u32[]{:S(2)}, u32[]{:S(2)}) collective-permute-start(bf16[512,512]{1,0:T(8,128)(2,1)} %collective-permute-done.9.x2), channel_id=1, source_target_pairs={{0,1},{1,0},{2,3},{3,2},{4,5},{5,4},{6,7},{7,6},{8,9},{9,8},{10,11... | collective-permute-start | bytes 1572872 | tf_op jit(solution)/shard_map/ppermute | solution.py:414
  72.6 3.3 %collective-permute-start.24 = (bf16[8,32,528]{2,1,0:T(8,128)(2,1)}, bf16[8,32,528]{2,1,0:T(8,128)(2,1)S(1)}, u32[]{:S(2)}, u32[]{:S(2)}) collective-permute-start(bf16[8,32,528]{2,1,0:T(8,128)(2,1)} %bitcast_dynamic-update-slice_fusion.refs_0_), channel_id=1, source_target_pairs={{0,4},{4,8},{8,12},{12,16},{16,20},{20,24},{24,28},{28,0},{32,36},... | collective-permute-start | bytes 811016 | tf_op jit(solution)/shard_map/ppermute | solution.py:401
  79.5 3.9 %collective-permute-done.24.refs_1_ = bf16[8,32,528]{2,1,0:T(8,128)(2,1)S(1)} collective-permute-done((bf16[8,32,528]{2,1,0:T(8,128)(2,1)}, bf16[8,32,528]{2,1,0:T(8,128)(2,1)S(1)}, u32[]{:S(2)}, u32[]{:S(2)}) %collective-permute-start.24) | collective-permute-done | bytes 270368 | tf_op jit(solution)/shard_map/ppermute | solution.py:401
  86.3 10.9 %collective-permute-done.25.refs_2_ = bf16[8,32,528]{2,1,0:T(8,128)(2,1)S(1)} collective-permute-done((bf16[8,32,528]{2,1,0:T(8,128)(2,1)}, bf16[8,32,528]{2,1,0:T(8,128)(2,1)S(1)}, u32[]{:S(2)}, u32[]{:S(2)}) %collective-permute-start.25) | collective-permute-done | bytes 270368 | tf_op jit(solution)/shard_map/ppermute | solution.py:401
  101.3 5.5 %hidden.2.h0.refs_9_ = bf16[512,384]{1,0:T(8,128)(2,1)} custom-call(s32[1]{0:T(128)} %bitcast.2.pos_ref, bf16[1024,512]{1,0:T(8,128)(2,1)} %bitcast.62, bf16[1024,512]{1,0:T(8,128)(2,1)} %copy-done.1, bf16[512,512]{1,0:T(8,128)(2,1)} %copy-done.7, bf16[512,512]{1,0:T(8,128)(2,1)} %collective-permute-done.2.x3, bf16[1,352,2048]{2,1,0:T(8,128)(2,1)} %bitcast.45, ...), custom_call_target="tpu_custom_call" | custom-call | flops 1476395008 | bytes 6000000 | tf_op jit(solution)/shard_map/hidden/pallas_call | solution.py:175
  109.4 5.4 %hidden.3.h0 = bf16[512,384]{1,0:T(8,128)(2,1)} custom-call(s32[1]{0:T(128)} %bitcast.2.pos_ref, bf16[1024,512]{1,0:T(8,128)(2,1)} %bitcast.63, bf16[1024,512]{1,0:T(8,128)(2,1)} %copy-done.1, bf16[512,512]{1,0:T(8,128)(2,1)} %collective-permute-done.9.x2, bf16[512,512]{1,0:T(8,128)(2,1)} %collective-permute-done.10.x3, bf16[1,352,2048]{2,1,0:T(8,128)(2,1)} %bitcast.49, ...), custom_call_target="tpu_custom_call" | custom-call | flops 1476395008 | bytes 6000000 | tf_op jit(solution)/shard_map/hidden/pallas_call | solution.py:175
  116.7 5.0 %collective-permute-done.31.refs_8_ = bf16[8,32,528]{2,1,0:T(8,128)(2,1)} collective-permute-done((bf16[8,32,528]{2,1,0:T(8,128)(2,1)}, bf16[8,32,528]{2,1,0:T(8,128)(2,1)}, u32[]{:S(2)}, u32[]{:S(2)}) %collective-permute-start.31) | collective-permute-done | bytes 270368 | tf_op jit(solution)/shard_map/ppermute | solution.py:401
  128.2 7.1 %collective-permute-done.12.h2 = bf16[512,384]{1,0:T(8,128)(2,1)S(1)} collective-permute-done((bf16[512,384]{1,0:T(8,128)(2,1)}, bf16[512,384]{1,0:T(8,128)(2,1)S(1)}, u32[]{:S(2)}, u32[]{:S(2)}) %collective-permute-start.12) | collective-permute-done | bytes 393248 | tf_op jit(solution)/shard_map/ppermute | solution.py:416
  137.1 2.9 %collective-permute-start.29 = (bf16[4,32,528]{2,1,0:T(8,128)(2,1)S(1)}, bf16[4,32,528]{2,1,0:T(8,128)(2,1)S(1)}, u32[]{:S(2)}, u32[]{:S(2)}) collective-permute-start(bf16[4,32,528]{2,1,0:T(8,128)(2,1)S(1)} %slice.83), channel_id=1, source_target_pairs={{0,24},{4,28},{8,0},{12,4},{16,8},{20,12},{24,16},{28,20},{32,56},... | collective-permute-start | bytes 405512 | tf_op jit(solution)/shard_map/ppermute | solution.py:405
  140.0 5.3 %collective-permute-done.29.refs_5_ = bf16[4,32,528]{2,1,0:T(8,128)(2,1)S(1)} collective-permute-done((bf16[4,32,528]{2,1,0:T(8,128)(2,1)S(1)}, bf16[4,32,528]{2,1,0:T(8,128)(2,1)S(1)}, u32[]{:S(2)}, u32[]{:S(2)}) %collective-permute-start.29) | collective-permute-done | bytes 135200 | tf_op jit(solution)/shard_map/ppermute | solution.py:405
  155.0 3.9 %down.2.rest_0_ = bf16[1024,512]{1,0:T(8,128)(2,1)} custom-call(s32[1]{0:T(128)} %bitcast.2.pos_ref, bf16[512,384]{1,0:T(8,128)(2,1)} %hidden.3.h0, bf16[512,384]{1,0:T(8,128)(2,1)} %copy-done.13, bf16[512,384]{1,0:T(8,128)(2,1)} %copy-done.12, bf16[512,384]{1,0:T(8,128)(2,1)} %copy-done.14, bf16[1,352,2048]{2,1,0:T(8,128)(2,1)} %w0.3, ...), custom_call_target="tpu_custom_call" | custom-call | flops 738197504 | bytes 4000000 | tf_op jit(solution)/shard_map/down/pallas_call | solution.py:207
  159.0 3.9 %down.3 = bf16[1024,512]{1,0:T(8,128)(2,1)} custom-call(s32[1]{0:T(128)} %bitcast.2.pos_ref, bf16[512,384]{1,0:T(8,128)(2,1)} %hidden.2.h0.refs_9_, bf16[512,384]{1,0:T(8,128)(2,1)} %copy-done.10, bf16[512,384]{1,0:T(8,128)(2,1)} %copy-done.9, bf16[512,384]{1,0:T(8,128)(2,1)} %copy-done.11, ...), custom_call_target="tpu_custom_call", output_to_operand_aliasing={{}: (9, {})} | custom-call | flops 738197504 | bytes 4000000 | tf_op jit(solution)/shard_map/down/pallas_call | solution.py:207
  162.9 7.0 %all-to-all-start.1 = ((bf16[64,16,512]{2,1,0:T(8,128)(2,1)}), bf16[64,16,512]{2,1,0:T(8,128)(2,1)S(1)}, u32[]{:S(2)}, u32[]{:S(2)}) async-start(bf16[64,16,512]{2,1,0:T(8,128)(2,1)} %bitcast.64), calls=%async_computation.1 | async-start | bytes 2097152 | tf_op jit(solution)/shard_map/all_to_all | solution.py:424
  173.3 7.9 %shared.1 = (bf16[4,128,1024]{2,1,0:T(8,128)(2,1)}, bf16[4,128,1024]{2,1,0:T(8,128)(2,1)}) custom-call(s32[4]{0:T(128)} %pad_add_fusion.place_ref, bf16[128,2048]{1,0:T(8,128)(2,1)} %t0.1, bf16[128,2048]{1,0:T(8,128)(2,1)} %collective-permute-done.14.t1, bf16[128,2048]{1,0:T(8,128)(2,1)} %collective-permute-done.15.t2, ...), custom_call_target="tpu_custom_call" | custom-call | flops 2214592512 | bytes 6000000 | tf_op jit(solution)/shard_map/shared/pallas_call | solution.py:273
  192.8 10.8 %collective-permute-done.33.s1 = bf16[128,1024]{1,0:T(8,128)(2,1)S(1)} collective-permute-done((bf16[128,1024]{1,0:T(8,128)(2,1)S(1)}, bf16[128,1024]{1,0:T(8,128)(2,1)S(1)}, u32[]{:S(2)}, u32[]{:S(2)}) %collective-permute-start.33) | collective-permute-done | bytes 262176 | tf_op jit(solution)/shard_map/ppermute | solution.py:431
  203.6 3.0 %collective-permute-done.35.s3 = bf16[128,1024]{1,0:T(8,128)(2,1)S(1)} collective-permute-done((bf16[128,1024]{1,0:T(8,128)(2,1)S(1)}, bf16[128,1024]{1,0:T(8,128)(2,1)S(1)}, u32[]{:S(2)}, u32[]{:S(2)}) %collective-permute-start.35) | collective-permute-done | bytes 262176 | tf_op jit(solution)/shard_map/ppermute | solution.py:431
  210.9 3.5 %collective-permute-done.36.got_ref = bf16[128,512]{1,0:T(8,128)(2,1)S(1)} collective-permute-done((bf16[128,512]{1,0:T(8,128)(2,1)}, bf16[128,512]{1,0:T(8,128)(2,1)S(1)}, u32[]{:S(2)}, u32[]{:S(2)}) %collective-permute-start.36) | collective-permute-done | bytes 131104 | tf_op jit(solution)/shard_map/ppermute | solution.py:434
  215.4 3.6 %combine.1 = bf16[128,512]{1,0:T(8,128)(2,1)} custom-call(s32[6,128]{1,0:T(8,128)} %bitcast.71, f32[6,128]{1,0:T(8,128)} %bitcast.72, bf16[1024,512]{1,0:T(8,128)(2,1)} %bitcast.65, f32[128,512]{1,0:T(8,128)} %get-tuple-element.17.keep_ref, bf16[128,512]{1,0:T(8,128)(2,1)} %copy-done.18), custom_call_target="tpu_custom_call" | custom-call | tf_op jit(solution)/shard_map/combine/pallas_call | solution.py:354
  (129 shorter events, 71.7 us)
Async XLA Ops:
  2.8 42.4 %all-to-all-start = ((bf16[64,16,512]{2,1,0:T(8,128)(2,1)}), bf16[64,16,512]{2,1,0:T(8,128)(2,1)S(1)}, u32[]{:S(2)}, u32[]{:S(2)}) async-start(bf16[64,16,512]{2,1,0:T(8,128)(2,1)} %bitcast.66), calls=%async_computation | async-start | bytes 2097152 | tf_op jit(solution)/shard_map/all_to_all | solution.py:382
  24.9 20.9 %collective-permute-start.19 = (bf16[32,528]{1,0:T(8,128)(2,1)S(1)}, bf16[32,528]{1,0:T(8,128)(2,1)S(1)}, u32[]{:S(2)}, u32[]{:S(2)}) collective-permute-start(bf16[32,528]{1,0:T(8,128)(2,1)S(1)} %get-tuple-element.28), channel_id=1, source_target_pairs={{0,96},{4,100},{8,104},{12,108},{16,112},{20,116},{24,120},{28,124... | collective-permute-start | bytes 101384 | tf_op jit(solution)/shard_map/ppermute | solution.py:390
  26.1 24.9 %collective-permute-start.20 = (bf16[32,528]{1,0:T(8,128)(2,1)S(1)}, bf16[32,528]{1,0:T(8,128)(2,1)S(1)}, u32[]{:S(2)}, u32[]{:S(2)}) collective-permute-start(bf16[32,528]{1,0:T(8,128)(2,1)S(1)} %get-tuple-element.27), channel_id=1, source_target_pairs={{0,128},{4,132},{8,136},{12,140},{16,144},{20,148},{24,152},{28,15... | collective-permute-start | bytes 101384 | tf_op jit(solution)/shard_map/ppermute | solution.py:390
  27.7 25.0 %collective-permute-start.21 = (bf16[32,528]{1,0:T(8,128)(2,1)S(1)}, bf16[32,528]{1,0:T(8,128)(2,1)S(1)}, u32[]{:S(2)}, u32[]{:S(2)}) collective-permute-start(bf16[32,528]{1,0:T(8,128)(2,1)S(1)} %get-tuple-element.27), channel_id=1, source_target_pairs={{0,160},{4,164},{8,168},{12,172},{16,176},{20,180},{24,184},{28,18... | collective-permute-start | bytes 101384 | tf_op jit(solution)/shard_map/ppermute | solution.py:390
  31.5 33.7 %collective-permute-start.22 = (bf16[32,528]{1,0:T(8,128)(2,1)S(1)}, bf16[32,528]{1,0:T(8,128)(2,1)S(1)}, u32[]{:S(2)}, u32[]{:S(2)}) collective-permute-start(bf16[32,528]{1,0:T(8,128)(2,1)S(1)} %get-tuple-element.25), channel_id=1, source_target_pairs={{0,192},{4,196},{8,200},{12,204},{16,208},{20,212},{24,216},{28,22... | collective-permute-start | bytes 101384 | tf_op jit(solution)/shard_map/ppermute | solution.py:390
  46.5 51.8 %collective-permute-start = (bf16[1024,512]{1,0:T(8,128)(2,1)S(1)}, bf16[1024,512]{1,0:T(8,128)(2,1)S(1)}, u32[]{:S(2)}, u32[]{:S(2)}) collective-permute-start(bf16[1024,512]{1,0:T(8,128)(2,1)S(1)} %bitcast.61), channel_id=1, source_target_pairs={{0,1},{1,0},{2,3},{3,2},{4,5},{5,4},{6,7},{7,6},{8,9},{9,8},{10,11... | collective-permute-start | bytes 3145736 | tf_op jit(solution)/shard_map/ppermute | solution.py:411
  52.7 19.3 %collective-permute-start.23 = (bf16[32,528]{1,0:T(8,128)(2,1)S(1)}, bf16[32,528]{1,0:T(8,128)(2,1)S(1)}, u32[]{:S(2)}, u32[]{:S(2)}) collective-permute-start(bf16[32,528]{1,0:T(8,128)(2,1)S(1)} %get-tuple-element.25), channel_id=1, source_target_pairs={{0,224},{4,228},{8,232},{12,236},{16,240},{20,244},{24,248},{28,25... | collective-permute-start | bytes 101384 | tf_op jit(solution)/shard_map/ppermute | solution.py:390
  54.7 46.2 %collective-permute-start.2 = (bf16[512,512]{1,0:T(8,128)(2,1)S(1)}, bf16[512,512]{1,0:T(8,128)(2,1)}, u32[]{:S(2)}, u32[]{:S(2)}) collective-permute-start(bf16[512,512]{1,0:T(8,128)(2,1)S(1)} %collective-permute-done.1.x2), channel_id=1, source_target_pairs={{0,1},{1,0},{2,3},{3,2},{4,5},{5,4},{6,7},{7,6},{8,9},{9,8},{10,11... | collective-permute-start | bytes 1572872 | tf_op jit(solution)/shard_map/ppermute | solution.py:414
  66.9 39.9 %collective-permute-start.10 = (bf16[512,512]{1,0:T(8,128)(2,1)}, bf16[512,512]{1,0:T(8,128)(2,1)}, u32[]{:S(2)}, u32[]{:S(2)}) collective-permute-start(bf16[512,512]{1,0:T(8,128)(2,1)} %collective-permute-done.9.x2), channel_id=1, source_target_pairs={{0,1},{1,0},{2,3},{3,2},{4,5},{5,4},{6,7},{7,6},{8,9},{9,8},{10,11... | collective-permute-start | bytes 1572872 | tf_op jit(solution)/shard_map/ppermute | solution.py:414
  75.9 21.3 %collective-permute-start.25 = (bf16[8,32,528]{2,1,0:T(8,128)(2,1)}, bf16[8,32,528]{2,1,0:T(8,128)(2,1)S(1)}, u32[]{:S(2)}, u32[]{:S(2)}) collective-permute-start(bf16[8,32,528]{2,1,0:T(8,128)(2,1)} %bitcast_dynamic-update-slice_fusion.refs_0_), channel_id=1, source_target_pairs={{0,8},{4,12},{8,16},{12,20},{16,24},{20,28},{24,0},{28,4},{32,40},... | collective-permute-start | bytes 811016 | tf_op jit(solution)/shard_map/ppermute | solution.py:401
  84.1 38.7 %collective-permute-start.6 = (bf16[352,512]{1,0:T(8,128)(2,1)}, bf16[352,512]{1,0:T(8,128)(2,1)S(1)}, u32[]{:S(2)}, u32[]{:S(2)}) collective-permute-start(bf16[352,512]{1,0:T(8,128)(2,1)} %get-tuple-element.12), channel_id=1, source_target_pairs={{0,1},{1,0},{2,3},{3,2},{4,5},{5,4},{6,7},{7,6},{8,9},{9,8},{10,11... | collective-permute-start | bytes 1081352 | tf_op jit(solution)/shard_map/ppermute | solution.py:396
  97.9 26.7 %collective-permute-start.7 = (bf16[352,512]{1,0:T(8,128)(2,1)}, bf16[352,512]{1,0:T(8,128)(2,1)S(1)}, u32[]{:S(2)}, u32[]{:S(2)}) collective-permute-start(bf16[352,512]{1,0:T(8,128)(2,1)} %get-tuple-element.13), channel_id=1, source_target_pairs={{0,2},{2,0},{1,3},{3,1},{4,6},{6,4},{5,7},{7,5},{8,10},{10,8},{9,1... | collective-permute-start | bytes 1081352 | tf_op jit(solution)/shard_map/ppermute | solution.py:396
  98.3 17.3 %collective-permute-start.28 = (bf16[8,32,528]{2,1,0:T(8,128)(2,1)}, bf16[8,32,528]{2,1,0:T(8,128)(2,1)}, u32[]{:S(2)}, u32[]{:S(2)}) collective-permute-start(bf16[8,32,528]{2,1,0:T(8,128)(2,1)} %bitcast_dynamic-update-slice_fusion.refs_0_), channel_id=1, source_target_pairs={{0,24},{4,28},{8,0},{12,4},{16,8},{20,12},{24,16},{28,20},{32,56},... | collective-permute-start | bytes 811016 | tf_op jit(solution)/shard_map/ppermute | solution.py:401
  100.9 20.8 %collective-permute-start.31 = (bf16[8,32,528]{2,1,0:T(8,128)(2,1)}, bf16[8,32,528]{2,1,0:T(8,128)(2,1)}, u32[]{:S(2)}, u32[]{:S(2)}) collective-permute-start(bf16[8,32,528]{2,1,0:T(8,128)(2,1)} %bitcast_dynamic-update-slice_fusion.refs_0_), channel_id=1, source_target_pairs={{0,28},{4,0},{8,4},{12,8},{16,12},{20,16},{24,20},{28,24},{32,60},... | collective-permute-start | bytes 811016 | tf_op jit(solution)/shard_map/ppermute | solution.py:401
  106.8 17.9 %collective-permute-start.8 = (bf16[352,512]{1,0:T(8,128)(2,1)}, bf16[352,512]{1,0:T(8,128)(2,1)S(1)}, u32[]{:S(2)}, u32[]{:S(2)}) collective-permute-start(bf16[352,512]{1,0:T(8,128)(2,1)} %get-tuple-element.14), channel_id=1, source_target_pairs={{0,3},{3,0},{1,2},{2,1},{4,7},{7,4},{5,6},{6,5},{8,11},{11,8},{9,1... | collective-permute-start | bytes 1081352 | tf_op jit(solution)/shard_map/ppermute | solution.py:396
  122.8 25.1 %collective-permute-start.3 = (bf16[512,384]{1,0:T(8,128)(2,1)S(1)}, bf16[512,384]{1,0:T(8,128)(2,1)S(1)}, u32[]{:S(2)}, u32[]{:S(2)}) collective-permute-start(bf16[512,384]{1,0:T(8,128)(2,1)S(1)} %copy-done.3), channel_id=1, source_target_pairs={{0,1},{1,0},{2,3},{3,2},{4,5},{5,4},{6,7},{7,6},{8,9},{9,8},{10,11... | collective-permute-start | bytes 1179656 | tf_op jit(solution)/shard_map/ppermute | solution.py:417
  124.6 24.9 %collective-permute-start.11 = (bf16[512,384]{1,0:T(8,128)(2,1)}, bf16[512,384]{1,0:T(8,128)(2,1)S(1)}, u32[]{:S(2)}, u32[]{:S(2)}) collective-permute-start(bf16[512,384]{1,0:T(8,128)(2,1)} %hidden.3.h0), channel_id=1, source_target_pairs={{0,1},{1,0},{2,3},{3,2},{4,5},{5,4},{6,7},{7,6},{8,9},{9,8},{10,11... | collective-permute-start | bytes 1179656 | tf_op jit(solution)/shard_map/ppermute | solution.py:417
  126.9 24.6 %collective-permute-start.5 = (bf16[512,384]{1,0:T(8,128)(2,1)S(1)}, bf16[512,384]{1,0:T(8,128)(2,1)S(1)}, u32[]{:S(2)}, u32[]{:S(2)}) collective-permute-start(bf16[512,384]{1,0:T(8,128)(2,1)S(1)} %collective-permute-done.4.h2), channel_id=1, source_target_pairs={{0,1},{1,0},{2,3},{3,2},{4,5},{5,4},{6,7},{7,6},{8,9},{9,8},{10,11... | collective-permute-start | bytes 1179656 | tf_op jit(solution)/shard_map/ppermute | solution.py:422
  145.3 24.6 %collective-permute-start.14 = (bf16[128,2048]{1,0:T(8,128)(2,1)S(1)}, bf16[128,2048]{1,0:T(8,128)(2,1)}, u32[]{:S(2)}, u32[]{:S(2)}) collective-permute-start(bf16[128,2048]{1,0:T(8,128)(2,1)S(1)} %copy-done.8), channel_id=1, source_target_pairs={{0,64},{4,68},{8,72},{12,76},{16,80},{20,84},{24,88},{28,92},{32,9... | collective-permute-start | bytes 1572872 | tf_op jit(solution)/shard_map/ppermute | solution.py:400
  148.0 24.5 %collective-permute-start.15 = (bf16[128,2048]{1,0:T(8,128)(2,1)S(1)}, bf16[128,2048]{1,0:T(8,128)(2,1)}, u32[]{:S(2)}, u32[]{:S(2)}) collective-permute-start(bf16[128,2048]{1,0:T(8,128)(2,1)S(1)} %copy-done.8), channel_id=1, source_target_pairs={{0,128},{4,132},{8,136},{12,140},{16,144},{20,148},{24,152},{28,15... | collective-permute-start | bytes 1572872 | tf_op jit(solution)/shard_map/ppermute | solution.py:400
  149.6 22.9 %collective-permute-start.16 = (bf16[128,2048]{1,0:T(8,128)(2,1)S(1)}, bf16[128,2048]{1,0:T(8,128)(2,1)}, u32[]{:S(2)}, u32[]{:S(2)}) collective-permute-start(bf16[128,2048]{1,0:T(8,128)(2,1)S(1)} %copy-done.8), channel_id=1, source_target_pairs={{0,192},{4,196},{8,200},{12,204},{16,208},{20,212},{24,216},{28,22... | collective-permute-start | bytes 1572872 | tf_op jit(solution)/shard_map/ppermute | solution.py:400
  151.5 21.0 %collective-permute-start.26 = (bf16[8,32,528]{2,1,0:T(8,128)(2,1)}, bf16[8,32,528]{2,1,0:T(8,128)(2,1)S(1)}, u32[]{:S(2)}, u32[]{:S(2)}) collective-permute-start(bf16[8,32,528]{2,1,0:T(8,128)(2,1)} %copy-done.19), channel_id=1, source_target_pairs={{0,4},{4,8},{8,12},{12,16},{16,20},{20,24},{24,28},{28,0},{32,36},... | collective-permute-start | bytes 811016 | tf_op jit(solution)/shard_map/ppermute | solution.py:402
  152.4 20.1 %collective-permute-start.30 = (bf16[8,32,528]{2,1,0:T(8,128)(2,1)}, bf16[8,32,528]{2,1,0:T(8,128)(2,1)}, u32[]{:S(2)}, u32[]{:S(2)}) collective-permute-start(bf16[8,32,528]{2,1,0:T(8,128)(2,1)} %collective-permute-done.28.refs_7_), channel_id=1, source_target_pairs={{0,28},{4,0},{8,4},{12,8},{16,12},{20,16},{24,20},{28,24},{32,60},... | collective-permute-start | bytes 811016 | tf_op jit(solution)/shard_map/ppermute | solution.py:403
  162.9 51.5 %all-to-all-start.1 = ((bf16[64,16,512]{2,1,0:T(8,128)(2,1)}), bf16[64,16,512]{2,1,0:T(8,128)(2,1)S(1)}, u32[]{:S(2)}, u32[]{:S(2)}) async-start(bf16[64,16,512]{2,1,0:T(8,128)(2,1)} %bitcast.64), calls=%async_computation.1 | async-start | bytes 2097152 | tf_op jit(solution)/shard_map/all_to_all | solution.py:424
  (41 other events, 515.4 us)

commit v5 on v4

--- a/solution.py
+++ b/solution.py
@@ -38,6 +38,9 @@
     ]
 
 
+PLANES = [[xy * NZ + z for xy in range(NX * NY)] for z in range(NZ)]
+
+
 def silu(v):
     return v / (1.0 + jnp.exp(-v))
 
@@ -101,24 +104,22 @@
     )(pos, ids_t, tokens)
 
 
-def pack_kernel(place_ref, gate_ref, up_ref, down_ref, out_ref):
+def pack_kernel(gate_ref, up_ref, down_ref, out_ref):
     fs = out_ref.shape[2] // 3
     for x in range(NX):
         cut = slice(x * fs, (x + 1) * fs)
         one = jnp.concatenate([gate_ref[:, cut], up_ref[:, cut], down_ref[:, cut]], axis=1)
-        out_ref[pl.ds((x - place_ref[1]) & (NX - 1), 1)] = one[None]
-
-
-def pack(place, gate, up, down_t):
+        for y in range(NY):
+            out_ref[x * NY + y] = one
+
+
+def pack(gate, up, down_t):
     fs = gate.shape[1] // NX
-    vmem = pl.BlockSpec(memory_space=pltpu.VMEM)
     return pl.pallas_call(
         pack_kernel,
-        in_specs=[pl.BlockSpec(memory_space=pltpu.SMEM)] + [vmem] * 3,
-        out_specs=vmem,
-        out_shape=jax.ShapeDtypeStruct((NX, gate.shape[0], 3 * fs), BF16),
+        out_shape=jax.ShapeDtypeStruct((NX * NY, gate.shape[0], 3 * fs), BF16),
         name="pack",
-    )(place, gate, up, down_t)
+    )(gate, up, down_t)
 
 
 def cut_kernel(pos_ref, a, b, c, out_a, out_b, out_c):
@@ -136,9 +137,9 @@
             num_scalar_prefetch=1,
             grid=(1,),
             in_specs=[
-                pl.BlockSpec((1, mf, COLS), lambda i, p: (0, 0, p[0] ^ 1)),
                 pl.BlockSpec((1, mf, COLS), lambda i, p: (0, 0, p[0] ^ 2)),
                 pl.BlockSpec((1, mf, COLS), lambda i, p: (0, 0, p[0] ^ 3)),
+                pl.BlockSpec((1, mf, COLS), lambda i, p: (0, 0, p[0] ^ 1)),
             ],
             out_specs=[pl.BlockSpec((mf, COLS), lambda i, p: (0, 0))] * 3,
         ),
@@ -225,15 +226,12 @@
 
 
 def shared_kernel(place_ref, t0, t1, t2, t3, *refs):
-    blocks, (keep_ref, send_ref, w_ref, sems) = refs[:9], refs[10:]
-    core, x, y, z = place_ref[0] & 1, place_ref[1], place_ref[2], place_ref[3]
+    blocks, (keep_ref, send_ref, w_ref, sems) = refs[:NZ], refs[NZ + 1 :]
+    core, z = place_ref[0] & 1, place_ref[1]
     copies = []
-    for j, (block, step) in enumerate(zip(blocks, (0, 1, 2, 3, 4, 4, 5, 6, 7))):
+    for step, block in enumerate(blocks):
         to = w_ref.at[(z - step) & (NZ - 1)]
-        if block.shape[0] < w_ref.shape[1]:
-            first = 0 if j == 4 else block.shape[0]
-            to = to.at[pl.ds(first, block.shape[0])]
-        copies.append(pltpu.make_async_copy(block, to, sems.at[j]))
+        copies.append(pltpu.make_async_copy(block, to, sems.at[step]))
     for copy in copies:
         copy.start()
     for copy in copies:
@@ -243,8 +241,7 @@
     rows = NZ * w_ref.shape[2]
 
     def columns(quarter, half):
-        at = ((x - quarter) & (NX - 1)) * NY + (half ^ y)
-        return w_ref[:, pl.ds(at, 1)].reshape(rows, fs3)
+        return w_ref[:, pl.ds(quarter * NY + half, 1)].reshape(rows, fs3)
 
     toks = (t0, t1, t2, t3)
     totals = [jnp.zeros((TOK, fs3), F32) for _ in toks]
@@ -274,12 +271,12 @@
         shared_kernel,
         in_specs=[pl.BlockSpec(memory_space=pltpu.SMEM)]
         + [vmem] * 4
-        + [pl.BlockSpec(memory_space=pl.ANY)] * 10,
+        + [pl.BlockSpec(memory_space=pl.ANY)] * (NZ + 1),
         out_specs=[vmem, vmem],
         out_shape=[jax.ShapeDtypeStruct((NX, TOK, D // 2), BF16)] * 2,
         scratch_shapes=[
             pltpu.VMEM((NZ,) + blocks[0].shape, BF16),
-            pltpu.SemaphoreType.DMA((9,)),
+            pltpu.SemaphoreType.DMA((NZ,)),
         ],
         cost_estimate=pl.CostEstimate(
             flops=2 * NX * TOK * D * fs3 * 2, bytes_accessed=6_000_000, transcendentals=NX * TOK * fs3 // 3
@@ -375,35 +372,27 @@
     gate_t = expert_gate.transpose(0, 2, 1)
     up_t = expert_up.transpose(0, 2, 1)
 
-    wide = lax.axis_index("wide").astype(jnp.int32)
-    place = jnp.stack([pos[0], wide >> 4, (wide >> 3) & 1, wide & 7])
+    place = jnp.stack([pos[0], lax.axis_index("wide").astype(jnp.int32) & (NZ - 1)])
+
+    pieces = pack(shared_gate, shared_up, shared_down.T)
+    column = lax.all_to_all(pieces, "wide", 0, 0, axis_index_groups=PLANES, tiled=True)
 
     outgoing = dispatch(pos, ids_t, tokens).reshape(EXPERTS, CAP, COLS)
     own = lax.all_to_all(outgoing, "wide", 0, 0, tiled=True).reshape(SLOTS, COLS)
 
-    pieces = pack(place, shared_gate, shared_up, shared_down.T)
-    column = []
-    for d in range(NX):
-        for flip in range(NY):
-            one = pieces[d]
-            if d or flip:
-                one = lax.ppermute(one, "wide", moved(d, flip, 0))
-            column.append(one)
-    column = jnp.stack(column)
     cuts = cut(pos, expert_down)
-    toks = [tokens]
     others = [
         lax.ppermute(w, "narrow", swap)
-        for w, swap in zip(cuts, (CORE_SWAP, Y_SWAP, BOTH_SWAP))
+        for w, swap in zip(cuts, (Y_SWAP, BOTH_SWAP, CORE_SWAP))
     ]
+    near = {k: lax.ppermute(column, "wide", moved(0, 0, k)) for k in (2, -2, 1, -1)}
+    toks = [tokens]
     for d in range(1, NX):
         toks.append(lax.ppermute(tokens, "wide", moved(d, 0, 0)))
-    near = {k: lax.ppermute(column, "wide", moved(0, 0, k)) for k in (2, -2, 1, -1)}
     third = lax.ppermute(near[2], "wide", moved(0, 0, 1))
+    fourth = lax.ppermute(near[2], "wide", moved(0, 0, 2))
     fifth = lax.ppermute(near[-2], "wide", moved(0, 0, -1))
-    fourth_a = lax.ppermute(near[2][:4], "wide", moved(0, 0, 2))
-    fourth_b = lax.ppermute(near[-2][4:], "wide", moved(0, 0, -2))
-    blocks = [column, near[1], near[2], third, fourth_a, fourth_b, fifth, near[-2], near[-1]]
+    blocks = [column, near[1], near[2], third, fourth, fifth, near[-2], near[-1]]
 
     ys = []
     for k in range(CHUNKS):
@@ -415,14 +404,8 @@
         hidden = expert_hidden(pos, k, own, core, ys[k], both, gate_t, up_t)
         hidden_y = lax.ppermute(hidden, "narrow", Y_SWAP)
         hidden_core = lax.ppermute(hidden, "narrow", CORE_SWAP)
-        hiddens.append([hidden, hidden_core, hidden_y])
+        hiddens.append([hidden, hidden_y, hidden_core])
     mine, theirs = shared_ffn(place, toks, blocks, hiddens[-1][0])
-    outputs = None
-    for k in range(CHUNKS):
-        hidden_both = lax.ppermute(hiddens[k][2], "narrow", CORE_SWAP)
-        outputs = expert_columns(pos, k, hiddens[k] + [hidden_both], expert_down, others, outputs)
-    returned = lax.all_to_all(outputs.reshape(EXPERTS, CAP, COLS), "wide", 0, 0, tiled=True)
-
     theirs = lax.ppermute(theirs, "narrow", CORE_SWAP)
     shared = []
     for d in range(NX):
@@ -430,6 +413,13 @@
         if d > 0:
             one = lax.ppermute(one, "wide", moved(-d, 0, 0))
         shared.append(one)
+    outputs = None
+    for k in range(CHUNKS):
+        hidden_both = lax.ppermute(hiddens[k][1], "narrow", CORE_SWAP)
+        hiddens[k].insert(2, hidden_both)
+        outputs = expert_columns(pos, k, hiddens[k], expert_down, others, outputs)
+    returned = lax.all_to_all(outputs.reshape(EXPERTS, CAP, COLS), "wide", 0, 0, tiled=True)
+
     kept, sent = fold(pos, shared)
     got = lax.ppermute(sent, "narrow", Y_SWAP)
     return combine(ids_t, gates_t, returned.reshape(SLOTS, COLS), kept, got)

time: 221 us -> 200 us (0.905)
  starting transfers between devices: 97 us -> 48.1 us
  blocking collectives: 0 us -> 42.4 us
  waiting for transfers between devices: 70.1 us -> 60.1 us
  local copies, waits for them, and re-layouts: 9.84 us -> 3.33 us
    all_to_all x0 -> x1, blocking collectives: none -> 42.4 us  [body(): lax.all_to_all(outgoing, 'wide', 0, 0, tiled=True).reshape(SLOTS, COLS)]
    ppermute x2, waiting for transfers between devices: 1.22 us -> 19.4 us  [body(): lax.ppermute(own[k * CHUNK_ROWS:(k + 1) * CHUNK_ROWS], 'narrow', Y_SWAP)]
    ppermute x11 -> x3, starting transfers between devices: 19.1 us -> 2.54 us  [the longest x2 2.07 us: body(): hidden_both = lax.ppermute(hiddens[k][1], 'narrow', CORE_SWAP)]
    ppermute x2, starting transfers between devices: 15.6 us -> 2.64 us  [body(): both = lax.ppermute(ys[k], 'narrow', CORE_SWAP)]
    ppermute x4, waiting for transfers between devices: 20.6 us -> 8.01 us  [body(): lax.ppermute(column, 'wide', moved(0, 0, k))]
    all_to_all x1, starting transfers between devices: 15.1 us -> 3.82 us  [body(): lax.all_to_all(pieces, 'wide', 0, 0, axis_index_groups=PLANES, tiled=True)]
    ppermute x2, waiting for transfers between devices: 8.28 us -> 0.01 us  [body(): hidden_y = lax.ppermute(hidden, 'narrow', Y_SWAP)]
    ppermute x11 -> x3, waiting for transfers between devices: 5.29 us -> 0.01 us  [the longest x2 0.01 us: body(): hidden_both = lax.ppermute(hiddens[k][1], 'narrow', CORE_SWAP)]
  transfers between devices with their start and end apart: 39 -> 31, of which waited for: 15 -> 13; matrix products, arithmetic and copies ran while one was open for 3% -> 2% of each run, Pallas kernels for 15% -> 17%
where the time goes in v5:
time: 200 us; the launch traced here: 196 us
  waiting for transfers between devices  60.1 us (30%)
  starting transfers between devices  48.1 us (24%)
  blocking collectives  42.4 us (21%)
  Pallas kernels  39.1 us (20%)
  local copies, waits for them, and re-layouts  3.33 us (2%)
  other arithmetic  2.96 us (1%)
    all_to_all x1, blocking collectives, body(): lax.all_to_all(outgoing, 'wide', 0, 0, tiled=True).reshape(SLOTS, COLS)  42.4 us
    ppermute x2, waiting for transfers between devices, body(): lax.ppermute(own[k * CHUNK_ROWS:(k + 1) * CHUNK_ROWS], 'narrow', Y_SWAP)  19.4 us
    ppermute x3, waiting for transfers between devices, body(): one = lax.ppermute(one, 'wide', moved(-d, 0, 0))  14.4 us
    pallas_call x2, Pallas kernels, expert_hidden(): pl.pallas_call(hidden_kernel, grid_spec=pltpu.PrefetchScalarGridSpec(num_...  10.9 us
    ppermute x4, starting transfers between devices, body(): lax.ppermute(column, 'wide', moved(0, 0, k))  10 us
    ppermute x4, waiting for transfers between devices, body(): lax.ppermute(column, 'wide', moved(0, 0, k))  8.01 us
    pallas_call x1, Pallas kernels, shared_ffn(): pl.pallas_call(shared_kernel, in_specs=[pl.BlockSpec(memory_space=pltpu.S...  7.94 us
    pallas_call x2, Pallas kernels, expert_columns(): pl.pallas_call(down_kernel, grid_spec=pltpu.PrefetchScalarGridSpec(num_sc...  7.83 us
  transfers between devices with their start and end apart: 31, of which 13 were waited for; matrix products, arithmetic and copies ran while one was open for 2% of the time, Pallas kernels for 17%

profile of v5, /device:TPU:1, one launch (start us, length us, event | category | flops | bytes accessed | tf_op | source)
XLA Modules:
  0.0 196.1 jit_solution(8053495032914707193)
XLA Ops:
  0.0 2.8 %dispatch.1 = bf16[1024,512]{1,0:T(8,128)(2,1)} custom-call(s32[1]{0:T(128)} %bitcast.2.pos_ref, s32[6,128]{1,0:T(8,128)} %bitcast.46, bf16[128,2048]{1,0:T(8,128)(2,1)} %t0.1), custom_call_target="tpu_custom_call" | custom-call | tf_op jit(solution)/shard_map/dispatch/pallas_call | solution.py:91
  2.8 42.4 %all_to_all.15 = bf16[64,16,512]{2,1,0:T(8,128)(2,1)S(1)} all-to-all(bf16[64,16,512]{2,1,0:T(8,128)(2,1)} %bitcast.42), channel_id=1, replica_groups=mesh['wide'=64,'narrow'=4] {'wide'}, dimensions={0} | all-to-all | bytes 2097152 | tf_op jit(solution)/shard_map/all_to_all | solution.py:381
  45.2 4.2 %collective-permute-start = (bf16[1024,512]{1,0:T(8,128)(2,1)S(1)}, bf16[1024,512]{1,0:T(8,128)(2,1)S(1)}, u32[]{:S(2)}, u32[]{:S(2)}) collective-permute-start(bf16[1024,512]{1,0:T(8,128)(2,1)S(1)} %bitcast.37), channel_id=1, source_target_pairs={{0,1},{1,0},{2,3},{3,2},{4,5},{5,4},{6,7},{7,6},{8,9},{9,8},{10,11... | collective-permute-start | bytes 3145736 | tf_op jit(solution)/shard_map/ppermute | solution.py:400
  51.0 12.1 %collective-permute-done.1.x2 = bf16[512,512]{1,0:T(8,128)(2,1)} collective-permute-done((bf16[512,512]{1,0:T(8,128)(2,1)S(1)}, bf16[512,512]{1,0:T(8,128)(2,1)}, u32[]{:S(2)}, u32[]{:S(2)}) %collective-permute-start.1) | collective-permute-done | bytes 524320 | tf_op jit(solution)/shard_map/ppermute | solution.py:399
  67.1 7.3 %collective-permute-done.9.x2 = bf16[512,512]{1,0:T(8,128)(2,1)} collective-permute-done((bf16[512,512]{1,0:T(8,128)(2,1)S(1)}, bf16[512,512]{1,0:T(8,128)(2,1)}, u32[]{:S(2)}, u32[]{:S(2)}) %collective-permute-start.9) | collective-permute-done | bytes 524320 | tf_op jit(solution)/shard_map/ppermute | solution.py:399
  77.4 3.8 %all-to-all-start.2 = ((bf16[8,32,528]{2,1,0:T(8,128)(2,1)}), bf16[8,32,528]{2,1,0:T(8,128)(2,1)S(1)}, u32[]{:S(2)}, u32[]{:S(2)}) async-start(bf16[8,32,528]{2,1,0:T(8,128)(2,1)} %pack.1), calls=%async_computation.2 | async-start | bytes 655360 | tf_op jit(solution)/shard_map/all_to_all | solution.py:378
  82.9 7.2 %all-to-all-done.2.refs_0_ = bf16[8,32,528]{2,1,0:T(8,128)(2,1)S(1)} async-done(((bf16[8,32,528]{2,1,0:T(8,128)(2,1)}), bf16[8,32,528]{2,1,0:T(8,128)(2,1)S(1)}, u32[]{:S(2)}, u32[]{:S(2)}) %all-to-all-start.2) | async-done | bytes 270368 | tf_op jit(solution)/shard_map/all_to_all | solution.py:378
  92.1 5.5 %hidden.2.h0.refs_8_ = bf16[512,384]{1,0:T(8,128)(2,1)} custom-call(s32[1]{0:T(128)} %bitcast.2.pos_ref, bf16[1024,512]{1,0:T(8,128)(2,1)} %bitcast.38, bf16[1024,512]{1,0:T(8,128)(2,1)} %copy-done.1, bf16[512,512]{1,0:T(8,128)(2,1)} %collective-permute-done.1.x2, bf16[512,512]{1,0:T(8,128)(2,1)} %collective-permute-done.2.x3, ...), custom_call_target="tpu_custom_call" | custom-call | flops 1476395008 | bytes 6000000 | tf_op jit(solution)/shard_map/hidden/pallas_call | solution.py:176
  97.6 2.8 %collective-permute-start.21 = (bf16[8,32,528]{2,1,0:T(8,128)(2,1)S(1)}, bf16[8,32,528]{2,1,0:T(8,128)(2,1)}, u32[]{:S(2)}, u32[]{:S(2)}) collective-permute-start(bf16[8,32,528]{2,1,0:T(8,128)(2,1)S(1)} %all-to-all-done.2.refs_0_), channel_id=1, source_target_pairs={{0,24},{4,28},{8,0},{12,4},{16,8},{20,12},{24,16},{28,20},{32,56},... | collective-permute-start | bytes 811016 | tf_op jit(solution)/shard_map/ppermute | solution.py:388
  100.4 5.4 %hidden.3.h0 = bf16[512,384]{1,0:T(8,128)(2,1)} custom-call(s32[1]{0:T(128)} %bitcast.2.pos_ref, bf16[1024,512]{1,0:T(8,128)(2,1)} %bitcast.39, bf16[1024,512]{1,0:T(8,128)(2,1)} %copy-done.1, bf16[512,512]{1,0:T(8,128)(2,1)} %collective-permute-done.9.x2, bf16[512,512]{1,0:T(8,128)(2,1)} %collective-permute-done.10.x3, bf16[1,352,2048]{2,1,0:T(8,128)(2,1)} %bitcast.25, ...), custom_call_target="tpu_custom_call" | custom-call | flops 1476395008 | bytes 6000000 | tf_op jit(solution)/shard_map/hidden/pallas_call | solution.py:176
  108.0 5.1 %collective-permute-start.23 = (bf16[8,32,528]{2,1,0:T(8,128)(2,1)S(1)}, bf16[8,32,528]{2,1,0:T(8,128)(2,1)}, u32[]{:S(2)}, u32[]{:S(2)}) collective-permute-start(bf16[8,32,528]{2,1,0:T(8,128)(2,1)S(1)} %all-to-all-done.2.refs_0_), channel_id=1, source_target_pairs={{0,28},{4,0},{8,4},{12,8},{16,12},{20,16},{24,20},{28,24},{32,60},... | collective-permute-start | bytes 811016 | tf_op jit(solution)/shard_map/ppermute | solution.py:388
  115.9 5.8 %collective-permute-done.23.refs_7_ = bf16[8,32,528]{2,1,0:T(8,128)(2,1)} collective-permute-done((bf16[8,32,528]{2,1,0:T(8,128)(2,1)S(1)}, bf16[8,32,528]{2,1,0:T(8,128)(2,1)}, u32[]{:S(2)}, u32[]{:S(2)}) %collective-permute-start.23) | collective-permute-done | bytes 270368 | tf_op jit(solution)/shard_map/ppermute | solution.py:388
  132.4 3.9 %down.2.rest_0_ = bf16[1024,512]{1,0:T(8,128)(2,1)} custom-call(s32[1]{0:T(128)} %bitcast.2.pos_ref, bf16[512,384]{1,0:T(8,128)(2,1)} %hidden.3.h0, bf16[512,384]{1,0:T(8,128)(2,1)} %copy-done.11, bf16[512,384]{1,0:T(8,128)(2,1)} %copy-done.13, bf16[512,384]{1,0:T(8,128)(2,1)} %copy-done.12, bf16[1,352,2048]{2,1,0:T(8,128)(2,1)} %w0.3, ...), custom_call_target="tpu_custom_call" | custom-call | flops 738197504 | bytes 4000000 | tf_op jit(solution)/shard_map/down/pallas_call | solution.py:208
  136.4 3.9 %down.3 = bf16[1024,512]{1,0:T(8,128)(2,1)} custom-call(s32[1]{0:T(128)} %bitcast.2.pos_ref, bf16[512,384]{1,0:T(8,128)(2,1)} %hidden.2.h0.refs_8_, bf16[512,384]{1,0:T(8,128)(2,1)} %copy-done.8, bf16[512,384]{1,0:T(8,128)(2,1)} %copy-done.10, bf16[512,384]{1,0:T(8,128)(2,1)} %copy-done.9, bf16[1,352,2048]{2,1,0:T(8,128)(2,1)} %w0.3, ...), custom_call_target="tpu_custom_call", output_to_operand_aliasing={{}: (9, {})} | custom-call | flops 738197504 | bytes 4000000 | tf_op jit(solution)/shard_map/down/pallas_call | solution.py:208
  140.3 5.4 %all-to-all-start.1 = ((bf16[64,16,512]{2,1,0:T(8,128)(2,1)}), bf16[64,16,512]{2,1,0:T(8,128)(2,1)S(1)}, u32[]{:S(2)}, u32[]{:S(2)}) async-start(bf16[64,16,512]{2,1,0:T(8,128)(2,1)} %bitcast.40), calls=%async_computation.1 | async-start | bytes 2097152 | tf_op jit(solution)/shard_map/all_to_all | solution.py:421
  146.3 4.0 %collective-permute-done.16.t3 = bf16[128,2048]{1,0:T(8,128)(2,1)} collective-permute-done((bf16[128,2048]{1,0:T(8,128)(2,1)S(1)}, bf16[128,2048]{1,0:T(8,128)(2,1)}, u32[]{:S(2)}, u32[]{:S(2)}) %collective-permute-start.16) | collective-permute-done | bytes 524320 | tf_op jit(solution)/shard_map/ppermute | solution.py:391
  151.1 7.9 %shared.1 = (bf16[4,128,1024]{2,1,0:T(8,128)(2,1)}, bf16[4,128,1024]{2,1,0:T(8,128)(2,1)}) custom-call(s32[2]{0:T(128)} %pad_add_fusion.place_ref, bf16[128,2048]{1,0:T(8,128)(2,1)} %t0.1, bf16[128,2048]{1,0:T(8,128)(2,1)} %copy-done.19, bf16[128,2048]{1,0:T(8,128)(2,1)} %collective-permute-done.15.t2, bf16[128,2048]{1,0:T(8,128)(2,1)} %collective-permute-done.16.t3, ...), custom_call_target="tpu_custom_call" | custom-call | flops 2214592512 | bytes 6000000 | tf_op jit(solution)/shard_map/shared/pallas_call | solution.py:270
  159.0 3.3 %collective-permute-start.24 = (bf16[4,128,1024]{2,1,0:T(8,128)(2,1)}, bf16[4,128,1024]{2,1,0:T(8,128)(2,1)S(1)}, u32[]{:S(2)}, u32[]{:S(2)}) collective-permute-start(bf16[4,128,1024]{2,1,0:T(8,128)(2,1)} %get-tuple-element.16), channel_id=1, source_target_pairs={{0,1},{1,0},{2,3},{3,2},{4,5},{5,4},{6,7},{7,6},{8,9},{9,8},{10,11... | collective-permute-start | bytes 3145736 | tf_op jit(solution)/shard_map/ppermute | solution.py:409
  162.4 2.5 %collective-permute-done.24 = bf16[4,128,1024]{2,1,0:T(8,128)(2,1)S(1)} collective-permute-done((bf16[4,128,1024]{2,1,0:T(8,128)(2,1)}, bf16[4,128,1024]{2,1,0:T(8,128)(2,1)S(1)}, u32[]{:S(2)}, u32[]{:S(2)}) %collective-permute-start.24) | collective-permute-done | bytes 1048608 | tf_op jit(solution)/shard_map/ppermute | solution.py:409
  164.9 2.3 %fusion.3 = (bf16[128,1024]{1,0:T(8,128)(2,1)S(1)}, bf16[128,1024]{1,0:T(8,128)(2,1)S(1)}, bf16[128,1024]{1,0:T(8,128)(2,1)S(1)}, bf16[128,1024]{1,0:T(8,128)(2,1)}) fusion(bf16[4,128,1024]{2,1,0:T(8,128)(2,1)S(1)} %collective-permute-done.24, bf16[4,128,1024]{2,1,0:T(8,128)(2,1)} %get-tuple-element.15), kind=kLoop, calls=%fused_computation.7 | loop fusion | flops 2097152 | bytes 3145728 | tf_op jit(solution)/shard_map/convert_element_type | solution.py:412
  169.6 6.7 %collective-permute-done.25.s1 = bf16[128,1024]{1,0:T(8,128)(2,1)S(1)} collective-permute-done((bf16[128,1024]{1,0:T(8,128)(2,1)S(1)}, bf16[128,1024]{1,0:T(8,128)(2,1)S(1)}, u32[]{:S(2)}, u32[]{:S(2)}) %collective-permute-start.25) | collective-permute-done | bytes 262176 | tf_op jit(solution)/shard_map/ppermute | solution.py:414
  177.7 6.3 %collective-permute-done.27.s3 = bf16[128,1024]{1,0:T(8,128)(2,1)S(1)} collective-permute-done((bf16[128,1024]{1,0:T(8,128)(2,1)S(1)}, bf16[128,1024]{1,0:T(8,128)(2,1)S(1)}, u32[]{:S(2)}, u32[]{:S(2)}) %collective-permute-start.27) | collective-permute-done | bytes 262176 | tf_op jit(solution)/shard_map/ppermute | solution.py:414
  187.1 4.4 %collective-permute-done.28.got_ref = bf16[128,512]{1,0:T(8,128)(2,1)S(1)} collective-permute-done((bf16[128,512]{1,0:T(8,128)(2,1)}, bf16[128,512]{1,0:T(8,128)(2,1)S(1)}, u32[]{:S(2)}, u32[]{:S(2)}) %collective-permute-start.28) | collective-permute-done | bytes 131104 | tf_op jit(solution)/shard_map/ppermute | solution.py:424
  192.6 3.6 %combine.1 = bf16[128,512]{1,0:T(8,128)(2,1)} custom-call(s32[6,128]{1,0:T(8,128)} %bitcast.47, f32[6,128]{1,0:T(8,128)} %bitcast.48, bf16[1024,512]{1,0:T(8,128)(2,1)} %bitcast.41, f32[128,512]{1,0:T(8,128)} %get-tuple-element.17.keep_ref, bf16[128,512]{1,0:T(8,128)(2,1)} %copy-done.18), custom_call_target="tpu_custom_call" | custom-call | tf_op jit(solution)/shard_map/combine/pallas_call | solution.py:351
  (98 shorter events, 37.3 us)
Async XLA Ops:
  45.2 44.8 %collective-permute-start = (bf16[1024,512]{1,0:T(8,128)(2,1)S(1)}, bf16[1024,512]{1,0:T(8,128)(2,1)S(1)}, u32[]{:S(2)}, u32[]{:S(2)}) collective-permute-start(bf16[1024,512]{1,0:T(8,128)(2,1)S(1)} %bitcast.37), channel_id=1, source_target_pairs={{0,1},{1,0},{2,3},{3,2},{4,5},{5,4},{6,7},{7,6},{8,9},{9,8},{10,11... | collective-permute-start | bytes 3145736 | tf_op jit(solution)/shard_map/ppermute | solution.py:400
  49.5 13.7 %collective-permute-start.1 = (bf16[512,512]{1,0:T(8,128)(2,1)S(1)}, bf16[512,512]{1,0:T(8,128)(2,1)}, u32[]{:S(2)}, u32[]{:S(2)}) collective-permute-start(bf16[512,512]{1,0:T(8,128)(2,1)S(1)} %bitcast.44), channel_id=1, source_target_pairs={{0,2},{2,0},{1,3},{3,1},{4,6},{6,4},{5,7},{7,5},{8,10},{10,8},{9,1... | collective-permute-start | bytes 1572872 | tf_op jit(solution)/shard_map/ppermute | solution.py:399
  50.0 24.4 %collective-permute-start.9 = (bf16[512,512]{1,0:T(8,128)(2,1)S(1)}, bf16[512,512]{1,0:T(8,128)(2,1)}, u32[]{:S(2)}, u32[]{:S(2)}) collective-permute-start(bf16[512,512]{1,0:T(8,128)(2,1)S(1)} %bitcast.43), channel_id=1, source_target_pairs={{0,2},{2,0},{1,3},{3,1},{4,6},{6,4},{5,7},{7,5},{8,10},{10,8},{9,1... | collective-permute-start | bytes 1572872 | tf_op jit(solution)/shard_map/ppermute | solution.py:399
  63.1 28.1 %collective-permute-start.2 = (bf16[512,512]{1,0:T(8,128)(2,1)}, bf16[512,512]{1,0:T(8,128)(2,1)}, u32[]{:S(2)}, u32[]{:S(2)}) collective-permute-start(bf16[512,512]{1,0:T(8,128)(2,1)} %collective-permute-done.1.x2), channel_id=1, source_target_pairs={{0,1},{1,0},{2,3},{3,2},{4,5},{5,4},{6,7},{7,6},{8,9},{9,8},{10,11... | collective-permute-start | bytes 1572872 | tf_op jit(solution)/shard_map/ppermute | solution.py:403
  66.7 15.3 %collective-permute-start.6 = (bf16[352,512]{1,0:T(8,128)(2,1)}, bf16[352,512]{1,0:T(8,128)(2,1)S(1)}, u32[]{:S(2)}, u32[]{:S(2)}) collective-permute-start(bf16[352,512]{1,0:T(8,128)(2,1)} %get-tuple-element.12), channel_id=1, source_target_pairs={{0,2},{2,0},{1,3},{3,1},{4,6},{6,4},{5,7},{7,5},{8,10},{10,8},{9,1... | collective-permute-start | bytes 1081352 | tf_op jit(solution)/shard_map/ppermute | solution.py:385
  74.4 23.2 %collective-permute-start.10 = (bf16[512,512]{1,0:T(8,128)(2,1)}, bf16[512,512]{1,0:T(8,128)(2,1)}, u32[]{:S(2)}, u32[]{:S(2)}) collective-permute-start(bf16[512,512]{1,0:T(8,128)(2,1)} %collective-permute-done.9.x2), channel_id=1, source_target_pairs={{0,1},{1,0},{2,3},{3,2},{4,5},{5,4},{6,7},{7,6},{8,9},{9,8},{10,11... | collective-permute-start | bytes 1572872 | tf_op jit(solution)/shard_map/ppermute | solution.py:403
  77.4 12.6 %all-to-all-start.2 = ((bf16[8,32,528]{2,1,0:T(8,128)(2,1)}), bf16[8,32,528]{2,1,0:T(8,128)(2,1)S(1)}, u32[]{:S(2)}, u32[]{:S(2)}) async-start(bf16[8,32,528]{2,1,0:T(8,128)(2,1)} %pack.1), calls=%async_computation.2 | async-start | bytes 655360 | tf_op jit(solution)/shard_map/all_to_all | solution.py:378
  81.2 24.6 %collective-permute-start.7 = (bf16[352,512]{1,0:T(8,128)(2,1)}, bf16[352,512]{1,0:T(8,128)(2,1)S(1)}, u32[]{:S(2)}, u32[]{:S(2)}) collective-permute-start(bf16[352,512]{1,0:T(8,128)(2,1)} %get-tuple-element.13), channel_id=1, source_target_pairs={{0,3},{3,0},{1,2},{2,1},{4,7},{7,4},{5,6},{6,5},{8,11},{11,8},{9,1... | collective-permute-start | bytes 1081352 | tf_op jit(solution)/shard_map/ppermute | solution.py:385
  82.0 24.4 %collective-permute-start.8 = (bf16[352,512]{1,0:T(8,128)(2,1)}, bf16[352,512]{1,0:T(8,128)(2,1)S(1)}, u32[]{:S(2)}, u32[]{:S(2)}) collective-permute-start(bf16[352,512]{1,0:T(8,128)(2,1)} %get-tuple-element.14), channel_id=1, source_target_pairs={{0,1},{1,0},{2,3},{3,2},{4,5},{5,4},{6,7},{7,6},{8,9},{9,8},{10,11... | collective-permute-start | bytes 1081352 | tf_op jit(solution)/shard_map/ppermute | solution.py:385
  90.0 17.4 %collective-permute-start.17 = (bf16[8,32,528]{2,1,0:T(8,128)(2,1)S(1)}, bf16[8,32,528]{2,1,0:T(8,128)(2,1)S(1)}, u32[]{:S(2)}, u32[]{:S(2)}) collective-permute-start(bf16[8,32,528]{2,1,0:T(8,128)(2,1)S(1)} %all-to-all-done.2.refs_0_), channel_id=1, source_target_pairs={{0,4},{4,8},{8,12},{12,16},{16,20},{20,24},{24,28},{28,0},{32,36},... | collective-permute-start | bytes 811016 | tf_op jit(solution)/shard_map/ppermute | solution.py:388
  91.3 16.7 %collective-permute-start.18 = (bf16[8,32,528]{2,1,0:T(8,128)(2,1)S(1)}, bf16[8,32,528]{2,1,0:T(8,128)(2,1)S(1)}, u32[]{:S(2)}, u32[]{:S(2)}) collective-permute-start(bf16[8,32,528]{2,1,0:T(8,128)(2,1)S(1)} %all-to-all-done.2.refs_0_), channel_id=1, source_target_pairs={{0,8},{4,12},{8,16},{12,20},{16,24},{20,28},{24,0},{28,4},{32,40},... | collective-permute-start | bytes 811016 | tf_op jit(solution)/shard_map/ppermute | solution.py:388
  97.6 17.5 %collective-permute-start.21 = (bf16[8,32,528]{2,1,0:T(8,128)(2,1)S(1)}, bf16[8,32,528]{2,1,0:T(8,128)(2,1)}, u32[]{:S(2)}, u32[]{:S(2)}) collective-permute-start(bf16[8,32,528]{2,1,0:T(8,128)(2,1)S(1)} %all-to-all-done.2.refs_0_), channel_id=1, source_target_pairs={{0,24},{4,28},{8,0},{12,4},{16,8},{20,12},{24,16},{28,20},{32,56},... | collective-permute-start | bytes 811016 | tf_op jit(solution)/shard_map/ppermute | solution.py:388
  105.9 18.0 %collective-permute-start.3 = (bf16[512,384]{1,0:T(8,128)(2,1)S(1)}, bf16[512,384]{1,0:T(8,128)(2,1)S(1)}, u32[]{:S(2)}, u32[]{:S(2)}) collective-permute-start(bf16[512,384]{1,0:T(8,128)(2,1)S(1)} %copy-done.3), channel_id=1, source_target_pairs={{0,2},{2,0},{1,3},{3,1},{4,6},{6,4},{5,7},{7,5},{8,10},{10,8},{9,1... | collective-permute-start | bytes 1179656 | tf_op jit(solution)/shard_map/ppermute | solution.py:405
  106.4 17.6 %collective-permute-start.11 = (bf16[512,384]{1,0:T(8,128)(2,1)}, bf16[512,384]{1,0:T(8,128)(2,1)S(1)}, u32[]{:S(2)}, u32[]{:S(2)}) collective-permute-start(bf16[512,384]{1,0:T(8,128)(2,1)} %hidden.3.h0), channel_id=1, source_target_pairs={{0,2},{2,0},{1,3},{3,1},{4,6},{6,4},{5,7},{7,5},{8,10},{10,8},{9,1... | collective-permute-start | bytes 1179656 | tf_op jit(solution)/shard_map/ppermute | solution.py:405
  107.5 18.5 %collective-permute-start.14 = (bf16[128,2048]{1,0:T(8,128)(2,1)S(1)}, bf16[128,2048]{1,0:T(8,128)(2,1)S(1)}, u32[]{:S(2)}, u32[]{:S(2)}) collective-permute-start(bf16[128,2048]{1,0:T(8,128)(2,1)S(1)} %copy-done.7), channel_id=1, source_target_pairs={{0,64},{4,68},{8,72},{12,76},{16,80},{20,84},{24,88},{28,92},{32,9... | collective-permute-start | bytes 1572872 | tf_op jit(solution)/shard_map/ppermute | solution.py:391
  108.0 13.7 %collective-permute-start.23 = (bf16[8,32,528]{2,1,0:T(8,128)(2,1)S(1)}, bf16[8,32,528]{2,1,0:T(8,128)(2,1)}, u32[]{:S(2)}, u32[]{:S(2)}) collective-permute-start(bf16[8,32,528]{2,1,0:T(8,128)(2,1)S(1)} %all-to-all-done.2.refs_0_), channel_id=1, source_target_pairs={{0,28},{4,0},{8,4},{12,8},{16,12},{20,16},{24,20},{28,24},{32,60},... | collective-permute-start | bytes 811016 | tf_op jit(solution)/shard_map/ppermute | solution.py:388
  115.1 11.9 %collective-permute-start.5 = (bf16[512,384]{1,0:T(8,128)(2,1)S(1)}, bf16[512,384]{1,0:T(8,128)(2,1)S(1)}, u32[]{:S(2)}, u32[]{:S(2)}) collective-permute-start(bf16[512,384]{1,0:T(8,128)(2,1)S(1)} %copy-done.3), channel_id=1, source_target_pairs={{0,1},{1,0},{2,3},{3,2},{4,5},{5,4},{6,7},{7,6},{8,9},{9,8},{10,11... | collective-permute-start | bytes 1179656 | tf_op jit(solution)/shard_map/ppermute | solution.py:406
  125.9 20.4 %collective-permute-start.15 = (bf16[128,2048]{1,0:T(8,128)(2,1)S(1)}, bf16[128,2048]{1,0:T(8,128)(2,1)}, u32[]{:S(2)}, u32[]{:S(2)}) collective-permute-start(bf16[128,2048]{1,0:T(8,128)(2,1)S(1)} %copy-done.7), channel_id=1, source_target_pairs={{0,128},{4,132},{8,136},{12,140},{16,144},{20,148},{24,152},{28,15... | collective-permute-start | bytes 1572872 | tf_op jit(solution)/shard_map/ppermute | solution.py:391
  127.0 23.4 %collective-permute-start.16 = (bf16[128,2048]{1,0:T(8,128)(2,1)S(1)}, bf16[128,2048]{1,0:T(8,128)(2,1)}, u32[]{:S(2)}, u32[]{:S(2)}) collective-permute-start(bf16[128,2048]{1,0:T(8,128)(2,1)S(1)} %copy-done.7), channel_id=1, source_target_pairs={{0,192},{4,196},{8,200},{12,204},{16,208},{20,212},{24,216},{28,22... | collective-permute-start | bytes 1572872 | tf_op jit(solution)/shard_map/ppermute | solution.py:391
  127.7 22.7 %collective-permute-start.19 = (bf16[8,32,528]{2,1,0:T(8,128)(2,1)}, bf16[8,32,528]{2,1,0:T(8,128)(2,1)S(1)}, u32[]{:S(2)}, u32[]{:S(2)}) collective-permute-start(bf16[8,32,528]{2,1,0:T(8,128)(2,1)} %copy-done.21), channel_id=1, source_target_pairs={{0,4},{4,8},{8,12},{12,16},{16,20},{20,24},{24,28},{28,0},{32,36},... | collective-permute-start | bytes 811016 | tf_op jit(solution)/shard_map/ppermute | solution.py:392
  129.2 21.2 %collective-permute-start.20 = (bf16[8,32,528]{2,1,0:T(8,128)(2,1)}, bf16[8,32,528]{2,1,0:T(8,128)(2,1)}, u32[]{:S(2)}, u32[]{:S(2)}) collective-permute-start(bf16[8,32,528]{2,1,0:T(8,128)(2,1)} %copy-done.21), channel_id=1, source_target_pairs={{0,8},{4,12},{8,16},{12,20},{16,24},{20,28},{24,0},{28,4},{32,40},... | collective-permute-start | bytes 811016 | tf_op jit(solution)/shard_map/ppermute | solution.py:393
  130.4 19.9 %collective-permute-start.22 = (bf16[8,32,528]{2,1,0:T(8,128)(2,1)}, bf16[8,32,528]{2,1,0:T(8,128)(2,1)}, u32[]{:S(2)}, u32[]{:S(2)}) collective-permute-start(bf16[8,32,528]{2,1,0:T(8,128)(2,1)} %collective-permute-done.21.refs_6_), channel_id=1, source_target_pairs={{0,28},{4,0},{8,4},{12,8},{16,12},{20,16},{24,20},{28,24},{32,60},... | collective-permute-start | bytes 811016 | tf_op jit(solution)/shard_map/ppermute | solution.py:394
  140.3 51.2 %all-to-all-start.1 = ((bf16[64,16,512]{2,1,0:T(8,128)(2,1)}), bf16[64,16,512]{2,1,0:T(8,128)(2,1)S(1)}, u32[]{:S(2)}, u32[]{:S(2)}) async-start(bf16[64,16,512]{2,1,0:T(8,128)(2,1)} %bitcast.40), calls=%async_computation.1 | async-start | bytes 2097152 | tf_op jit(solution)/shard_map/all_to_all | solution.py:421
  169.6 14.4 %collective-permute-start.27 = (bf16[128,1024]{1,0:T(8,128)(2,1)S(1)}, bf16[128,1024]{1,0:T(8,128)(2,1)S(1)}, u32[]{:S(2)}, u32[]{:S(2)}) collective-permute-start(bf16[128,1024]{1,0:T(8,128)(2,1)S(1)} %get-tuple-element.19), channel_id=1, source_target_pairs={{0,64},{4,68},{8,72},{12,76},{16,80},{20,84},{24,88},{28,92},{32,9... | collective-permute-start | bytes 786440 | tf_op jit(solution)/shard_map/ppermute | solution.py:414
  (30 other events, 246.2 us)

commit v6 on v5

--- a/solution.py
+++ b/solution.py
@@ -13,6 +13,7 @@
 SLOTS = EXPERTS * CAP
 TOK = 128
 D = 2048
+FS = 2816
 NX = 4
 NY = 2
 NZ = 8
@@ -38,7 +39,17 @@
     ]
 
 
-PLANES = [[xy * NZ + z for xy in range(NX * NY)] for z in range(NZ)]
+def turned_about(k):
+    def index(x, y, z, n):
+        return ((x * NY + y) * NZ + z) * 4 + n
+
+    return [
+        (index(x, y, z, n), index((n + k) % 4, y, z, x))
+        for x in range(NX)
+        for y in range(NY)
+        for z in range(NZ)
+        for n in range(4)
+    ]
 
 
 def silu(v):
@@ -104,22 +115,67 @@
     )(pos, ids_t, tokens)
 
 
-def pack_kernel(gate_ref, up_ref, down_ref, out_ref):
-    fs = out_ref.shape[2] // 3
-    for x in range(NX):
-        cut = slice(x * fs, (x + 1) * fs)
-        one = jnp.concatenate([gate_ref[:, cut], up_ref[:, cut], down_ref[:, cut]], axis=1)
-        for y in range(NY):
-            out_ref[x * NY + y] = one
-
-
-def pack(gate, up, down_t):
+def padded_to(value, lanes):
+    return jnp.concatenate([value, jnp.zeros((value.shape[0], lanes - value.shape[1]), F32)], axis=1)
+
+
+def chosen(parts, at):
+    total = parts[-1]
+    for i in range(len(parts) - 1):
+        total = jnp.where(at == i, parts[i], total)
+    return total
+
+
+def pack_kernel(place_ref, gate_ref, up_ref, down_ref, *outs):
+    n, x = place_ref[0], place_ref[1]
+    fs = gate_ref.shape[1] // NX
+    gate, up, down = gate_ref[...].astype(F32), up_ref[...].astype(F32), down_ref[...].astype(F32)
+    inward, outward = [], []
+    for i in range(NX):
+        cut = slice(i * fs, (i + 1) * fs)
+        both = jnp.concatenate([gate[:, cut], up[:, cut]], axis=1)
+        inward.append(padded_to(both, outs[0].shape[1]))
+        outward.append(padded_to(down[:, cut], outs[NX].shape[1]))
+    for d in range(NX):
+        outs[d][...] = chosen(inward, (x + d) & 3).astype(BF16)
+        outs[NX + d][...] = chosen(outward, (n + d) & 3).astype(BF16)
+
+
+def pack(place, gate, up, down_t):
     fs = gate.shape[1] // NX
+    rows = gate.shape[0]
+    vmem = pl.BlockSpec(memory_space=pltpu.VMEM)
+    inward = jax.ShapeDtypeStruct((rows, -(-2 * fs // 128) * 128), BF16)
+    outward = jax.ShapeDtypeStruct((rows, -(-fs // 128) * 128), BF16)
     return pl.pallas_call(
         pack_kernel,
-        out_shape=jax.ShapeDtypeStruct((NX * NY, gate.shape[0], 3 * fs), BF16),
+        in_specs=[pl.BlockSpec(memory_space=pltpu.SMEM)] + [vmem] * 3,
+        out_specs=[vmem] * 8,
+        out_shape=[inward] * 4 + [outward] * 4,
         name="pack",
-    )(gate, up, down_t)
+    )(place, gate, up, down_t)
+
+
+def stack_kernel(place_ref, *refs):
+    pieces, out_ref = refs[:8], refs[8]
+    x = place_ref[1]
+    lanes = pieces[0].shape[1]
+    for d in range(NX):
+        at = (x - d) & 3
+        out_ref[pl.ds(at, 1), :, :lanes] = pieces[d][...][None]
+        out_ref[pl.ds(at, 1), :, lanes:] = pieces[NX + d][...][None]
+
+
+def stack(place, pieces):
+    vmem = pl.BlockSpec(memory_space=pltpu.VMEM)
+    lanes = pieces[0].shape[1] + pieces[NX].shape[1]
+    return pl.pallas_call(
+        stack_kernel,
+        in_specs=[pl.BlockSpec(memory_space=pltpu.SMEM)] + [vmem] * 8,
+        out_specs=vmem,
+        out_shape=jax.ShapeDtypeStruct((NX, pieces[0].shape[0], lanes), BF16),
+        name="stack",
+    )(place, *pieces)
 
 
 def cut_kernel(pos_ref, a, b, c, out_a, out_b, out_c):
@@ -225,64 +281,89 @@
     )(pos, *hiddens, w_own, *w_others, *more)
 
 
-def shared_kernel(place_ref, t0, t1, t2, t3, *refs):
-    blocks, (keep_ref, send_ref, w_ref, sems) = refs[:NZ], refs[NZ + 1 :]
-    core, z = place_ref[0] & 1, place_ref[1]
+def fetch(blocks, w_ref, sems, z, first):
     copies = []
     for step, block in enumerate(blocks):
-        to = w_ref.at[(z - step) & (NZ - 1)]
-        copies.append(pltpu.make_async_copy(block, to, sems.at[step]))
+        part = block.at[:, :, :, pl.ds(first, w_ref.shape[4])]
+        copies.append(pltpu.make_async_copy(part, w_ref.at[(z - step) & (NZ - 1)], sems.at[step]))
     for copy in copies:
         copy.start()
     for copy in copies:
         copy.wait()
-    fs3 = w_ref.shape[3]
-    fs = fs3 // 3
-    rows = NZ * w_ref.shape[2]
-
-    def columns(quarter, half):
-        return w_ref[:, pl.ds(quarter * NY + half, 1)].reshape(rows, fs3)
-
-    toks = (t0, t1, t2, t3)
-    totals = [jnp.zeros((TOK, fs3), F32) for _ in toks]
+
+
+def shared_hidden_kernel(place_ref, t0, t1, t2, t3, *refs):
+    blocks, (out_ref, w_ref, sems) = refs[:NZ], refs[NZ + 1 :]
+    y, z = place_ref[2], place_ref[3]
+    fetch(blocks, w_ref, sems, z, 0)
+    rows = NZ * w_ref.shape[3]
+    lanes = w_ref.shape[4]
+    fs = FS // (4 * NX)
+    total = jnp.zeros((NX * TOK, lanes), F32)
     for quarter in range(NX):
         for half in range(NY):
-            w = columns(quarter, half)
+            w = w_ref[:, pl.ds(half ^ y, 1), quarter].reshape(rows, lanes)
             first = (quarter * NY + half) * rows
-            for d, tok_ref in enumerate(toks):
-                totals[d] = totals[d] + dot(tok_ref[:, first : first + rows], w)
-    hidden = []
-    for total in totals:
-        one = silu(total[:, :fs]) * total[:, fs : 2 * fs]
-        hidden.append(jnp.concatenate([jnp.zeros((TOK, 2 * fs), F32), one], axis=1).astype(BF16))
-    for side in range(2):
-        for half in range(NY):
-            cut = slice((side * NY + half) * rows, (side * NY + half + 1) * rows)
-            for out_ref, at in ((keep_ref, core), (send_ref, 1 - core)):
-                w = columns(2 * side + at, half)
-                for d in range(NX):
-                    out_ref[d, :, cut] = dot_nt(hidden[d], w).astype(BF16)
-
-
-def shared_ffn(place, toks, blocks, after):
-    fs3 = blocks[0].shape[2]
+            tok = jnp.concatenate([t[:, first : first + rows] for t in (t0, t1, t2, t3)], axis=0)
+            total = total + dot(tok, w)
+    hidden = silu(total[:, :fs]) * total[:, fs : 2 * fs]
+    out_ref[...] = padded_to(hidden, out_ref.shape[1]).astype(BF16)
+
+
+def shared_hidden(place, toks, blocks, after, lanes, units):
     vmem = pl.BlockSpec(memory_space=pltpu.VMEM)
     return pl.pallas_call(
-        shared_kernel,
+        shared_hidden_kernel,
         in_specs=[pl.BlockSpec(memory_space=pltpu.SMEM)]
         + [vmem] * 4
         + [pl.BlockSpec(memory_space=pl.ANY)] * (NZ + 1),
-        out_specs=[vmem, vmem],
-        out_shape=[jax.ShapeDtypeStruct((NX, TOK, D // 2), BF16)] * 2,
+        out_specs=vmem,
+        out_shape=jax.ShapeDtypeStruct((NX * TOK, units), BF16),
         scratch_shapes=[
-            pltpu.VMEM((NZ,) + blocks[0].shape, BF16),
+            pltpu.VMEM((NZ,) + blocks[0].shape[:3] + (lanes,), BF16),
             pltpu.SemaphoreType.DMA((NZ,)),
         ],
         cost_estimate=pl.CostEstimate(
-            flops=2 * NX * TOK * D * fs3 * 2, bytes_accessed=6_000_000, transcendentals=NX * TOK * fs3 // 3
-        ),
-        name="shared",
+            flops=2 * NX * TOK * D * lanes, bytes_accessed=5_000_000, transcendentals=NX * TOK * units
+        ),
+        name="shared_hidden",
     )(place, *toks, *blocks, after)
+
+
+def shared_down_kernel(place_ref, h0, h1, h2, h3, *refs):
+    blocks, outs, (w_ref, sems) = refs[:NZ], refs[NZ + 1 : NZ + 5], refs[NZ + 5 :]
+    n, y, z = place_ref[0], place_ref[2], place_ref[3]
+    units = w_ref.shape[4]
+    fetch(blocks, w_ref, sems, z, blocks[0].shape[3] - units)
+    rows = NZ * w_ref.shape[3]
+    for half in range(NY):
+        total = jnp.zeros((NX * TOK, rows), F32)
+        for j, h in enumerate((h0, h1, h2, h3)):
+            w = w_ref[:, pl.ds(half ^ y, 1), pl.ds(n ^ j, 1)].reshape(rows, units)
+            total = total + dot_nt(h[...], w)
+        for d in range(NX):
+            outs[d][:, half * rows : (half + 1) * rows] = total[d * TOK : (d + 1) * TOK].astype(BF16)
+
+
+def shared_columns(place, hiddens, blocks, after):
+    vmem = pl.BlockSpec(memory_space=pltpu.VMEM)
+    units = hiddens[0].shape[1]
+    return pl.pallas_call(
+        shared_down_kernel,
+        in_specs=[pl.BlockSpec(memory_space=pltpu.SMEM)]
+        + [vmem] * 4
+        + [pl.BlockSpec(memory_space=pl.ANY)] * (NZ + 1),
+        out_specs=[vmem] * 4,
+        out_shape=[jax.ShapeDtypeStruct((TOK, COLS), BF16)] * 4,
+        scratch_shapes=[
+            pltpu.VMEM((NZ,) + blocks[0].shape[:3] + (units,), BF16),
+            pltpu.SemaphoreType.DMA((NZ,)),
+        ],
+        cost_estimate=pl.CostEstimate(
+            flops=2 * NX * TOK * D * units, bytes_accessed=4_000_000, transcendentals=0
+        ),
+        name="shared_down",
+    )(place, *hiddens, *blocks, after)
 
 
 def turned(values):
@@ -299,29 +380,7 @@
     return total
 
 
-def fold_kernel(pos_ref, s0, s1, s2, s3, keep_ref, send_ref):
-    total = s0[...].astype(F32)
-    for one in (s1, s2, s3):
-        total = total + one[...].astype(F32)
-    low = total[:, :COLS]
-    high = total[:, COLS:]
-    first = pos_ref[0] < 2
-    keep_ref[...] = jnp.where(first, low, high)
-    send_ref[...] = jnp.where(first, high, low).astype(BF16)
-
-
-def fold(pos, parts):
-    vmem = pl.BlockSpec(memory_space=pltpu.VMEM)
-    return pl.pallas_call(
-        fold_kernel,
-        in_specs=[pl.BlockSpec(memory_space=pltpu.SMEM)] + [vmem] * 4,
-        out_specs=[vmem, vmem],
-        out_shape=[jax.ShapeDtypeStruct((TOK, COLS), F32), jax.ShapeDtypeStruct((TOK, COLS), BF16)],
-        name="fold",
-    )(pos, *parts)
-
-
-def combine_kernel(ids_ref, gw_ref, ret_ref, keep_ref, got_ref, out_ref):
+def combine_kernel(ids_ref, gw_ref, ret_ref, s0, s1, s2, s3, out_ref):
     ids = turned(ids_ref[...].astype(F32))
     gates = turned(gw_ref[...])
     named = named_counts(ids, (TOK, EXPERTS), 1)
@@ -337,7 +396,9 @@
     slot = (lax.broadcasted_iota(jnp.int32, (TOK, SLOTS), 1) & 15).astype(F32)
     hit = dot(keys, spread) == slot
     ret = ret_ref[...]
-    total = keep_ref[...] + got_ref[...].astype(F32)
+    total = s0[...].astype(F32)
+    for part in (s1, s2, s3):
+        total = total + part[...].astype(F32)
     rest = weight
     for _ in range(3):
         part = rest.astype(BF16)
@@ -347,12 +408,12 @@
     out_ref[...] = total.astype(BF16)
 
 
-def combine(ids, gate_weights, returned, keep, got):
+def combine(ids, gate_weights, returned, shared):
     return pl.pallas_call(
         combine_kernel,
         out_shape=jax.ShapeDtypeStruct((TOK, COLS), BF16),
         name="combine",
-    )(ids, gate_weights, returned, keep, got)
+    )(ids, gate_weights, returned, *shared)
 
 
 def body(
@@ -372,27 +433,32 @@
     gate_t = expert_gate.transpose(0, 2, 1)
     up_t = expert_up.transpose(0, 2, 1)
 
-    place = jnp.stack([pos[0], lax.axis_index("wide").astype(jnp.int32) & (NZ - 1)])
-
-    pieces = pack(shared_gate, shared_up, shared_down.T)
-    column = lax.all_to_all(pieces, "wide", 0, 0, axis_index_groups=PLANES, tiled=True)
+    wide = lax.axis_index("wide").astype(jnp.int32)
+    place = jnp.stack([pos[0], wide >> 4, (wide >> 3) & 1, wide & 7])
 
     outgoing = dispatch(pos, ids_t, tokens).reshape(EXPERTS, CAP, COLS)
     own = lax.all_to_all(outgoing, "wide", 0, 0, tiled=True).reshape(SLOTS, COLS)
 
+    pieces = list(pack(place, shared_gate, shared_up, shared_down.T))
+    for d in range(1, NX):
+        pieces[d] = lax.ppermute(pieces[d], "wide", moved(d, 0, 0))
+    for d in range(NX):
+        pieces[NX + d] = lax.ppermute(pieces[NX + d], ("wide", "narrow"), turned_about(d))
     cuts = cut(pos, expert_down)
     others = [
         lax.ppermute(w, "narrow", swap)
         for w, swap in zip(cuts, (Y_SWAP, BOTH_SWAP, CORE_SWAP))
     ]
-    near = {k: lax.ppermute(column, "wide", moved(0, 0, k)) for k in (2, -2, 1, -1)}
+    column = stack(place, pieces)
+    flipped = lax.ppermute(column, "wide", moved(0, 1, 0))
+    column = jnp.stack([column, flipped])
+    near = {k: lax.ppermute(column, "wide", moved(0, 0, k)) for k in (2, -2, 1, -1, 4)}
     toks = [tokens]
     for d in range(1, NX):
         toks.append(lax.ppermute(tokens, "wide", moved(d, 0, 0)))
     third = lax.ppermute(near[2], "wide", moved(0, 0, 1))
-    fourth = lax.ppermute(near[2], "wide", moved(0, 0, 2))
     fifth = lax.ppermute(near[-2], "wide", moved(0, 0, -1))
-    blocks = [column, near[1], near[2], third, fourth, fifth, near[-2], near[-1]]
+    blocks = [column, near[1], near[2], third, near[4], fifth, near[-2], near[-1]]
 
     ys = []
     for k in range(CHUNKS):
@@ -405,14 +471,11 @@
         hidden_y = lax.ppermute(hidden, "narrow", Y_SWAP)
         hidden_core = lax.ppermute(hidden, "narrow", CORE_SWAP)
         hiddens.append([hidden, hidden_y, hidden_core])
-    mine, theirs = shared_ffn(place, toks, blocks, hiddens[-1][0])
-    theirs = lax.ppermute(theirs, "narrow", CORE_SWAP)
-    shared = []
-    for d in range(NX):
-        one = (mine[d].astype(F32) + theirs[d].astype(F32)).astype(BF16)
-        if d > 0:
-            one = lax.ppermute(one, "wide", moved(-d, 0, 0))
-        shared.append(one)
+    lanes, units = pieces[0].shape[1], pieces[NX].shape[1]
+    common = shared_hidden(place, toks, blocks, hiddens[-1][0], lanes, units)
+    common_y = lax.ppermute(common, "narrow", Y_SWAP)
+    common_core = lax.ppermute(common, "narrow", CORE_SWAP)
+    common_both = lax.ppermute(common_y, "narrow", CORE_SWAP)
     outputs = None
     for k in range(CHUNKS):
         hidden_both = lax.ppermute(hiddens[k][1], "narrow", CORE_SWAP)
@@ -420,9 +483,10 @@
         outputs = expert_columns(pos, k, hiddens[k], expert_down, others, outputs)
     returned = lax.all_to_all(outputs.reshape(EXPERTS, CAP, COLS), "wide", 0, 0, tiled=True)
 
-    kept, sent = fold(pos, shared)
-    got = lax.ppermute(sent, "narrow", Y_SWAP)
-    return combine(ids_t, gates_t, returned.reshape(SLOTS, COLS), kept, got)
+    shared = list(shared_columns(place, [common, common_core, common_y, common_both], blocks, outputs))
+    for d in range(1, NX):
+        shared[d] = lax.ppermute(shared[d], "wide", moved(-d, 0, 0))
+    return combine(ids_t, gates_t, returned.reshape(SLOTS, COLS), shared)
 
 
 def solution(mesh):

time: 200 us -> 260 us (1.30)
  the two profiles are of different devices: /device:TPU:1 before, /device:TPU:160 now
where the time goes in v6:
time: 260 us; the launch traced here: 259 us
  waiting for transfers between devices  120 us (46%)
  starting transfers between devices  49.7 us (19%)
  blocking collectives  40.1 us (15%)
  Pallas kernels  39.8 us (15%)
  local copies, waits for them, and re-layouts  7.16 us (3%)
    all_to_all x1, blocking collectives, body(): lax.all_to_all(outgoing, 'wide', 0, 0, tiled=True).reshape(SLOTS, COLS)  40.1 us
    ppermute x5, waiting for transfers between devices, body(): lax.ppermute(column, 'wide', moved(0, 0, k))  32.3 us
    ppermute x2, waiting for transfers between devices, body(): lax.ppermute(own[k * CHUNK_ROWS:(k + 1) * CHUNK_ROWS], 'narrow', Y_SWAP)  23.6 us
    ppermute x3, waiting for transfers between devices, body(): toks.append(lax.ppermute(tokens, 'wide', moved(d, 0, 0)))  20.5 us
    ppermute x3, waiting for transfers between devices, body(): lax.ppermute(w, 'narrow', swap)  14.7 us
    pallas_call x2, Pallas kernels, expert_hidden(): pl.pallas_call(hidden_kernel, grid_spec=pltpu.PrefetchScalarGridSpec(num_...  10.9 us
    all_to_all x1, starting transfers between devices, body(): lax.all_to_all(outputs.reshape(EXPERTS, CAP, COLS), 'wide', 0, 0, tiled=T...  9.09 us
    ppermute x3, waiting for transfers between devices, body(): shared[d] = lax.ppermute(shared[d], 'wide', moved(-d, 0, 0))  8.53 us
  transfers between devices with their start and end apart: 39, of which 15 were waited for; matrix products, arithmetic and copies ran while one was open for 1% of the time, Pallas kernels for 11%

profile of v6, /device:TPU:160, one launch (start us, length us, event | category | flops | bytes accessed | tf_op | source)
XLA Modules:
  0.0 259.1 jit_solution(2815438720670728854)
XLA Ops:
  2.8 40.1 %all_to_all.10 = bf16[64,16,512]{2,1,0:T(8,128)(2,1)S(1)} all-to-all(bf16[64,16,512]{2,1,0:T(8,128)(2,1)} %bitcast.38), channel_id=1, replica_groups=mesh['wide'=64,'narrow'=4] {'wide'}, dimensions={0} | all-to-all | bytes 2097152 | tf_op jit(solution)/shard_map/all_to_all | solution.py:440
  45.1 12.8 %collective-permute-done.9.x2 = bf16[512,512]{1,0:T(8,128)(2,1)S(1)} collective-permute-done((bf16[512,512]{1,0:T(8,128)(2,1)S(1)}, bf16[512,512]{1,0:T(8,128)(2,1)S(1)}, u32[]{:S(2)}, u32[]{:S(2)}) %collective-permute-start.9) | collective-permute-done | bytes 524320 | tf_op jit(solution)/shard_map/ppermute | solution.py:465
  57.9 10.9 %collective-permute-done.1.x2 = bf16[512,512]{1,0:T(8,128)(2,1)} collective-permute-done((bf16[512,512]{1,0:T(8,128)(2,1)S(1)}, bf16[512,512]{1,0:T(8,128)(2,1)}, u32[]{:S(2)}, u32[]{:S(2)}) %collective-permute-start.1) | collective-permute-done | bytes 524320 | tf_op jit(solution)/shard_map/ppermute | solution.py:465
  72.7 5.5 %hidden.3.h0 = bf16[512,384]{1,0:T(8,128)(2,1)} custom-call(s32[1]{0:T(128)} %bitcast.2.pos_ref, bf16[1024,512]{1,0:T(8,128)(2,1)} %bitcast.34, bf16[1024,512]{1,0:T(8,128)(2,1)} %copy-done.1, bf16[512,512]{1,0:T(8,128)(2,1)} %copy-done.15, bf16[512,512]{1,0:T(8,128)(2,1)} %collective-permute-done.10.x3, bf16[1,352,2048]{2,1,0:T(8,128)(2,1)} %bitcast.17, ...), custom_call_target="tpu_custom_call" | custom-call | flops 1476395008 | bytes 6000000 | tf_op jit(solution)/shard_map/hidden/pallas_call | solution.py:232
  79.6 5.5 %hidden.2.h0.refs_8_ = bf16[512,384]{1,0:T(8,128)(2,1)} custom-call(s32[1]{0:T(128)} %bitcast.2.pos_ref, bf16[1024,512]{1,0:T(8,128)(2,1)} %bitcast.35, bf16[1024,512]{1,0:T(8,128)(2,1)} %copy-done.1, bf16[512,512]{1,0:T(8,128)(2,1)} %collective-permute-done.1.x2, bf16[512,512]{1,0:T(8,128)(2,1)} %collective-permute-done.2.x3, ...), custom_call_target="tpu_custom_call" | custom-call | flops 1476395008 | bytes 6000000 | tf_op jit(solution)/shard_map/hidden/pallas_call | solution.py:232
  87.3 3.7 %collective-permute-done.11.h1 = bf16[512,384]{1,0:T(8,128)(2,1)S(1)} collective-permute-done((bf16[512,384]{1,0:T(8,128)(2,1)}, bf16[512,384]{1,0:T(8,128)(2,1)S(1)}, u32[]{:S(2)}, u32[]{:S(2)}) %collective-permute-start.11) | collective-permute-done | bytes 393248 | tf_op jit(solution)/shard_map/ppermute | solution.py:471
  91.5 14.7 %collective-permute-done.7.w2 = bf16[352,512]{1,0:T(8,128)(2,1)S(1)} collective-permute-done((bf16[352,512]{1,0:T(8,128)(2,1)S(1)}, bf16[352,512]{1,0:T(8,128)(2,1)S(1)}, u32[]{:S(2)}, u32[]{:S(2)}) %collective-permute-start.7) | collective-permute-done | bytes 360480 | tf_op jit(solution)/shard_map/ppermute | solution.py:449
  107.5 3.9 %down.2.rest_0_ = bf16[1024,512]{1,0:T(8,128)(2,1)} custom-call(s32[1]{0:T(128)} %bitcast.2.pos_ref, bf16[512,384]{1,0:T(8,128)(2,1)} %hidden.3.h0, bf16[512,384]{1,0:T(8,128)(2,1)} %copy-done.22, bf16[512,384]{1,0:T(8,128)(2,1)} %collective-permute-done.12.h2, bf16[512,384]{1,0:T(8,128)(2,1)} %collective-permute-done.13.h3, bf16[1,352,2048]{2,1,0:T(8,128)(2,1)} %w0.3, ...), custom_call_target="tpu_custom_call" | custom-call | flops 738197504 | bytes 4000000 | tf_op jit(solution)/shard_map/down/pallas_call | solution.py:264
  112.9 3.9 %down.3.refs_8_ = bf16[1024,512]{1,0:T(8,128)(2,1)} custom-call(s32[1]{0:T(128)} %bitcast.2.pos_ref, bf16[512,384]{1,0:T(8,128)(2,1)} %hidden.2.h0.refs_8_, bf16[512,384]{1,0:T(8,128)(2,1)} %copy-done.19, bf16[512,384]{1,0:T(8,128)(2,1)} %copy-done.21, bf16[512,384]{1,0:T(8,128)(2,1)} %copy-done.20, ...), custom_call_target="tpu_custom_call", output_to_operand_aliasing={{}: (9, {})} | custom-call | flops 738197504 | bytes 4000000 | tf_op jit(solution)/shard_map/down/pallas_call | solution.py:264
  116.8 9.1 %all-to-all-start.1 = ((bf16[64,16,512]{2,1,0:T(8,128)(2,1)}), bf16[64,16,512]{2,1,0:T(8,128)(2,1)S(1)}, u32[]{:S(2)}, u32[]{:S(2)}) async-start(bf16[64,16,512]{2,1,0:T(8,128)(2,1)} %bitcast.36), calls=%async_computation.1 | async-start | bytes 2097152 | tf_op jit(solution)/shard_map/all_to_all | solution.py:484
  131.7 6.4 %collective-permute-start.18 = (bf16[32,384]{1,0:T(8,128)(2,1)}, bf16[32,384]{1,0:T(8,128)(2,1)S(1)}, u32[]{:S(2)}, u32[]{:S(2)}) collective-permute-start(bf16[32,384]{1,0:T(8,128)(2,1)} %get-tuple-element.25), channel_id=1, source_target_pairs={{0,128},{4,132},{8,136},{12,140},{16,144},{20,148},{24,152},{28,15... | collective-permute-start | bytes 73736 | tf_op jit(solution)/shard_map/ppermute | solution.py:444
  144.4 3.8 %collective-permute-start.24 = (bf16[4,32,640]{2,1,0:T(8,128)(2,1)}, bf16[4,32,640]{2,1,0:T(8,128)(2,1)S(1)}, u32[]{:S(2)}, u32[]{:S(2)}) collective-permute-start(bf16[4,32,640]{2,1,0:T(8,128)(2,1)} %stack.29), channel_id=1, source_target_pairs={{0,32},{4,36},{8,40},{12,44},{16,48},{20,52},{24,56},{28,60},{32,0... | collective-permute-start | bytes 491528 | tf_op jit(solution)/shard_map/ppermute | solution.py:453
  148.2 6.2 %collective-permute-done.24 = bf16[4,32,640]{2,1,0:T(8,128)(2,1)S(1)} collective-permute-done((bf16[4,32,640]{2,1,0:T(8,128)(2,1)}, bf16[4,32,640]{2,1,0:T(8,128)(2,1)S(1)}, u32[]{:S(2)}, u32[]{:S(2)}) %collective-permute-start.24) | collective-permute-done | bytes 163872 | tf_op jit(solution)/shard_map/ppermute | solution.py:453
  157.3 4.4 %collective-permute-start.28 = (bf16[2,4,32,640]{3,2,1,0:T(8,128)(2,1)S(1)}, bf16[2,4,32,640]{3,2,1,0:T(8,128)(2,1)S(1)}, u32[]{:S(2)}, u32[]{:S(2)}) collective-permute-start(bf16[2,4,32,640]{3,2,1,0:T(8,128)(2,1)S(1)} %pad_maximum_fusion.refs_0_), channel_id=1, source_target_pairs={{0,16},{4,20},{8,24},{12,28},{16,0},{20,4},{24,8},{28,12},{32,48},... | collective-permute-start | bytes 983048 | tf_op jit(solution)/shard_map/ppermute | solution.py:455
  162.8 6.8 %collective-permute-done.25.refs_1_ = bf16[2,4,32,640]{3,2,1,0:T(8,128)(2,1)S(1)} collective-permute-done((bf16[2,4,32,640]{3,2,1,0:T(8,128)(2,1)S(1)}, bf16[2,4,32,640]{3,2,1,0:T(8,128)(2,1)S(1)}, u32[]{:S(2)}, u32[]{:S(2)}) %collective-permute-start.25) | collective-permute-done | bytes 327712 | tf_op jit(solution)/shard_map/ppermute | solution.py:455
  169.6 25.4 %collective-permute-done.26.refs_2_ = bf16[2,4,32,640]{3,2,1,0:T(8,128)(2,1)S(1)} collective-permute-done((bf16[2,4,32,640]{3,2,1,0:T(8,128)(2,1)S(1)}, bf16[2,4,32,640]{3,2,1,0:T(8,128)(2,1)S(1)}, u32[]{:S(2)}, u32[]{:S(2)}) %collective-permute-start.26) | collective-permute-done | bytes 327712 | tf_op jit(solution)/shard_map/ppermute | solution.py:455
  200.7 5.0 %collective-permute-done.15.t2 = bf16[128,2048]{1,0:T(8,128)(2,1)S(1)} collective-permute-done((bf16[128,2048]{1,0:T(8,128)(2,1)S(1)}, bf16[128,2048]{1,0:T(8,128)(2,1)S(1)}, u32[]{:S(2)}, u32[]{:S(2)}) %collective-permute-start.15) | collective-permute-done | bytes 524320 | tf_op jit(solution)/shard_map/ppermute | solution.py:458
  205.7 15.4 %collective-permute-done.16.t3 = bf16[128,2048]{1,0:T(8,128)(2,1)S(1)} collective-permute-done((bf16[128,2048]{1,0:T(8,128)(2,1)S(1)}, bf16[128,2048]{1,0:T(8,128)(2,1)S(1)}, u32[]{:S(2)}, u32[]{:S(2)}) %collective-permute-start.16) | collective-permute-done | bytes 524320 | tf_op jit(solution)/shard_map/ppermute | solution.py:458
  222.7 5.1 %shared_hidden.1.h0 = bf16[512,256]{1,0:T(8,128)(2,1)} custom-call(s32[4]{0:T(128)} %pad_add_fusion.place_ref, bf16[128,2048]{1,0:T(8,128)(2,1)} %t0.1, bf16[128,2048]{1,0:T(8,128)(2,1)} %copy-done.16, bf16[128,2048]{1,0:T(8,128)(2,1)} %copy-done.17, bf16[128,2048]{1,0:T(8,128)(2,1)} %copy-done.18, bf16[2,4,32,640]{3,2,1,0:T(8,128)(2,1)} %copy-done.3, ...), custom_call_target="tpu_custom_call" | custom-call | flops 805306368 | bytes 5000000 | tf_op jit(solution)/shard_map/shared_hidden/pallas_call | solution.py:315
  228.0 6.9 %collective-permute-done.33.h2 = bf16[512,256]{1,0:T(8,128)(2,1)S(1)} collective-permute-done((bf16[512,256]{1,0:T(8,128)(2,1)}, bf16[512,256]{1,0:T(8,128)(2,1)S(1)}, u32[]{:S(2)}, u32[]{:S(2)}) %collective-permute-start.33) | collective-permute-done | bytes 262176 | tf_op jit(solution)/shard_map/ppermute | solution.py:476
  237.2 4.0 %shared_down.1 = (bf16[128,512]{1,0:T(8,128)(2,1)}, bf16[128,512]{1,0:T(8,128)(2,1)}, bf16[128,512]{1,0:T(8,128)(2,1)}, bf16[128,512]{1,0:T(8,128)(2,1)}) custom-call(s32[4]{0:T(128)} %pad_add_fusion.place_ref, bf16[512,256]{1,0:T(8,128)(2,1)} %shared_hidden.1.h0, bf16[512,256]{1,0:T(8,128)(2,1)} %copy-done.24, bf16[512,256]{1,0:T(8,128)(2,1)} %copy-done.23, ...), custom_call_target="tpu_custom_call" | custom-call | flops 536870912 | bytes 4000000 | tf_op jit(solution)/shard_map/shared_down/pallas_call | solution.py:351
  241.2 3.8 %collective-permute-start.35 = (bf16[128,512]{1,0:T(8,128)(2,1)}, bf16[128,512]{1,0:T(8,128)(2,1)S(1)}, u32[]{:S(2)}, u32[]{:S(2)}) collective-permute-start(bf16[128,512]{1,0:T(8,128)(2,1)} %get-tuple-element.32), channel_id=1, source_target_pairs={{0,192},{4,196},{8,200},{12,204},{16,208},{20,212},{24,216},{28,22... | collective-permute-start | bytes 393224 | tf_op jit(solution)/shard_map/ppermute | solution.py:488
  245.9 5.2 %collective-permute-done.35.s1 = bf16[128,512]{1,0:T(8,128)(2,1)S(1)} collective-permute-done((bf16[128,512]{1,0:T(8,128)(2,1)}, bf16[128,512]{1,0:T(8,128)(2,1)S(1)}, u32[]{:S(2)}, u32[]{:S(2)}) %collective-permute-start.35) | collective-permute-done | bytes 131104 | tf_op jit(solution)/shard_map/ppermute | solution.py:488
  255.5 3.6 %combine.1 = bf16[128,512]{1,0:T(8,128)(2,1)} custom-call(s32[6,128]{1,0:T(8,128)} %bitcast.45, f32[6,128]{1,0:T(8,128)} %bitcast.46, bf16[1024,512]{1,0:T(8,128)(2,1)} %bitcast.37, bf16[128,512]{1,0:T(8,128)(2,1)} %get-tuple-element.31.s0, bf16[128,512]{1,0:T(8,128)(2,1)} %copy-done.26, bf16[128,512]{1,0:T(8,128)(2,1)} %copy-done.27, ...), custom_call_target="tpu_custom_call" | custom-call | tf_op jit(solution)/shard_map/combine/pallas_call | solution.py:412
  (143 shorter events, 46.7 us)
Async XLA Ops:
  42.9 28.8 %collective-permute-start = (bf16[1024,512]{1,0:T(8,128)(2,1)S(1)}, bf16[1024,512]{1,0:T(8,128)(2,1)S(1)}, u32[]{:S(2)}, u32[]{:S(2)}) collective-permute-start(bf16[1024,512]{1,0:T(8,128)(2,1)S(1)} %bitcast.33), channel_id=1, source_target_pairs={{0,1},{1,0},{2,3},{3,2},{4,5},{5,4},{6,7},{7,6},{8,9},{9,8},{10,11... | collective-permute-start | bytes 3145736 | tf_op jit(solution)/shard_map/ppermute | solution.py:466
  43.0 14.9 %collective-permute-start.9 = (bf16[512,512]{1,0:T(8,128)(2,1)S(1)}, bf16[512,512]{1,0:T(8,128)(2,1)S(1)}, u32[]{:S(2)}, u32[]{:S(2)}) collective-permute-start(bf16[512,512]{1,0:T(8,128)(2,1)S(1)} %bitcast.41), channel_id=1, source_target_pairs={{0,2},{2,0},{1,3},{3,1},{4,6},{6,4},{5,7},{7,5},{8,10},{10,8},{9,1... | collective-permute-start | bytes 1572872 | tf_op jit(solution)/shard_map/ppermute | solution.py:465
  43.8 25.0 %collective-permute-start.1 = (bf16[512,512]{1,0:T(8,128)(2,1)S(1)}, bf16[512,512]{1,0:T(8,128)(2,1)}, u32[]{:S(2)}, u32[]{:S(2)}) collective-permute-start(bf16[512,512]{1,0:T(8,128)(2,1)S(1)} %bitcast.40), channel_id=1, source_target_pairs={{0,2},{2,0},{1,3},{3,1},{4,6},{6,4},{5,7},{7,5},{8,10},{10,8},{9,1... | collective-permute-start | bytes 1572872 | tf_op jit(solution)/shard_map/ppermute | solution.py:465
  57.9 13.8 %collective-permute-start.10 = (bf16[512,512]{1,0:T(8,128)(2,1)S(1)}, bf16[512,512]{1,0:T(8,128)(2,1)}, u32[]{:S(2)}, u32[]{:S(2)}) collective-permute-start(bf16[512,512]{1,0:T(8,128)(2,1)S(1)} %collective-permute-done.9.x2), channel_id=1, source_target_pairs={{0,1},{1,0},{2,3},{3,2},{4,5},{5,4},{6,7},{7,6},{8,9},{9,8},{10,11... | collective-permute-start | bytes 1572872 | tf_op jit(solution)/shard_map/ppermute | solution.py:469
  68.8 10.9 %collective-permute-start.2 = (bf16[512,512]{1,0:T(8,128)(2,1)}, bf16[512,512]{1,0:T(8,128)(2,1)}, u32[]{:S(2)}, u32[]{:S(2)}) collective-permute-start(bf16[512,512]{1,0:T(8,128)(2,1)} %collective-permute-done.1.x2), channel_id=1, source_target_pairs={{0,1},{1,0},{2,3},{3,2},{4,5},{5,4},{6,7},{7,6},{8,9},{9,8},{10,11... | collective-permute-start | bytes 1572872 | tf_op jit(solution)/shard_map/ppermute | solution.py:469
  71.1 19.9 %collective-permute-start.6 = (bf16[352,512]{1,0:T(8,128)(2,1)}, bf16[352,512]{1,0:T(8,128)(2,1)S(1)}, u32[]{:S(2)}, u32[]{:S(2)}) collective-permute-start(bf16[352,512]{1,0:T(8,128)(2,1)} %get-tuple-element.20), channel_id=1, source_target_pairs={{0,2},{2,0},{1,3},{3,1},{4,6},{6,4},{5,7},{7,5},{8,10},{10,8},{9,1... | collective-permute-start | bytes 1081352 | tf_op jit(solution)/shard_map/ppermute | solution.py:449
  78.2 12.8 %collective-permute-start.11 = (bf16[512,384]{1,0:T(8,128)(2,1)}, bf16[512,384]{1,0:T(8,128)(2,1)S(1)}, u32[]{:S(2)}, u32[]{:S(2)}) collective-permute-start(bf16[512,384]{1,0:T(8,128)(2,1)} %hidden.3.h0), channel_id=1, source_target_pairs={{0,2},{2,0},{1,3},{3,1},{4,6},{6,4},{5,7},{7,5},{8,10},{10,8},{9,1... | collective-permute-start | bytes 1179656 | tf_op jit(solution)/shard_map/ppermute | solution.py:471
  85.1 21.4 %collective-permute-start.3 = (bf16[512,384]{1,0:T(8,128)(2,1)}, bf16[512,384]{1,0:T(8,128)(2,1)S(1)}, u32[]{:S(2)}, u32[]{:S(2)}) collective-permute-start(bf16[512,384]{1,0:T(8,128)(2,1)} %hidden.2.h0.refs_8_), channel_id=1, source_target_pairs={{0,2},{2,0},{1,3},{3,1},{4,6},{6,4},{5,7},{7,5},{8,10},{10,8},{9,1... | collective-permute-start | bytes 1179656 | tf_op jit(solution)/shard_map/ppermute | solution.py:471
  85.8 20.4 %collective-permute-start.7 = (bf16[352,512]{1,0:T(8,128)(2,1)S(1)}, bf16[352,512]{1,0:T(8,128)(2,1)S(1)}, u32[]{:S(2)}, u32[]{:S(2)}) collective-permute-start(bf16[352,512]{1,0:T(8,128)(2,1)S(1)} %copy-done.36), channel_id=1, source_target_pairs={{0,3},{3,0},{1,2},{2,1},{4,7},{7,4},{5,6},{6,5},{8,11},{11,8},{9,1... | collective-permute-start | bytes 1081352 | tf_op jit(solution)/shard_map/ppermute | solution.py:449
  86.4 20.3 %collective-permute-start.13 = (bf16[512,384]{1,0:T(8,128)(2,1)S(1)}, bf16[512,384]{1,0:T(8,128)(2,1)}, u32[]{:S(2)}, u32[]{:S(2)}) collective-permute-start(bf16[512,384]{1,0:T(8,128)(2,1)S(1)} %copy-done.5), channel_id=1, source_target_pairs={{0,1},{1,0},{2,3},{3,2},{4,5},{5,4},{6,7},{7,6},{8,9},{9,8},{10,11... | collective-permute-start | bytes 1179656 | tf_op jit(solution)/shard_map/ppermute | solution.py:472
  91.0 15.8 %collective-permute-start.12 = (bf16[512,384]{1,0:T(8,128)(2,1)S(1)}, bf16[512,384]{1,0:T(8,128)(2,1)}, u32[]{:S(2)}, u32[]{:S(2)}) collective-permute-start(bf16[512,384]{1,0:T(8,128)(2,1)S(1)} %collective-permute-done.11.h1), channel_id=1, source_target_pairs={{0,1},{1,0},{2,3},{3,2},{4,5},{5,4},{6,7},{7,6},{8,9},{9,8},{10,11... | collective-permute-start | bytes 1179656 | tf_op jit(solution)/shard_map/ppermute | solution.py:481
  91.0 15.7 %collective-permute-start.8 = (bf16[352,512]{1,0:T(8,128)(2,1)}, bf16[352,512]{1,0:T(8,128)(2,1)S(1)}, u32[]{:S(2)}, u32[]{:S(2)}) collective-permute-start(bf16[352,512]{1,0:T(8,128)(2,1)} %get-tuple-element.22), channel_id=1, source_target_pairs={{0,1},{1,0},{2,3},{3,2},{4,5},{5,4},{6,7},{7,6},{8,9},{9,8},{10,11... | collective-permute-start | bytes 1081352 | tf_op jit(solution)/shard_map/ppermute | solution.py:449
  116.8 137.6 %all-to-all-start.1 = ((bf16[64,16,512]{2,1,0:T(8,128)(2,1)}), bf16[64,16,512]{2,1,0:T(8,128)(2,1)S(1)}, u32[]{:S(2)}, u32[]{:S(2)}) async-start(bf16[64,16,512]{2,1,0:T(8,128)(2,1)} %bitcast.36), calls=%async_computation.1 | async-start | bytes 2097152 | tf_op jit(solution)/shard_map/all_to_all | solution.py:484
  131.6 10.5 %collective-permute-start.17 = (bf16[32,384]{1,0:T(8,128)(2,1)}, bf16[32,384]{1,0:T(8,128)(2,1)S(1)}, u32[]{:S(2)}, u32[]{:S(2)}) collective-permute-start(bf16[32,384]{1,0:T(8,128)(2,1)} %get-tuple-element.24), channel_id=1, source_target_pairs={{0,64},{4,68},{8,72},{12,76},{16,80},{20,84},{24,88},{28,92},{32,9... | collective-permute-start | bytes 73736 | tf_op jit(solution)/shard_map/ppermute | solution.py:444
  155.3 14.2 %collective-permute-start.25 = (bf16[2,4,32,640]{3,2,1,0:T(8,128)(2,1)S(1)}, bf16[2,4,32,640]{3,2,1,0:T(8,128)(2,1)S(1)}, u32[]{:S(2)}, u32[]{:S(2)}) collective-permute-start(bf16[2,4,32,640]{3,2,1,0:T(8,128)(2,1)S(1)} %pad_maximum_fusion.refs_0_), channel_id=1, source_target_pairs={{0,4},{4,8},{8,12},{12,16},{16,20},{20,24},{24,28},{28,0},{32,36},... | collective-permute-start | bytes 983048 | tf_op jit(solution)/shard_map/ppermute | solution.py:455
  156.4 38.6 %collective-permute-start.26 = (bf16[2,4,32,640]{3,2,1,0:T(8,128)(2,1)S(1)}, bf16[2,4,32,640]{3,2,1,0:T(8,128)(2,1)S(1)}, u32[]{:S(2)}, u32[]{:S(2)}) collective-permute-start(bf16[2,4,32,640]{3,2,1,0:T(8,128)(2,1)S(1)} %pad_maximum_fusion.refs_0_), channel_id=1, source_target_pairs={{0,8},{4,12},{8,16},{12,20},{16,24},{20,28},{24,0},{28,4},{32,40},... | collective-permute-start | bytes 983048 | tf_op jit(solution)/shard_map/ppermute | solution.py:455
  157.3 41.1 %collective-permute-start.28 = (bf16[2,4,32,640]{3,2,1,0:T(8,128)(2,1)S(1)}, bf16[2,4,32,640]{3,2,1,0:T(8,128)(2,1)S(1)}, u32[]{:S(2)}, u32[]{:S(2)}) collective-permute-start(bf16[2,4,32,640]{3,2,1,0:T(8,128)(2,1)S(1)} %pad_maximum_fusion.refs_0_), channel_id=1, source_target_pairs={{0,16},{4,20},{8,24},{12,28},{16,0},{20,4},{24,8},{28,12},{32,48},... | collective-permute-start | bytes 983048 | tf_op jit(solution)/shard_map/ppermute | solution.py:455
  161.6 36.7 %collective-permute-start.29 = (bf16[2,4,32,640]{3,2,1,0:T(8,128)(2,1)S(1)}, bf16[2,4,32,640]{3,2,1,0:T(8,128)(2,1)S(1)}, u32[]{:S(2)}, u32[]{:S(2)}) collective-permute-start(bf16[2,4,32,640]{3,2,1,0:T(8,128)(2,1)S(1)} %pad_maximum_fusion.refs_0_), channel_id=1, source_target_pairs={{0,24},{4,28},{8,0},{12,4},{16,8},{20,12},{24,16},{28,20},{32,56},... | collective-permute-start | bytes 983048 | tf_op jit(solution)/shard_map/ppermute | solution.py:455
  162.0 36.6 %collective-permute-start.31 = (bf16[2,4,32,640]{3,2,1,0:T(8,128)(2,1)S(1)}, bf16[2,4,32,640]{3,2,1,0:T(8,128)(2,1)S(1)}, u32[]{:S(2)}, u32[]{:S(2)}) collective-permute-start(bf16[2,4,32,640]{3,2,1,0:T(8,128)(2,1)S(1)} %pad_maximum_fusion.refs_0_), channel_id=1, source_target_pairs={{0,28},{4,0},{8,4},{12,8},{16,12},{20,16},{24,20},{28,24},{32,60},... | collective-permute-start | bytes 983048 | tf_op jit(solution)/shard_map/ppermute | solution.py:455
  169.6 31.1 %collective-permute-start.14 = (bf16[128,2048]{1,0:T(8,128)(2,1)S(1)}, bf16[128,2048]{1,0:T(8,128)(2,1)S(1)}, u32[]{:S(2)}, u32[]{:S(2)}) collective-permute-start(bf16[128,2048]{1,0:T(8,128)(2,1)S(1)} %copy-done.4), channel_id=1, source_target_pairs={{0,64},{4,68},{8,72},{12,76},{16,80},{20,84},{24,88},{28,92},{32,9... | collective-permute-start | bytes 1572872 | tf_op jit(solution)/shard_map/ppermute | solution.py:458
  195.0 10.7 %collective-permute-start.15 = (bf16[128,2048]{1,0:T(8,128)(2,1)S(1)}, bf16[128,2048]{1,0:T(8,128)(2,1)S(1)}, u32[]{:S(2)}, u32[]{:S(2)}) collective-permute-start(bf16[128,2048]{1,0:T(8,128)(2,1)S(1)} %copy-done.4), channel_id=1, source_target_pairs={{0,128},{4,132},{8,136},{12,140},{16,144},{20,148},{24,152},{28,15... | collective-permute-start | bytes 1572872 | tf_op jit(solution)/shard_map/ppermute | solution.py:458
  198.3 22.8 %collective-permute-start.16 = (bf16[128,2048]{1,0:T(8,128)(2,1)S(1)}, bf16[128,2048]{1,0:T(8,128)(2,1)S(1)}, u32[]{:S(2)}, u32[]{:S(2)}) collective-permute-start(bf16[128,2048]{1,0:T(8,128)(2,1)S(1)} %copy-done.4), channel_id=1, source_target_pairs={{0,192},{4,196},{8,200},{12,204},{16,208},{20,212},{24,216},{28,22... | collective-permute-start | bytes 1572872 | tf_op jit(solution)/shard_map/ppermute | solution.py:458
  198.4 22.8 %collective-permute-start.27 = (bf16[2,4,32,640]{3,2,1,0:T(8,128)(2,1)S(1)}, bf16[2,4,32,640]{3,2,1,0:T(8,128)(2,1)S(1)}, u32[]{:S(2)}, u32[]{:S(2)}) collective-permute-start(bf16[2,4,32,640]{3,2,1,0:T(8,128)(2,1)S(1)} %collective-permute-done.26.refs_2_), channel_id=1, source_target_pairs={{0,4},{4,8},{8,12},{12,16},{16,20},{20,24},{24,28},{28,0},{32,36},... | collective-permute-start | bytes 983048 | tf_op jit(solution)/shard_map/ppermute | solution.py:459
  198.7 24.0 %collective-permute-start.30 = (bf16[2,4,32,640]{3,2,1,0:T(8,128)(2,1)S(1)}, bf16[2,4,32,640]{3,2,1,0:T(8,128)(2,1)}, u32[]{:S(2)}, u32[]{:S(2)}) collective-permute-start(bf16[2,4,32,640]{3,2,1,0:T(8,128)(2,1)S(1)} %collective-permute-done.29.refs_6_), channel_id=1, source_target_pairs={{0,28},{4,0},{8,4},{12,8},{16,12},{20,16},{24,20},{28,24},{32,60},... | collective-permute-start | bytes 983048 | tf_op jit(solution)/shard_map/ppermute | solution.py:460
  (52 other events, 532.7 us)

commit v7 on v6

--- a/solution.py
+++ b/solution.py
@@ -452,14 +452,12 @@
     column = stack(place, pieces)
     flipped = lax.ppermute(column, "wide", moved(0, 1, 0))
     column = jnp.stack([column, flipped])
-    near = {k: lax.ppermute(column, "wide", moved(0, 0, k)) for k in (2, -2, 1, -1, 4)}
+    blocks = [column]
+    for k in range(1, NZ):
+        blocks.append(lax.ppermute(column, "wide", moved(0, 0, k)))
     toks = [tokens]
     for d in range(1, NX):
         toks.append(lax.ppermute(tokens, "wide", moved(d, 0, 0)))
-    third = lax.ppermute(near[2], "wide", moved(0, 0, 1))
-    fifth = lax.ppermute(near[-2], "wide", moved(0, 0, -1))
-    blocks = [column, near[1], near[2], third, near[4], fifth, near[-2], near[-1]]
-
     ys = []
     for k in range(CHUNKS):
         ys.append(lax.ppermute(own[k * CHUNK_ROWS : (k + 1) * CHUNK_ROWS], "narrow", Y_SWAP))

time: 260 us -> 278 us (1.069)
  the two profiles are of different devices: /device:TPU:160 before, /device:TPU:1 now
where the time goes in v7:
time: 278 us; the launch traced here: 277 us
  waiting for transfers between devices  113 us (41%)
  starting transfers between devices  73.3 us (26%)
  blocking collectives  42.4 us (15%)
  Pallas kernels  39.8 us (14%)
  local copies, waits for them, and re-layouts  7.35 us (3%)
    ppermute x7, waiting for transfers between devices, body(): blocks.append(lax.ppermute(column, 'wide', moved(0, 0, k)))  50.4 us
    all_to_all x1, blocking collectives, body(): lax.all_to_all(outgoing, 'wide', 0, 0, tiled=True).reshape(SLOTS, COLS)  42.4 us
    ppermute x7, starting transfers between devices, body(): blocks.append(lax.ppermute(column, 'wide', moved(0, 0, k)))  25.7 us
    ppermute x2, waiting for transfers between devices, body(): lax.ppermute(own[k * CHUNK_ROWS:(k + 1) * CHUNK_ROWS], 'narrow', Y_SWAP)  22 us
    ppermute x3, waiting for transfers between devices, body(): lax.ppermute(w, 'narrow', swap)  14.9 us
    pallas_call x2, Pallas kernels, expert_hidden(): pl.pallas_call(hidden_kernel, grid_spec=pltpu.PrefetchScalarGridSpec(num_...  10.9 us
    ppermute x4, starting transfers between devices, body(): lax.ppermute(pieces[NX + d], ('wide', 'narrow'), turned_about(d))  9.23 us
    ppermute x3, waiting for transfers between devices, body(): shared[d] = lax.ppermute(shared[d], 'wide', moved(-d, 0, 0))  8.68 us
  transfers between devices with their start and end apart: 39, of which 16 were waited for; matrix products, arithmetic and copies ran while one was open for 1% of the time, Pallas kernels for 11%

profile of v7, /device:TPU:1, one launch (start us, length us, event | category | flops | bytes accessed | tf_op | source)
XLA Modules:
  0.0 277.4 jit_solution(8474872304163016513)
XLA Ops:
  2.8 42.4 %all_to_all.10 = bf16[64,16,512]{2,1,0:T(8,128)(2,1)S(1)} all-to-all(bf16[64,16,512]{2,1,0:T(8,128)(2,1)} %bitcast.38), channel_id=1, replica_groups=mesh['wide'=64,'narrow'=4] {'wide'}, dimensions={0} | all-to-all | bytes 2097152 | tf_op jit(solution)/shard_map/all_to_all | solution.py:440
  45.2 4.2 %collective-permute-start = (bf16[1024,512]{1,0:T(8,128)(2,1)S(1)}, bf16[1024,512]{1,0:T(8,128)(2,1)S(1)}, u32[]{:S(2)}, u32[]{:S(2)}) collective-permute-start(bf16[1024,512]{1,0:T(8,128)(2,1)S(1)} %bitcast.33), channel_id=1, source_target_pairs={{0,1},{1,0},{2,3},{3,2},{4,5},{5,4},{6,7},{7,6},{8,9},{9,8},{10,11... | collective-permute-start | bytes 3145736 | tf_op jit(solution)/shard_map/ppermute | solution.py:464
  51.0 12.0 %collective-permute-done.9.x2 = bf16[512,512]{1,0:T(8,128)(2,1)S(1)} collective-permute-done((bf16[512,512]{1,0:T(8,128)(2,1)S(1)}, bf16[512,512]{1,0:T(8,128)(2,1)S(1)}, u32[]{:S(2)}, u32[]{:S(2)}) %collective-permute-start.9) | collective-permute-done | bytes 524320 | tf_op jit(solution)/shard_map/ppermute | solution.py:463
  64.4 10.0 %collective-permute-done.1.x2 = bf16[512,512]{1,0:T(8,128)(2,1)} collective-permute-done((bf16[512,512]{1,0:T(8,128)(2,1)S(1)}, bf16[512,512]{1,0:T(8,128)(2,1)}, u32[]{:S(2)}, u32[]{:S(2)}) %collective-permute-start.1) | collective-permute-done | bytes 524320 | tf_op jit(solution)/shard_map/ppermute | solution.py:463
  78.9 5.5 %hidden.3.h0 = bf16[512,384]{1,0:T(8,128)(2,1)} custom-call(s32[1]{0:T(128)} %bitcast.2.pos_ref, bf16[1024,512]{1,0:T(8,128)(2,1)} %bitcast.34, bf16[1024,512]{1,0:T(8,128)(2,1)} %copy-done.1, bf16[512,512]{1,0:T(8,128)(2,1)} %copy-done.16, bf16[512,512]{1,0:T(8,128)(2,1)} %collective-permute-done.10.x3, bf16[1,352,2048]{2,1,0:T(8,128)(2,1)} %bitcast.17, ...), custom_call_target="tpu_custom_call" | custom-call | flops 1476395008 | bytes 6000000 | tf_op jit(solution)/shard_map/hidden/pallas_call | solution.py:232
  85.6 5.5 %hidden.2.h0.refs_8_ = bf16[512,384]{1,0:T(8,128)(2,1)} custom-call(s32[1]{0:T(128)} %bitcast.2.pos_ref, bf16[1024,512]{1,0:T(8,128)(2,1)} %bitcast.35, bf16[1024,512]{1,0:T(8,128)(2,1)} %copy-done.1, bf16[512,512]{1,0:T(8,128)(2,1)} %collective-permute-done.1.x2, bf16[512,512]{1,0:T(8,128)(2,1)} %collective-permute-done.2.x3, ...), custom_call_target="tpu_custom_call" | custom-call | flops 1476395008 | bytes 6000000 | tf_op jit(solution)/shard_map/hidden/pallas_call | solution.py:232
  97.6 14.9 %collective-permute-done.7.w2 = bf16[352,512]{1,0:T(8,128)(2,1)S(1)} collective-permute-done((bf16[352,512]{1,0:T(8,128)(2,1)S(1)}, bf16[352,512]{1,0:T(8,128)(2,1)S(1)}, u32[]{:S(2)}, u32[]{:S(2)}) %collective-permute-start.7) | collective-permute-done | bytes 360480 | tf_op jit(solution)/shard_map/ppermute | solution.py:449
  113.7 3.9 %down.2.rest_0_ = bf16[1024,512]{1,0:T(8,128)(2,1)} custom-call(s32[1]{0:T(128)} %bitcast.2.pos_ref, bf16[512,384]{1,0:T(8,128)(2,1)} %hidden.3.h0, bf16[512,384]{1,0:T(8,128)(2,1)} %copy-done.22, bf16[512,384]{1,0:T(8,128)(2,1)} %collective-permute-done.12.h2, bf16[512,384]{1,0:T(8,128)(2,1)} %collective-permute-done.13.h3, bf16[1,352,2048]{2,1,0:T(8,128)(2,1)} %w0.3, ...), custom_call_target="tpu_custom_call" | custom-call | flops 738197504 | bytes 4000000 | tf_op jit(solution)/shard_map/down/pallas_call | solution.py:264
  119.1 3.9 %down.3.refs_8_ = bf16[1024,512]{1,0:T(8,128)(2,1)} custom-call(s32[1]{0:T(128)} %bitcast.2.pos_ref, bf16[512,384]{1,0:T(8,128)(2,1)} %hidden.2.h0.refs_8_, bf16[512,384]{1,0:T(8,128)(2,1)} %copy-done.19, bf16[512,384]{1,0:T(8,128)(2,1)} %copy-done.21, bf16[512,384]{1,0:T(8,128)(2,1)} %copy-done.20, ...), custom_call_target="tpu_custom_call", output_to_operand_aliasing={{}: (9, {})} | custom-call | flops 738197504 | bytes 4000000 | tf_op jit(solution)/shard_map/down/pallas_call | solution.py:264
  123.1 6.1 %all-to-all-start.1 = ((bf16[64,16,512]{2,1,0:T(8,128)(2,1)}), bf16[64,16,512]{2,1,0:T(8,128)(2,1)S(1)}, u32[]{:S(2)}, u32[]{:S(2)}) async-start(bf16[64,16,512]{2,1,0:T(8,128)(2,1)} %bitcast.36), calls=%async_computation.1 | async-start | bytes 2097152 | tf_op jit(solution)/shard_map/all_to_all | solution.py:482
  150.3 5.5 %collective-permute-done.24 = bf16[4,32,640]{2,1,0:T(8,128)(2,1)S(1)} collective-permute-done((bf16[4,32,640]{2,1,0:T(8,128)(2,1)}, bf16[4,32,640]{2,1,0:T(8,128)(2,1)S(1)}, u32[]{:S(2)}, u32[]{:S(2)}) %collective-permute-start.24) | collective-permute-done | bytes 163872 | tf_op jit(solution)/shard_map/ppermute | solution.py:453
  161.2 3.7 %collective-permute-start.27 = (bf16[2,4,32,640]{3,2,1,0:T(8,128)(2,1)S(1)}, bf16[2,4,32,640]{3,2,1,0:T(8,128)(2,1)S(1)}, u32[]{:S(2)}, u32[]{:S(2)}) collective-permute-start(bf16[2,4,32,640]{3,2,1,0:T(8,128)(2,1)S(1)} %pad_maximum_fusion.refs_0_), channel_id=1, source_target_pairs={{0,12},{4,16},{8,20},{12,24},{16,28},{20,0},{24,4},{28,8},{32,44},... | collective-permute-start | bytes 983048 | tf_op jit(solution)/shard_map/ppermute | solution.py:457
  165.5 4.5 %collective-permute-start.29 = (bf16[2,4,32,640]{3,2,1,0:T(8,128)(2,1)S(1)}, bf16[2,4,32,640]{3,2,1,0:T(8,128)(2,1)S(1)}, u32[]{:S(2)}, u32[]{:S(2)}) collective-permute-start(bf16[2,4,32,640]{3,2,1,0:T(8,128)(2,1)S(1)} %pad_maximum_fusion.refs_0_), channel_id=1, source_target_pairs={{0,20},{4,24},{8,28},{12,0},{16,4},{20,8},{24,12},{28,16},{32,52},... | collective-permute-start | bytes 983048 | tf_op jit(solution)/shard_map/ppermute | solution.py:457
  170.0 8.8 %collective-permute-done.26.refs_2_ = bf16[2,4,32,640]{3,2,1,0:T(8,128)(2,1)S(1)} collective-permute-done((bf16[2,4,32,640]{3,2,1,0:T(8,128)(2,1)S(1)}, bf16[2,4,32,640]{3,2,1,0:T(8,128)(2,1)S(1)}, u32[]{:S(2)}, u32[]{:S(2)}) %collective-permute-start.26) | collective-permute-done | bytes 327712 | tf_op jit(solution)/shard_map/ppermute | solution.py:457
  178.9 5.0 %collective-permute-start.15 = (bf16[128,2048]{1,0:T(8,128)(2,1)S(1)}, bf16[128,2048]{1,0:T(8,128)(2,1)S(1)}, u32[]{:S(2)}, u32[]{:S(2)}) collective-permute-start(bf16[128,2048]{1,0:T(8,128)(2,1)S(1)} %copy-done.4), channel_id=1, source_target_pairs={{0,128},{4,132},{8,136},{12,140},{16,144},{20,148},{24,152},{28,15... | collective-permute-start | bytes 1572872 | tf_op jit(solution)/shard_map/ppermute | solution.py:460
  183.9 29.0 %collective-permute-done.27.refs_3_ = bf16[2,4,32,640]{3,2,1,0:T(8,128)(2,1)S(1)} collective-permute-done((bf16[2,4,32,640]{3,2,1,0:T(8,128)(2,1)S(1)}, bf16[2,4,32,640]{3,2,1,0:T(8,128)(2,1)S(1)}, u32[]{:S(2)}, u32[]{:S(2)}) %collective-permute-start.27) | collective-permute-done | bytes 327712 | tf_op jit(solution)/shard_map/ppermute | solution.py:457
  212.9 12.6 %collective-permute-start.30 = (bf16[2,4,32,640]{3,2,1,0:T(8,128)(2,1)S(1)}, bf16[2,4,32,640]{3,2,1,0:T(8,128)(2,1)S(1)}, u32[]{:S(2)}, u32[]{:S(2)}) collective-permute-start(bf16[2,4,32,640]{3,2,1,0:T(8,128)(2,1)S(1)} %pad_maximum_fusion.refs_0_), channel_id=1, source_target_pairs={{0,24},{4,28},{8,0},{12,4},{16,8},{20,12},{24,16},{28,20},{32,56},... | collective-permute-start | bytes 983048 | tf_op jit(solution)/shard_map/ppermute | solution.py:457
  225.5 5.6 %collective-permute-done.30.refs_6_ = bf16[2,4,32,640]{3,2,1,0:T(8,128)(2,1)S(1)} collective-permute-done((bf16[2,4,32,640]{3,2,1,0:T(8,128)(2,1)S(1)}, bf16[2,4,32,640]{3,2,1,0:T(8,128)(2,1)S(1)}, u32[]{:S(2)}, u32[]{:S(2)}) %collective-permute-start.30) | collective-permute-done | bytes 327712 | tf_op jit(solution)/shard_map/ppermute | solution.py:457
  231.0 7.0 %collective-permute-done.31.refs_7_ = bf16[2,4,32,640]{3,2,1,0:T(8,128)(2,1)S(1)} collective-permute-done((bf16[2,4,32,640]{3,2,1,0:T(8,128)(2,1)S(1)}, bf16[2,4,32,640]{3,2,1,0:T(8,128)(2,1)S(1)}, u32[]{:S(2)}, u32[]{:S(2)}) %collective-permute-start.31) | collective-permute-done | bytes 327712 | tf_op jit(solution)/shard_map/ppermute | solution.py:457
  239.8 5.1 %shared_hidden.1.h0 = bf16[512,256]{1,0:T(8,128)(2,1)} custom-call(s32[4]{0:T(128)} %pad_add_fusion.place_ref, bf16[128,2048]{1,0:T(8,128)(2,1)} %t0.1, bf16[128,2048]{1,0:T(8,128)(2,1)} %copy-done.17, bf16[128,2048]{1,0:T(8,128)(2,1)} %copy-done.18, bf16[128,2048]{1,0:T(8,128)(2,1)} %collective-permute-done.16.t3, bf16[2,4,32,640]{3,2,1,0:T(8,128)(2,1)} %copy-done.3, ...), custom_call_target="tpu_custom_call" | custom-call | flops 805306368 | bytes 5000000 | tf_op jit(solution)/shard_map/shared_hidden/pallas_call | solution.py:315
  247.8 4.5 %collective-permute-done.33.h2 = bf16[512,256]{1,0:T(8,128)(2,1)S(1)} collective-permute-done((bf16[512,256]{1,0:T(8,128)(2,1)}, bf16[512,256]{1,0:T(8,128)(2,1)S(1)}, u32[]{:S(2)}, u32[]{:S(2)}) %collective-permute-start.33) | collective-permute-done | bytes 262176 | tf_op jit(solution)/shard_map/ppermute | solution.py:474
  256.3 4.0 %shared_down.1 = (bf16[128,512]{1,0:T(8,128)(2,1)}, bf16[128,512]{1,0:T(8,128)(2,1)}, bf16[128,512]{1,0:T(8,128)(2,1)}, bf16[128,512]{1,0:T(8,128)(2,1)}) custom-call(s32[4]{0:T(128)} %pad_add_fusion.place_ref, bf16[512,256]{1,0:T(8,128)(2,1)} %shared_hidden.1.h0, bf16[512,256]{1,0:T(8,128)(2,1)} %copy-done.24, bf16[512,256]{1,0:T(8,128)(2,1)} %copy-done.23, ...), custom_call_target="tpu_custom_call" | custom-call | flops 536870912 | bytes 4000000 | tf_op jit(solution)/shard_map/shared_down/pallas_call | solution.py:351
  264.0 5.0 %collective-permute-done.35.s1 = bf16[128,512]{1,0:T(8,128)(2,1)S(1)} collective-permute-done((bf16[128,512]{1,0:T(8,128)(2,1)}, bf16[128,512]{1,0:T(8,128)(2,1)S(1)}, u32[]{:S(2)}, u32[]{:S(2)}) %collective-permute-start.35) | collective-permute-done | bytes 131104 | tf_op jit(solution)/shard_map/ppermute | solution.py:486
  273.7 3.6 %combine.1 = bf16[128,512]{1,0:T(8,128)(2,1)} custom-call(s32[6,128]{1,0:T(8,128)} %bitcast.45, f32[6,128]{1,0:T(8,128)} %bitcast.46, bf16[1024,512]{1,0:T(8,128)(2,1)} %bitcast.37, bf16[128,512]{1,0:T(8,128)(2,1)} %get-tuple-element.31.s0, bf16[128,512]{1,0:T(8,128)(2,1)} %copy-done.26, bf16[128,512]{1,0:T(8,128)(2,1)} %copy-done.27, ...), custom_call_target="tpu_custom_call" | custom-call | tf_op jit(solution)/shard_map/combine/pallas_call | solution.py:412
  (143 shorter events, 64.8 us)
Async XLA Ops:
  45.2 32.7 %collective-permute-start = (bf16[1024,512]{1,0:T(8,128)(2,1)S(1)}, bf16[1024,512]{1,0:T(8,128)(2,1)S(1)}, u32[]{:S(2)}, u32[]{:S(2)}) collective-permute-start(bf16[1024,512]{1,0:T(8,128)(2,1)S(1)} %bitcast.33), channel_id=1, source_target_pairs={{0,1},{1,0},{2,3},{3,2},{4,5},{5,4},{6,7},{7,6},{8,9},{9,8},{10,11... | collective-permute-start | bytes 3145736 | tf_op jit(solution)/shard_map/ppermute | solution.py:464
  49.5 13.6 %collective-permute-start.9 = (bf16[512,512]{1,0:T(8,128)(2,1)S(1)}, bf16[512,512]{1,0:T(8,128)(2,1)S(1)}, u32[]{:S(2)}, u32[]{:S(2)}) collective-permute-start(bf16[512,512]{1,0:T(8,128)(2,1)S(1)} %bitcast.41), channel_id=1, source_target_pairs={{0,2},{2,0},{1,3},{3,1},{4,6},{6,4},{5,7},{7,5},{8,10},{10,8},{9,1... | collective-permute-start | bytes 1572872 | tf_op jit(solution)/shard_map/ppermute | solution.py:463
  50.0 24.4 %collective-permute-start.1 = (bf16[512,512]{1,0:T(8,128)(2,1)S(1)}, bf16[512,512]{1,0:T(8,128)(2,1)}, u32[]{:S(2)}, u32[]{:S(2)}) collective-permute-start(bf16[512,512]{1,0:T(8,128)(2,1)S(1)} %bitcast.40), channel_id=1, source_target_pairs={{0,2},{2,0},{1,3},{3,1},{4,6},{6,4},{5,7},{7,5},{8,10},{10,8},{9,1... | collective-permute-start | bytes 1572872 | tf_op jit(solution)/shard_map/ppermute | solution.py:463
  63.1 14.9 %collective-permute-start.10 = (bf16[512,512]{1,0:T(8,128)(2,1)S(1)}, bf16[512,512]{1,0:T(8,128)(2,1)}, u32[]{:S(2)}, u32[]{:S(2)}) collective-permute-start(bf16[512,512]{1,0:T(8,128)(2,1)S(1)} %collective-permute-done.9.x2), channel_id=1, source_target_pairs={{0,1},{1,0},{2,3},{3,2},{4,5},{5,4},{6,7},{7,6},{8,9},{9,8},{10,11... | collective-permute-start | bytes 1572872 | tf_op jit(solution)/shard_map/ppermute | solution.py:467
  74.4 11.2 %collective-permute-start.2 = (bf16[512,512]{1,0:T(8,128)(2,1)}, bf16[512,512]{1,0:T(8,128)(2,1)}, u32[]{:S(2)}, u32[]{:S(2)}) collective-permute-start(bf16[512,512]{1,0:T(8,128)(2,1)} %collective-permute-done.1.x2), channel_id=1, source_target_pairs={{0,1},{1,0},{2,3},{3,2},{4,5},{5,4},{6,7},{7,6},{8,9},{9,8},{10,11... | collective-permute-start | bytes 1572872 | tf_op jit(solution)/shard_map/ppermute | solution.py:467
  77.5 19.9 %collective-permute-start.6 = (bf16[352,512]{1,0:T(8,128)(2,1)}, bf16[352,512]{1,0:T(8,128)(2,1)S(1)}, u32[]{:S(2)}, u32[]{:S(2)}) collective-permute-start(bf16[352,512]{1,0:T(8,128)(2,1)} %get-tuple-element.20), channel_id=1, source_target_pairs={{0,2},{2,0},{1,3},{3,1},{4,6},{6,4},{5,7},{7,5},{8,10},{10,8},{9,1... | collective-permute-start | bytes 1081352 | tf_op jit(solution)/shard_map/ppermute | solution.py:449
  84.4 11.7 %collective-permute-start.11 = (bf16[512,384]{1,0:T(8,128)(2,1)}, bf16[512,384]{1,0:T(8,128)(2,1)S(1)}, u32[]{:S(2)}, u32[]{:S(2)}) collective-permute-start(bf16[512,384]{1,0:T(8,128)(2,1)} %hidden.3.h0), channel_id=1, source_target_pairs={{0,2},{2,0},{1,3},{3,1},{4,6},{6,4},{5,7},{7,5},{8,10},{10,8},{9,1... | collective-permute-start | bytes 1179656 | tf_op jit(solution)/shard_map/ppermute | solution.py:469
  91.0 21.7 %collective-permute-start.3 = (bf16[512,384]{1,0:T(8,128)(2,1)}, bf16[512,384]{1,0:T(8,128)(2,1)S(1)}, u32[]{:S(2)}, u32[]{:S(2)}) collective-permute-start(bf16[512,384]{1,0:T(8,128)(2,1)} %hidden.2.h0.refs_8_), channel_id=1, source_target_pairs={{0,2},{2,0},{1,3},{3,1},{4,6},{6,4},{5,7},{7,5},{8,10},{10,8},{9,1... | collective-permute-start | bytes 1179656 | tf_op jit(solution)/shard_map/ppermute | solution.py:469
  91.4 21.0 %collective-permute-start.7 = (bf16[352,512]{1,0:T(8,128)(2,1)S(1)}, bf16[352,512]{1,0:T(8,128)(2,1)S(1)}, u32[]{:S(2)}, u32[]{:S(2)}) collective-permute-start(bf16[352,512]{1,0:T(8,128)(2,1)S(1)} %copy-done.36), channel_id=1, source_target_pairs={{0,3},{3,0},{1,2},{2,1},{4,7},{7,4},{5,6},{6,5},{8,11},{11,8},{9,1... | collective-permute-start | bytes 1081352 | tf_op jit(solution)/shard_map/ppermute | solution.py:449
  93.2 19.8 %collective-permute-start.13 = (bf16[512,384]{1,0:T(8,128)(2,1)S(1)}, bf16[512,384]{1,0:T(8,128)(2,1)}, u32[]{:S(2)}, u32[]{:S(2)}) collective-permute-start(bf16[512,384]{1,0:T(8,128)(2,1)S(1)} %copy-done.5), channel_id=1, source_target_pairs={{0,1},{1,0},{2,3},{3,2},{4,5},{5,4},{6,7},{7,6},{8,9},{9,8},{10,11... | collective-permute-start | bytes 1179656 | tf_op jit(solution)/shard_map/ppermute | solution.py:470
  96.1 16.9 %collective-permute-start.12 = (bf16[512,384]{1,0:T(8,128)(2,1)S(1)}, bf16[512,384]{1,0:T(8,128)(2,1)}, u32[]{:S(2)}, u32[]{:S(2)}) collective-permute-start(bf16[512,384]{1,0:T(8,128)(2,1)S(1)} %collective-permute-done.11.h1), channel_id=1, source_target_pairs={{0,1},{1,0},{2,3},{3,2},{4,5},{5,4},{6,7},{7,6},{8,9},{9,8},{10,11... | collective-permute-start | bytes 1179656 | tf_op jit(solution)/shard_map/ppermute | solution.py:479
  97.5 15.5 %collective-permute-start.8 = (bf16[352,512]{1,0:T(8,128)(2,1)}, bf16[352,512]{1,0:T(8,128)(2,1)S(1)}, u32[]{:S(2)}, u32[]{:S(2)}) collective-permute-start(bf16[352,512]{1,0:T(8,128)(2,1)} %get-tuple-element.22), channel_id=1, source_target_pairs={{0,1},{1,0},{2,3},{3,2},{4,5},{5,4},{6,7},{7,6},{8,9},{9,8},{10,11... | collective-permute-start | bytes 1081352 | tf_op jit(solution)/shard_map/ppermute | solution.py:449
  123.1 149.6 %all-to-all-start.1 = ((bf16[64,16,512]{2,1,0:T(8,128)(2,1)}), bf16[64,16,512]{2,1,0:T(8,128)(2,1)S(1)}, u32[]{:S(2)}, u32[]{:S(2)}) async-start(bf16[64,16,512]{2,1,0:T(8,128)(2,1)} %bitcast.36), calls=%async_computation.1 | async-start | bytes 2097152 | tf_op jit(solution)/shard_map/all_to_all | solution.py:482
  156.8 13.1 %collective-permute-start.25 = (bf16[2,4,32,640]{3,2,1,0:T(8,128)(2,1)S(1)}, bf16[2,4,32,640]{3,2,1,0:T(8,128)(2,1)S(1)}, u32[]{:S(2)}, u32[]{:S(2)}) collective-permute-start(bf16[2,4,32,640]{3,2,1,0:T(8,128)(2,1)S(1)} %pad_maximum_fusion.refs_0_), channel_id=1, source_target_pairs={{0,4},{4,8},{8,12},{12,16},{16,20},{20,24},{24,28},{28,0},{32,36},... | collective-permute-start | bytes 983048 | tf_op jit(solution)/shard_map/ppermute | solution.py:457
  158.1 20.7 %collective-permute-start.26 = (bf16[2,4,32,640]{3,2,1,0:T(8,128)(2,1)S(1)}, bf16[2,4,32,640]{3,2,1,0:T(8,128)(2,1)S(1)}, u32[]{:S(2)}, u32[]{:S(2)}) collective-permute-start(bf16[2,4,32,640]{3,2,1,0:T(8,128)(2,1)S(1)} %pad_maximum_fusion.refs_0_), channel_id=1, source_target_pairs={{0,8},{4,12},{8,16},{12,20},{16,24},{20,28},{24,0},{28,4},{32,40},... | collective-permute-start | bytes 983048 | tf_op jit(solution)/shard_map/ppermute | solution.py:457
  161.2 51.6 %collective-permute-start.27 = (bf16[2,4,32,640]{3,2,1,0:T(8,128)(2,1)S(1)}, bf16[2,4,32,640]{3,2,1,0:T(8,128)(2,1)S(1)}, u32[]{:S(2)}, u32[]{:S(2)}) collective-permute-start(bf16[2,4,32,640]{3,2,1,0:T(8,128)(2,1)S(1)} %pad_maximum_fusion.refs_0_), channel_id=1, source_target_pairs={{0,12},{4,16},{8,20},{12,24},{16,28},{20,0},{24,4},{28,8},{32,44},... | collective-permute-start | bytes 983048 | tf_op jit(solution)/shard_map/ppermute | solution.py:457
  164.9 48.0 %collective-permute-start.28 = (bf16[2,4,32,640]{3,2,1,0:T(8,128)(2,1)S(1)}, bf16[2,4,32,640]{3,2,1,0:T(8,128)(2,1)S(1)}, u32[]{:S(2)}, u32[]{:S(2)}) collective-permute-start(bf16[2,4,32,640]{3,2,1,0:T(8,128)(2,1)S(1)} %pad_maximum_fusion.refs_0_), channel_id=1, source_target_pairs={{0,16},{4,20},{8,24},{12,28},{16,0},{20,4},{24,8},{28,12},{32,48},... | collective-permute-start | bytes 983048 | tf_op jit(solution)/shard_map/ppermute | solution.py:457
  165.5 60.0 %collective-permute-start.29 = (bf16[2,4,32,640]{3,2,1,0:T(8,128)(2,1)S(1)}, bf16[2,4,32,640]{3,2,1,0:T(8,128)(2,1)S(1)}, u32[]{:S(2)}, u32[]{:S(2)}) collective-permute-start(bf16[2,4,32,640]{3,2,1,0:T(8,128)(2,1)S(1)} %pad_maximum_fusion.refs_0_), channel_id=1, source_target_pairs={{0,20},{4,24},{8,28},{12,0},{16,4},{20,8},{24,12},{28,16},{32,52},... | collective-permute-start | bytes 983048 | tf_op jit(solution)/shard_map/ppermute | solution.py:457
  169.9 68.1 %collective-permute-start.14 = (bf16[128,2048]{1,0:T(8,128)(2,1)S(1)}, bf16[128,2048]{1,0:T(8,128)(2,1)S(1)}, u32[]{:S(2)}, u32[]{:S(2)}) collective-permute-start(bf16[128,2048]{1,0:T(8,128)(2,1)S(1)} %copy-done.4), channel_id=1, source_target_pairs={{0,64},{4,68},{8,72},{12,76},{16,80},{20,84},{24,88},{28,92},{32,9... | collective-permute-start | bytes 1572872 | tf_op jit(solution)/shard_map/ppermute | solution.py:460
  178.9 59.2 %collective-permute-start.15 = (bf16[128,2048]{1,0:T(8,128)(2,1)S(1)}, bf16[128,2048]{1,0:T(8,128)(2,1)S(1)}, u32[]{:S(2)}, u32[]{:S(2)}) collective-permute-start(bf16[128,2048]{1,0:T(8,128)(2,1)S(1)} %copy-done.4), channel_id=1, source_target_pairs={{0,128},{4,132},{8,136},{12,140},{16,144},{20,148},{24,152},{28,15... | collective-permute-start | bytes 1572872 | tf_op jit(solution)/shard_map/ppermute | solution.py:460
  212.8 26.9 %collective-permute-start.16 = (bf16[128,2048]{1,0:T(8,128)(2,1)S(1)}, bf16[128,2048]{1,0:T(8,128)(2,1)}, u32[]{:S(2)}, u32[]{:S(2)}) collective-permute-start(bf16[128,2048]{1,0:T(8,128)(2,1)S(1)} %copy-done.4), channel_id=1, source_target_pairs={{0,192},{4,196},{8,200},{12,204},{16,208},{20,212},{24,216},{28,22... | collective-permute-start | bytes 1572872 | tf_op jit(solution)/shard_map/ppermute | solution.py:460
  212.9 18.2 %collective-permute-start.30 = (bf16[2,4,32,640]{3,2,1,0:T(8,128)(2,1)S(1)}, bf16[2,4,32,640]{3,2,1,0:T(8,128)(2,1)S(1)}, u32[]{:S(2)}, u32[]{:S(2)}) collective-permute-start(bf16[2,4,32,640]{3,2,1,0:T(8,128)(2,1)S(1)} %pad_maximum_fusion.refs_0_), channel_id=1, source_target_pairs={{0,24},{4,28},{8,0},{12,4},{16,8},{20,12},{24,16},{28,20},{32,56},... | collective-permute-start | bytes 983048 | tf_op jit(solution)/shard_map/ppermute | solution.py:457
  225.5 12.6 %collective-permute-start.31 = (bf16[2,4,32,640]{3,2,1,0:T(8,128)(2,1)S(1)}, bf16[2,4,32,640]{3,2,1,0:T(8,128)(2,1)S(1)}, u32[]{:S(2)}, u32[]{:S(2)}) collective-permute-start(bf16[2,4,32,640]{3,2,1,0:T(8,128)(2,1)S(1)} %pad_maximum_fusion.refs_0_), channel_id=1, source_target_pairs={{0,28},{4,0},{8,4},{12,8},{16,12},{20,16},{24,20},{28,24},{32,60},... | collective-permute-start | bytes 983048 | tf_op jit(solution)/shard_map/ppermute | solution.py:457
  263.3 9.4 %collective-permute-start.37 = (bf16[128,512]{1,0:T(8,128)(2,1)}, bf16[128,512]{1,0:T(8,128)(2,1)S(1)}, u32[]{:S(2)}, u32[]{:S(2)}) collective-permute-start(bf16[128,512]{1,0:T(8,128)(2,1)} %get-tuple-element.34), channel_id=1, source_target_pairs={{0,64},{4,68},{8,72},{12,76},{16,80},{20,84},{24,88},{28,92},{32,9... | collective-permute-start | bytes 393224 | tf_op jit(solution)/shard_map/ppermute | solution.py:486
  (52 other events, 568.7 us)
